TPU v7x, 32 devices: a whole 2x2x4 slice. The times are simulated.
32 devices in a mesh: dp: 8 (over z, y), section: 4 (over x, core).
Axes of the slice: x: 2, y: 2, z: 4, core: 2. Of those that a mesh axis runs over, the one named last changes fastest.
Arguments:
- patches: bfloat16 [64, 197, 1024], P('dp'), may hold values from -6 to 6
- ln1_gain: float32 [4, 1024], P('section'), may hold values from 0.5 to 1.5
- w_qkv: bfloat16 [4, 1024, 3072], P('section'), may hold values from -1 to 1
- w_out: bfloat16 [4, 1024, 1024], P('section'), may hold values from -0.1875 to 0.1875
- ln2_gain: float32 [4, 1024], P('section'), may hold values from 0.5 to 1.5
- w_fc1: bfloat16 [4, 1024, 2048], P('section'), may hold values from -0.1875 to 0.1875
- w_fc2: bfloat16 [4, 2048, 1024], P('section'), may hold values from -0.125 to 0.125
- final_norm_gain: float32 [1024], replicated, may hold values from 0.5 to 1.5
- w_head: bfloat16 [1024, 256], replicated, may hold values from -0.1875 to 0.1875
- online_embeddings: bfloat16 [64, 256], P('dp'), may hold values from -60 to 60
- queue: bfloat16 [32768, 256], P(('dp', 'section')), may hold values from -1 to 1, as said below
- owner: int32 [64], replicated, may hold values from 0 to 63, each once
- pointer: int32 [8], P('dp'), may hold values from 0 to 4088
Outputs:
- momentum_embeddings: bfloat16 [64, 256], P('dp')
- query_loss: float32 [64], P('dp')
- total_loss: float32 [], replicated
- new_queue: bfloat16 [32768, 256], P(('dp', 'section'))
Inputs may be any that keep to these rules, and one draw needn't show every extreme that they name: `queue`: every row has Euclidean norm below 1. Each value appears once: key j goes to group owner[j] // 8, so every group receives exactly 8 keys. `pointer`: first row of the group's shard where its new keys are written.
All inputs are finite; a program needn't handle non-finite values.
Results may differ from a plain program's by a relative error of at most 0.02.
Values may be sent and summed in bfloat16 or wider, within the bound.
No kernel may reach another device: no remote copies, remote signals or barrier semaphores. Data moves between devices by JAX's collectives and lax.ppermute only.
A program may use at most 128 MiB of HBM per device.

v0:
```python
import functools
import math

import jax
import jax.numpy as jnp
from jax import lax
from jax.experimental import pallas as pl
from jax.experimental.pallas import tpu as pltpu
from jax.sharding import PartitionSpec as P

F32 = jnp.float32
BF16 = jnp.bfloat16
HEAD_DIM = 64
LANES = 128
WIDE = 256
SHARPNESS = 0.2
HOP = 2
UNROLL = 2


def layer_norm(values, gain):
    center = values - jnp.mean(values, axis=-1, keepdims=True)
    spread = jnp.mean(center * center, axis=-1, keepdims=True)
    return center * lax.rsqrt(spread + 1e-06) * gain


def mm(left, right):
    return jnp.dot(left, right, preferred_element_type=F32)


def mm_t(left, right):
    return lax.dot_general(left, right, (((1,), (1,)), ((), ())), preferred_element_type=F32)


def attention_tools(rows, toks):
    pair = LANES // HEAD_DIM
    lane = lax.broadcasted_iota(jnp.int32, (rows, LANES), 1) // HEAD_DIM
    keep = lax.broadcasted_iota(jnp.int32, (rows, rows), 1) < toks
    return pair, lane, keep


def encode(wqkv, wout, g2, wfc1, wfc2, out_ref, norm, qkv, ctx, res, act, toks, ready=None):
    rows, width = norm.shape
    ff = wfc1.shape[1]
    quad = WIDE // HEAD_DIM
    pair, lane, keep = attention_tools(rows, toks)
    scale = 1.0 / math.sqrt(HEAD_DIM)
    ready = ready or (lambda k: None)

    def project(j):
        for part in range(3):
            o = part * width + j * WIDE
            y = mm(norm[...], wqkv[:, o : o + WIDE])
            if part == 0:
                y = y * scale
            qkv[:, o : o + WIDE] = y.astype(BF16)

    def scores(j):
        found = []
        for h in range(quad):
            o = j * WIDE + (h // pair) * LANES
            q = qkv[:, o : o + LANES]
            q = jnp.where(lane == h % pair, q, jnp.zeros_like(q))
            found.append(mm_t(q, qkv[:, width + o : width + o + LANES]))
        return found

    def soften(found):
        out = []
        for s in found:
            s = jnp.where(keep, s, -1e30)
            out.append(jnp.exp(s - jnp.max(s, axis=-1, keepdims=True)).astype(BF16))
        return out

    def mix(j, weights):
        ones = jnp.ones((rows, LANES), BF16)
        for half in range(quad // pair):
            o = j * WIDE + half * LANES
            v = jnp.concatenate([qkv[:, 2 * width + o : 2 * width + o + LANES], ones], axis=1)
            got = None
            for i in range(pair):
                y = mm(weights[half * pair + i], v)
                y = y[:, :LANES] / y[:, LANES:]
                got = y if got is None else jnp.where(lane == i, y, got)
            ctx[:, o : o + LANES] = got.astype(BF16)

    groups = width // WIDE
    ready(0)
    project(0)
    found = scores(0)
    for j in range(groups):
        if j + 1 < groups:
            project(j + 1)
        mix(j, soften(found))
        if j + 1 < groups:
            found = scores(j + 1)
    ready(1)
    for n in range(0, width, WIDE):
        res[:, n : n + WIDE] += mm(ctx[...], wout[:, n : n + WIDE])
    norm[...] = layer_norm(res[...], g2[...]).astype(BF16)
    ready(2)
    for n in range(0, ff, WIDE):
        t = mm(norm[...], wfc1[:, n : n + WIDE])
        t = 0.5 * t * (1.0 + lax.erf(t * (1.0 / math.sqrt(2.0))))
        act[:, n : n + WIDE] = t.astype(BF16)
    ready(3)
    for n in range(0, width, WIDE):
        out_ref[:, n : n + WIDE] = (res[:, n : n + WIDE] + mm(act[...], wfc2[:, n : n + WIDE])).astype(BF16)


def encode_class(x_ref, g1, wqkv, wout, g2, wfc1, wfc2, norm, qkv, toks):
    rows, width = norm.shape
    heads = width // HEAD_DIM
    scale = 1.0 / math.sqrt(HEAD_DIM)
    norm[...] = layer_norm(x_ref[...].astype(F32), g1[...]).astype(BF16)
    q = mm(norm[0:16, :], wqkv[:, 0:width])[0:1, :] * scale
    own = lax.broadcasted_iota(jnp.int32, (heads, width), 1) // HEAD_DIM
    own = own == lax.broadcasted_iota(jnp.int32, (heads, width), 0)
    q = jnp.where(own, jnp.broadcast_to(q, (heads, width)), 0.0).astype(BF16)
    for o in range(width, 2 * width, WIDE):
        qkv[:, o : o + WIDE] = mm(norm[...], wqkv[:, o : o + WIDE]).astype(BF16)
    s = mm_t(q, qkv[:, width : 2 * width])
    s = jnp.where(lax.broadcasted_iota(jnp.int32, s.shape, 1) < toks, s, -1e30)
    e = jnp.exp(s - jnp.max(s, axis=-1, keepdims=True))
    p = (e / jnp.sum(e, axis=-1, keepdims=True)).astype(BF16)
    mixed = mm(p, norm[...]).astype(BF16)
    c = mm(mixed, wqkv[:, 2 * width : 3 * width])
    c = jnp.sum(jnp.where(own, c, 0.0), axis=0, keepdims=True)
    c = jnp.broadcast_to(c, (8, width)).astype(BF16)
    r = x_ref[0:8, :].astype(F32)[0:1, :] + mm(c, wout[...])
    n = layer_norm(r, g2[...]).astype(BF16)
    t = mm(n, wfc1[...])
    t = 0.5 * t * (1.0 + lax.erf(t * (1.0 / math.sqrt(2.0))))
    return (r + mm(t.astype(BF16), wfc2[...]))[0:1, :].astype(BF16).astype(F32)


def first_kernel(
    patch_hbm, wqkv_hbm, wout_hbm, wfc1_hbm, wfc2_hbm, g1, g2,
    out_ref, turned, wqkv, wout, wfc1, wfc2, marks, blank, count,
    flat, norm, qkv, ctx, res, act, sems, *, images, toks,
):
    copies = [
        pltpu.make_async_copy(a, b, sems.at[k])
        for k, (a, b) in enumerate(((wqkv_hbm, wqkv), (wout_hbm, wout), (wfc1_hbm, wfc1), (wfc2_hbm, wfc2)))
    ]
    total = toks * images
    fetch = pltpu.make_async_copy(patch_hbm, flat.at[0:total, :], sems.at[4])
    fetch.start()
    for c in copies:
        c.start()
    section = lax.axis_index("section")
    marks[...] = jnp.zeros_like(marks)
    blank[...] = jnp.zeros_like(blank)
    count[0] = 1

    @pl.when(section == 0)
    def _():
        span = flat.shape[0]
        flat[total:span, :] = jnp.zeros((span - total, flat.shape[1]), BF16)
        fetch.wait()
        take = WIDE // images
        r = lax.broadcasted_iota(jnp.int32, (WIDE, WIDE), 0)
        c = lax.broadcasted_iota(jnp.int32, (WIDE, WIDE), 1)
        order = (c == (r % take) * images + r // take).astype(F32).astype(BF16)
        rows = turned.shape[1]
        for k in range(0, rows, take):
            got = mm(order, flat[k * images : k * images + WIDE, :]).astype(BF16)
            size = min(take, rows - k)
            for i in range(images):
                turned[i, k : k + size, :] = got[i * take : i * take + size, :]
        x = turned[0].astype(F32)
        res[...] = x
        norm[...] = layer_norm(x, g1[...]).astype(BF16)
        encode(wqkv, wout, g2, wfc1, wfc2, out_ref, norm, qkv, ctx, res, act, toks, ready=lambda k: copies[k].wait())

    @pl.when(section != 0)
    def _():
        fetch.wait()
        for c in copies:
            c.wait()


def first_tick(patches, weights, rows):
    images, toks, width = patches.shape
    g1, wqkv, wout, g2, wfc1, wfc2 = weights
    ff = wfc1.shape[1]
    whole = pl.BlockSpec(memory_space=pltpu.VMEM)
    hbm = pl.BlockSpec(memory_space=pl.ANY)
    span = -(-rows * images // WIDE) * WIDE
    return pl.pallas_call(
        functools.partial(first_kernel, images=images, toks=toks),
        out_shape=(
            pltpu.VMEM((rows, width), BF16),
            pltpu.VMEM((images, rows, width), BF16),
            pltpu.VMEM(wqkv.shape, BF16),
            pltpu.VMEM(wout.shape, BF16),
            pltpu.VMEM(wfc1.shape, BF16),
            pltpu.VMEM(wfc2.shape, BF16),
            pltpu.VMEM((images, width), F32),
            pltpu.VMEM((rows, width), BF16),
            pltpu.SMEM((1,), jnp.int32),
        ),
        in_specs=[hbm] * 5 + [whole] * 2,
        out_specs=(whole,) * 8 + (pl.BlockSpec(memory_space=pltpu.SMEM),),
        scratch_shapes=[
            pltpu.VMEM((span, width), BF16),
            pltpu.VMEM((rows, width), BF16),
            pltpu.VMEM((rows, 3 * width), BF16),
            pltpu.VMEM((rows, width), BF16),
            pltpu.VMEM((rows, width), F32),
            pltpu.VMEM((rows, ff), BF16),
            pltpu.SemaphoreType.DMA((5,)),
        ],
        compiler_params=pltpu.CompilerParams(vmem_limit_bytes=14 * 2**20),
        name="first",
    )(far(patches.transpose(1, 0, 2).reshape(toks * images, width)), far(wqkv), far(wout), far(wfc1), far(wfc2), g1, g2)


def tick_kernel(
    tick, turned, came, marks_in, g1, wqkv, wout, g2, wfc1, wfc2, out_ref, marks, after, norm, qkv, ctx, res, act, *, toks
):
    after[0] = tick[0] + 1
    section = lax.axis_index("section")
    last = lax.axis_size("section") - 1
    images = turned.shape[0]
    step = tick[0] - HOP * section
    active = jnp.logical_and(step >= 0, step < images)

    def start(x):
        res[...] = x
        norm[...] = layer_norm(x, g1[...]).astype(BF16)

    @pl.when(jnp.logical_and(active, section != last))
    def _():
        @pl.when(section == 0)
        def _():
            start(turned[step].astype(F32))

        @pl.when(section != 0)
        def _():
            start(came[...].astype(F32))

        encode(wqkv, wout, g2, wfc1, wfc2, out_ref, norm, qkv, ctx, res, act, toks)

    @pl.when(jnp.logical_and(active, section == last))
    def _():
        marks[pl.ds(step, 1), :] = encode_class(came, g1, wqkv, wout, g2, wfc1, wfc2, norm, qkv, toks)


def hold(x):
    return pltpu.with_memory_space_constraint(x, pltpu.VMEM)


def far(x):
    return pltpu.with_memory_space_constraint(x, pltpu.HBM)


def held_weights(weights):
    g1, wqkv, wout, g2, wfc1, wfc2 = weights
    return g1, hold(wqkv), hold(wout), g2, hold(wfc1), hold(wfc2)


def run_tick(tick, turned, came, marks, weights, toks):
    rows, width = came.shape
    ff = weights[4].shape[1]
    whole = pl.BlockSpec(memory_space=pltpu.VMEM)
    return pl.pallas_call(
        functools.partial(tick_kernel, toks=toks),
        out_shape=(pltpu.VMEM((rows, width), BF16), pltpu.VMEM(marks.shape, F32), pltpu.SMEM((1,), jnp.int32)),
        in_specs=[pl.BlockSpec(memory_space=pltpu.SMEM)] + [whole] * 9,
        out_specs=(whole, whole, pl.BlockSpec(memory_space=pltpu.SMEM)),
        scratch_shapes=[
            pltpu.VMEM((rows, width), BF16),
            pltpu.VMEM((rows, 3 * width), BF16),
            pltpu.VMEM((rows, width), BF16),
            pltpu.VMEM((rows, width), F32),
            pltpu.VMEM((rows, ff), BF16),
        ],
        input_output_aliases={3: 1},
        compiler_params=pltpu.CompilerParams(vmem_limit_bytes=12 * 2**20),
        name="block",
    )(tick, hold(turned), hold(came), hold(marks), *held_weights(weights))


def merge_kernel(left, right, out_ref):
    half = left.shape[0]
    out_ref[0:half, :] = left[...]
    out_ref[half : 2 * half, :] = right[...]


def merge(left, right):
    whole = pl.BlockSpec(memory_space=pltpu.VMEM)
    return pl.pallas_call(
        merge_kernel,
        out_shape=pltpu.VMEM((2 * left.shape[0], left.shape[1]), left.dtype),
        in_specs=[whole, whole],
        out_specs=whole,
        compiler_params=pltpu.CompilerParams(vmem_limit_bytes=2**20),
        name="merge",
    )(left, right)


def lse_kernel(swapped, queue_hbm, out_ref, query_ref, copy_ref, ordered, queue, sems, *, images):
    fetch = pltpu.make_async_copy(queue_hbm, queue, sems.at[0])
    fetch.start()
    group = lax.axis_index("dp")
    count = swapped.shape[0]
    ordered[...] = jnp.zeros_like(ordered)
    for b in range(count // images):
        place = pl.multiple_of(jnp.bitwise_xor(group, b) * images, images)
        ordered[pl.ds(place, images), :] = swapped[b * images : (b + 1) * images, :].astype(F32)
    query_ref[...] = ordered[0:count, :].astype(BF16)
    fetch.wait()
    back = pltpu.make_async_copy(queue, copy_ref, sems.at[1])
    back.start()
    lanes = out_ref.shape[1]
    for k in range(out_ref.shape[0]):
        s = mm_t(queue[...], ordered[k * lanes : (k + 1) * lanes, :].astype(BF16)) * (1.0 / SHARPNESS)
        peak = jnp.max(s, axis=0, keepdims=True)
        out_ref[k : k + 1, :] = peak + jnp.log(jnp.sum(jnp.exp(s - peak), axis=0, keepdims=True))
    back.wait()


def head_kernel(came, marks, g1, wqkv, wout, g2, wfc1, wfc2, gain, head, lse, out_ref, found, norm, qkv, *, toks):
    images = found.shape[0]

    @pl.when(lax.axis_index("section") == lax.axis_size("section") - 1)
    def _():
        found[...] = marks[...]
        found[images - 1 : images, :] = encode_class(came, g1, wqkv, wout, g2, wfc1, wfc2, norm, qkv, toks)

    @pl.when(lax.axis_index("section") != lax.axis_size("section") - 1)
    def _():
        found[...] = jnp.zeros_like(found)

    normed = layer_norm(found[...], gain[...]).astype(BF16)
    z = mm(normed, head[...])
    z = z * lax.rsqrt(1.0 + jnp.sum(z * z, axis=1, keepdims=True))
    kd = z.shape[1]
    peers, rows, lanes = out_ref.shape
    parts = [z[:, o : o + lanes] for o in range(0, kd, lanes)]
    high = lse[...].astype(BF16).astype(F32)
    mid = (lse[...] - high).astype(BF16).astype(F32)
    low = lse[...] - high - mid
    parts += [high, mid, low]
    used = sum(p.shape[0] for p in parts)
    if rows > used:
        parts.append(jnp.zeros((rows - used, lanes), F32))
    block = jnp.concatenate(parts, axis=0).astype(BF16)
    out_ref[...] = jnp.broadcast_to(block[None], out_ref.shape)


def final_kernel(
    pointer, got, query, owner, queue_in, keys_ref, loss_ref, total_ref, queue_ref, window, sem, *, images, extra, kd
):
    section = lax.axis_index("section")
    group = lax.axis_index("dp")
    start = pointer[0]
    share = queue_ref.shape[0]
    local = start - section * share
    span = window.shape[0]
    base = jnp.clip((local // 16) * 16, 0, share - span)
    base = pl.multiple_of(base, 16)
    fetch = pltpu.make_async_copy(queue_ref.at[pl.ds(base, span), :], window, sem)
    fetch.start()
    peers, rows, lanes = got.shape
    halves = kd // lanes
    last = peers // query.shape[0] * images
    count = query.shape[0]
    n_sec = peers * images // count
    pieces = []
    for g in range(count // images):
        src = g * n_sec + n_sec - 1
        one = got[src].astype(F32)
        pieces.append(jnp.concatenate([one[h * images : (h + 1) * images] for h in range(halves)], axis=1))
    keys = jnp.concatenate(pieces, axis=0)
    keys16 = keys.astype(BF16)
    msgs = got[...].astype(F32)
    off = halves * images
    lse = msgs[:, off : off + extra, :] + msgs[:, off + extra : off + 2 * extra, :] + msgs[:, off + 2 * extra : off + 3 * extra, :]
    peak = jnp.max(lse, axis=0)
    negative = peak + jnp.log(jnp.sum(jnp.exp(lse - peak[None]), axis=0))
    square = mm_t(query[...], keys16)
    r = lax.broadcasted_iota(jnp.int32, square.shape, 0)
    c = lax.broadcasted_iota(jnp.int32, square.shape, 1)
    positive = jnp.sum(jnp.where(r == c, square, 0.0), axis=0, keepdims=True) * (1.0 / SHARPNESS)
    positive = jnp.pad(positive, ((0, 0), (0, lanes - count)))
    larger = jnp.maximum(negative, positive)
    loss = larger + jnp.log(jnp.exp(negative - larger) + jnp.exp(positive - larger)) - positive
    lane = lax.broadcasted_iota(jnp.int32, loss.shape, 1)
    total_ref[...] = jnp.sum(jnp.where(lane < count, loss, 0.0), axis=1, keepdims=True) * (1.0 / count)
    turned = pltpu.roll(jnp.broadcast_to(loss, (8, lanes)), lanes - group * images, 1)
    loss_ref[...] = turned[0:1, 0:images]
    mine = got[group * n_sec + n_sec - 1].astype(F32)
    keys_ref[...] = jnp.concatenate([mine[h * images : (h + 1) * images] for h in range(halves)], axis=1).astype(BF16)
    row = lax.broadcasted_iota(jnp.int32, (span, count), 0) + (base - local)
    slot = owner[...] - group * images
    pick = jnp.logical_and(row == slot, jnp.logical_and(slot >= 0, slot < images))
    fresh = mm(pick.astype(F32).astype(BF16), keys16)
    hit = jnp.sum(pick.astype(F32), axis=1, keepdims=True) > 0.5
    fetch.wait()
    window[...] = jnp.where(hit, fresh, window[...].astype(F32)).astype(BF16)
    back = pltpu.make_async_copy(window, queue_ref.at[pl.ds(base, span), :], sem)
    back.start()
    back.wait()


def on_device(
    patches,
    ln1_gain,
    w_qkv,
    w_out,
    ln2_gain,
    w_fc1,
    w_fc2,
    final_norm_gain,
    w_head,
    online_embeddings,
    queue,
    owner,
    pointer,
):
    sections = lax.axis_size("section")
    groups = lax.axis_size("dp")
    section = lax.axis_index("section").astype(jnp.int32)
    group = lax.axis_index("dp").astype(jnp.int32)
    images, toks, width = patches.shape
    kd = w_head.shape[1]
    peers = sections * groups
    count = groups * images
    rows = -(-toks // 16) * 16
    whole = pl.BlockSpec(memory_space=pltpu.VMEM)
    smem = pl.BlockSpec(memory_space=pltpu.SMEM)
    hbm = pl.BlockSpec(memory_space=pl.ANY)

    query = online_embeddings
    hop = 1
    while hop < groups:
        query = merge(query, lax.ppermute(query, "dp", [(k, k ^ hop) for k in range(groups)]))
        hop *= 2
    extra = -(-count // LANES)
    lse, query, queue_copy = pl.pallas_call(
        functools.partial(lse_kernel, images=images),
        out_shape=(
            pltpu.VMEM((extra, LANES), F32),
            pltpu.VMEM((count, kd), BF16),
            jax.ShapeDtypeStruct(queue.shape, BF16),
        ),
        in_specs=[whole, hbm],
        out_specs=(whole, whole, hbm),
        scratch_shapes=[
            pltpu.VMEM((extra * LANES, kd), F32),
            pltpu.VMEM(queue.shape, BF16),
            pltpu.SemaphoreType.DMA((2,)),
        ],
        compiler_params=pltpu.CompilerParams(vmem_limit_bytes=4 * 2**20),
        name="lse",
    )(query, far(queue))

    chain = [(k, k + 1) for k in range(sections - 1)]
    ticks = images + HOP * (sections - 1)
    sent, turned, *held, marks, blank, tick = first_tick(
        patches, (ln1_gain, w_qkv[0], w_out[0], ln2_gain, w_fc1[0], w_fc2[0]), rows
    )
    weights = (ln1_gain, held[0], held[1], ln2_gain, held[2], held[3])

    def advance(carry):
        tick, came, sent, marks = carry
        for _ in range(UNROLL):
            coming = lax.ppermute(sent, "section", chain)
            sent, marks, tick = run_tick(tick, turned, came, marks, weights, toks)
            came = coming
        return tick, came, sent, marks

    _, came, sent, marks = lax.while_loop(lambda carry: carry[0][0] < ticks - 1, advance, (tick, blank, sent, marks))

    height = -(-(kd // LANES * images + 3 * extra) // 8) * 8
    message = pl.pallas_call(
        functools.partial(head_kernel, toks=toks),
        out_shape=jax.ShapeDtypeStruct((peers, height, LANES), BF16),
        in_specs=[whole] * 11,
        out_specs=whole,
        scratch_shapes=[
            pltpu.VMEM((images, width), F32),
            pltpu.VMEM((rows, width), BF16),
            pltpu.VMEM((rows, 3 * width), BF16),
        ],
        compiler_params=pltpu.CompilerParams(vmem_limit_bytes=12 * 2**20),
        name="head",
    )(hold(came), hold(marks), *held_weights(weights), final_norm_gain.reshape(1, width), w_head, hold(lse))
    got = lax.all_to_all(message, ("dp", "section"), 0, 0, tiled=True)

    keys, loss, total, new_queue = pl.pallas_call(
        functools.partial(final_kernel, images=images, extra=extra, kd=kd),
        out_shape=(
            jax.ShapeDtypeStruct((images, kd), BF16),
            jax.ShapeDtypeStruct((1, images), F32),
            jax.ShapeDtypeStruct((1, 1), F32),
            jax.ShapeDtypeStruct(queue.shape, BF16),
        ),
        in_specs=[smem, whole, whole, whole, hbm],
        out_specs=(whole, whole, whole, hbm),
        scratch_shapes=[pltpu.VMEM((32, kd), BF16), pltpu.SemaphoreType.DMA],
        input_output_aliases={4: 3},
        name="final",
    )(pointer, got, hold(query), owner.reshape(1, count), far(queue_copy))
    return keys, loss.reshape(images), total.reshape(()), new_queue


def solution(mesh):
    placed = (
        P("dp", None, None),
        P("section", None),
        P("section", None, None),
        P("section", None, None),
        P("section", None),
        P("section", None, None),
        P("section", None, None),
        P(),
        P(),
        P("dp", None),
        P(("dp", "section"), None),
        P(),
        P("dp"),
    )
    return jax.shard_map(
        on_device,
        mesh=mesh,
        in_specs=placed,
        out_specs=(P("dp", None), P("dp"), P(), P(("dp", "section"), None)),
        check_vma=False,
    )
```

profile of v0, /device:TPU:1, one launch (start us, length us, event | category | flops | bytes accessed | tf_op | source)
XLA Modules:
  0.0 140.4 jit_solution(10410337231699050468)
XLA Ops:
  7.2 2.5 %collective-permute-start.4 = (bf16[32,256]{1,0:T(8,128)(2,1)S(1)}, bf16[32,256]{1,0:T(8,128)(2,1)S(1)}, u32[]{:S(2)}, u32[]{:S(2)}) collective-permute-start(bf16[32,256]{1,0:T(8,128)(2,1)S(1)} %merge.4.left), channel_id=1, source_target_pairs={{0,16},{4,20},{8,24},{12,28},{16,0},{20,4},{24,8},{28,12},{1,17},{... | collective-permute-start | bytes 49160 | tf_op jit(solution)/shard_map/ppermute | solution.py:438
  9.7 7.6 %first.1 = (bf16[208,1024]{1,0:T(8,128)(2,1)S(1)}, bf16[8,208,1024]{2,1,0:T(8,128)(2,1)S(1)}, bf16[1024,3072]{1,0:T(8,128)(2,1)S(1)}, bf16[1024,1024]{1,0:T(8,12...) custom-call(bf16[1576,1024]{1,0:T(8,128)(2,1)} %bitcast.16, ...), custom_call_target="tpu_custom_call" | custom-call | tf_op jit(solution)/shard_map/first/pallas_call | solution.py:189
  19.2 102.2 %while.13 = (s32[1]{0:T(128)S(4)}, bf16[208,1024]{1,0:T(8,128)(2,1)S(1)}, bf16[208,1024]{1,0:T(8,128)(2,1)S(1)}, f32[8,1024]{1,0:T(8,128)S(1)}, bf16[8,208,1024]...) while((s32[1]{0:T(128)S(4)}, ...), condition=%region_1.0_spmd, body=%region_0.0_spmd | while | flops 1 | bytes 3408049 | solution.py:474
  19.4 6.3 %collective-permute-start = (bf16[208,1024]{1,0:T(8,128)(2,1)S(1)}, bf16[208,1024]{1,0:T(8,128)(2,1)S(1)}, u32[]{:S(2)}, u32[]{:S(2)}) collective-permute-start(bf16[208,1024]{1,0:T(8,128)(2,1)S(1)} %get-tuple-element.148), channel_id=1, source_target_pairs={{0,1},{1,2},{2,3},{4,5},{5,6},{6,7},{8,9},{9,10},{10,11},{12,13},{... | collective-permute-start | bytes 1277960 | tf_op jit(solution)/shard_map/while/body/ppermute | solution.py:469
  27.6 3.1 %collective-permute-done.came = bf16[208,1024]{1,0:T(8,128)(2,1)S(1)} collective-permute-done((bf16[208,1024]{1,0:T(8,128)(2,1)S(1)}, bf16[208,1024]{1,0:T(8,128)(2,1)S(1)}, u32[]{:S(2)}, u32[]{:S(2)}) %collective-permute-start) | collective-permute-done | bytes 426016 | tf_op jit(solution)/shard_map/while/body/ppermute | solution.py:469
  30.7 5.8 %block.3 = (bf16[208,1024]{1,0:T(8,128)(2,1)S(1)}, f32[8,1024]{1,0:T(8,128)S(1)}, s32[1]{0:T(128)S(4)}) custom-call(s32[1]{0:T(128)S(4)} %get-tuple-element.54.tick, bf16[8,208,1024]{2,1,0:T(8,128)(2,1)S(1)} %get-tuple-element.161.turned, bf16[208,1024]{1,0:T(8,128)(2,1)S(1)} %collective-permute-done.came, ...), custom_call_target="tpu_custom_call", output_to_operand_aliasing={{1}: (3, {})} | custom-call | tf_op jit(solution)/shard_map/while/body/block/pallas_call | solution.py:266
  36.6 3.1 %collective-permute-start = (bf16[208,1024]{1,0:T(8,128)(2,1)S(1)}, bf16[208,1024]{1,0:T(8,128)(2,1)S(1)}, u32[]{:S(2)}, u32[]{:S(2)}) collective-permute-start(bf16[208,1024]{1,0:T(8,128)(2,1)S(1)} %get-tuple-element.148), channel_id=1, source_target_pairs={{0,1},{1,2},{2,3},{4,5},{5,6},{6,7},{8,9},{9,10},{10,11},{12,13},{... | collective-permute-start | bytes 1277960 | tf_op jit(solution)/shard_map/while/body/ppermute | solution.py:469
  39.7 5.8 %block.2 = (bf16[208,1024]{1,0:T(8,128)(2,1)S(1)}, f32[8,1024]{1,0:T(8,128)S(1)}, s32[1]{0:T(128)S(4)}) custom-call(s32[1]{0:T(128)S(4)} %get-tuple-element.146.tick, bf16[8,208,1024]{2,1,0:T(8,128)(2,1)S(1)} %get-tuple-element.161.turned, bf16[208,1024]{1,0:T(8,128)(2,1)S(1)} %get-tuple-element.147.came, ...), custom_call_target="tpu_custom_call", output_to_operand_aliasing={{1}: (3, {})} | custom-call | tf_op jit(solution)/shard_map/while/body/block/pallas_call | solution.py:266
  47.4 5.8 %block.3 = (bf16[208,1024]{1,0:T(8,128)(2,1)S(1)}, f32[8,1024]{1,0:T(8,128)S(1)}, s32[1]{0:T(128)S(4)}) custom-call(s32[1]{0:T(128)S(4)} %get-tuple-element.54.tick, bf16[8,208,1024]{2,1,0:T(8,128)(2,1)S(1)} %get-tuple-element.161.turned, bf16[208,1024]{1,0:T(8,128)(2,1)S(1)} %collective-permute-done.came, ...), custom_call_target="tpu_custom_call", output_to_operand_aliasing={{1}: (3, {})} | custom-call | tf_op jit(solution)/shard_map/while/body/block/pallas_call | solution.py:266
  53.3 3.5 %collective-permute-start = (bf16[208,1024]{1,0:T(8,128)(2,1)S(1)}, bf16[208,1024]{1,0:T(8,128)(2,1)S(1)}, u32[]{:S(2)}, u32[]{:S(2)}) collective-permute-start(bf16[208,1024]{1,0:T(8,128)(2,1)S(1)} %get-tuple-element.148), channel_id=1, source_target_pairs={{0,1},{1,2},{2,3},{4,5},{5,6},{6,7},{8,9},{9,10},{10,11},{12,13},{... | collective-permute-start | bytes 1277960 | tf_op jit(solution)/shard_map/while/body/ppermute | solution.py:469
  56.9 5.8 %block.2 = (bf16[208,1024]{1,0:T(8,128)(2,1)S(1)}, f32[8,1024]{1,0:T(8,128)S(1)}, s32[1]{0:T(128)S(4)}) custom-call(s32[1]{0:T(128)S(4)} %get-tuple-element.146.tick, bf16[8,208,1024]{2,1,0:T(8,128)(2,1)S(1)} %get-tuple-element.161.turned, bf16[208,1024]{1,0:T(8,128)(2,1)S(1)} %get-tuple-element.147.came, ...), custom_call_target="tpu_custom_call", output_to_operand_aliasing={{1}: (3, {})} | custom-call | tf_op jit(solution)/shard_map/while/body/block/pallas_call | solution.py:266
  64.7 5.8 %block.3 = (bf16[208,1024]{1,0:T(8,128)(2,1)S(1)}, f32[8,1024]{1,0:T(8,128)S(1)}, s32[1]{0:T(128)S(4)}) custom-call(s32[1]{0:T(128)S(4)} %get-tuple-element.54.tick, bf16[8,208,1024]{2,1,0:T(8,128)(2,1)S(1)} %get-tuple-element.161.turned, bf16[208,1024]{1,0:T(8,128)(2,1)S(1)} %collective-permute-done.came, ...), custom_call_target="tpu_custom_call", output_to_operand_aliasing={{1}: (3, {})} | custom-call | tf_op jit(solution)/shard_map/while/body/block/pallas_call | solution.py:266
  70.5 3.6 %collective-permute-start = (bf16[208,1024]{1,0:T(8,128)(2,1)S(1)}, bf16[208,1024]{1,0:T(8,128)(2,1)S(1)}, u32[]{:S(2)}, u32[]{:S(2)}) collective-permute-start(bf16[208,1024]{1,0:T(8,128)(2,1)S(1)} %get-tuple-element.148), channel_id=1, source_target_pairs={{0,1},{1,2},{2,3},{4,5},{5,6},{6,7},{8,9},{9,10},{10,11},{12,13},{... | collective-permute-start | bytes 1277960 | tf_op jit(solution)/shard_map/while/body/ppermute | solution.py:469
  74.1 5.8 %block.2 = (bf16[208,1024]{1,0:T(8,128)(2,1)S(1)}, f32[8,1024]{1,0:T(8,128)S(1)}, s32[1]{0:T(128)S(4)}) custom-call(s32[1]{0:T(128)S(4)} %get-tuple-element.146.tick, bf16[8,208,1024]{2,1,0:T(8,128)(2,1)S(1)} %get-tuple-element.161.turned, bf16[208,1024]{1,0:T(8,128)(2,1)S(1)} %get-tuple-element.147.came, ...), custom_call_target="tpu_custom_call", output_to_operand_aliasing={{1}: (3, {})} | custom-call | tf_op jit(solution)/shard_map/while/body/block/pallas_call | solution.py:266
  81.9 5.8 %block.3 = (bf16[208,1024]{1,0:T(8,128)(2,1)S(1)}, f32[8,1024]{1,0:T(8,128)S(1)}, s32[1]{0:T(128)S(4)}) custom-call(s32[1]{0:T(128)S(4)} %get-tuple-element.54.tick, bf16[8,208,1024]{2,1,0:T(8,128)(2,1)S(1)} %get-tuple-element.161.turned, bf16[208,1024]{1,0:T(8,128)(2,1)S(1)} %collective-permute-done.came, ...), custom_call_target="tpu_custom_call", output_to_operand_aliasing={{1}: (3, {})} | custom-call | tf_op jit(solution)/shard_map/while/body/block/pallas_call | solution.py:266
  87.7 3.5 %collective-permute-start = (bf16[208,1024]{1,0:T(8,128)(2,1)S(1)}, bf16[208,1024]{1,0:T(8,128)(2,1)S(1)}, u32[]{:S(2)}, u32[]{:S(2)}) collective-permute-start(bf16[208,1024]{1,0:T(8,128)(2,1)S(1)} %get-tuple-element.148), channel_id=1, source_target_pairs={{0,1},{1,2},{2,3},{4,5},{5,6},{6,7},{8,9},{9,10},{10,11},{12,13},{... | collective-permute-start | bytes 1277960 | tf_op jit(solution)/shard_map/while/body/ppermute | solution.py:469
  91.3 5.9 %block.2 = (bf16[208,1024]{1,0:T(8,128)(2,1)S(1)}, f32[8,1024]{1,0:T(8,128)S(1)}, s32[1]{0:T(128)S(4)}) custom-call(s32[1]{0:T(128)S(4)} %get-tuple-element.146.tick, bf16[8,208,1024]{2,1,0:T(8,128)(2,1)S(1)} %get-tuple-element.161.turned, bf16[208,1024]{1,0:T(8,128)(2,1)S(1)} %get-tuple-element.147.came, ...), custom_call_target="tpu_custom_call", output_to_operand_aliasing={{1}: (3, {})} | custom-call | tf_op jit(solution)/shard_map/while/body/block/pallas_call | solution.py:266
  99.1 5.0 %collective-permute-done.1 = bf16[208,1024]{1,0:T(8,128)(2,1)S(1)} collective-permute-done((bf16[208,1024]{1,0:T(8,128)(2,1)S(1)}, bf16[208,1024]{1,0:T(8,128)(2,1)S(1)}, u32[]{:S(2)}, u32[]{:S(2)}) %collective-permute-start.1) | collective-permute-done | bytes 426016 | tf_op jit(solution)/shard_map/while/body/ppermute | solution.py:469
  104.1 4.4 %collective-permute-start = (bf16[208,1024]{1,0:T(8,128)(2,1)S(1)}, bf16[208,1024]{1,0:T(8,128)(2,1)S(1)}, u32[]{:S(2)}, u32[]{:S(2)}) collective-permute-start(bf16[208,1024]{1,0:T(8,128)(2,1)S(1)} %get-tuple-element.148), channel_id=1, source_target_pairs={{0,1},{1,2},{2,3},{4,5},{5,6},{6,7},{8,9},{9,10},{10,11},{12,13},{... | collective-permute-start | bytes 1277960 | tf_op jit(solution)/shard_map/while/body/ppermute | solution.py:469
  108.6 7.7 %collective-permute-start.1 = (bf16[208,1024]{1,0:T(8,128)(2,1)S(1)}, bf16[208,1024]{1,0:T(8,128)(2,1)S(1)}, u32[]{:S(2)}, u32[]{:S(2)}) collective-permute-start(bf16[208,1024]{1,0:T(8,128)(2,1)S(1)} %get-tuple-element.58), channel_id=1, source_target_pairs={{0,1},{1,2},{2,3},{4,5},{5,6},{6,7},{8,9},{9,10},{10,11},{12,13},{... | collective-permute-start | bytes 1277960 | tf_op jit(solution)/shard_map/while/body/ppermute | solution.py:469
  116.3 5.0 %collective-permute-done.1 = bf16[208,1024]{1,0:T(8,128)(2,1)S(1)} collective-permute-done((bf16[208,1024]{1,0:T(8,128)(2,1)S(1)}, bf16[208,1024]{1,0:T(8,128)(2,1)S(1)}, u32[]{:S(2)}, u32[]{:S(2)}) %collective-permute-start.1) | collective-permute-done | bytes 426016 | tf_op jit(solution)/shard_map/while/body/ppermute | solution.py:469
  122.5 4.9 %all-to-all-start = ((bf16[32,24,128]{2,1,0:T(8,128)(2,1)}), bf16[32,24,128]{2,1,0:T(8,128)(2,1)S(1)}, u32[]{:S(2)}, u32[]{:S(2)}) async-start(bf16[32,24,128]{2,1,0:T(8,128)(2,1)} %head.2), calls=%async_computation | async-start | bytes 393216 | tf_op jit(solution)/shard_map/all_to_all | solution.py:490
  128.1 8.6 %all-to-all-done.got = bf16[32,24,128]{2,1,0:T(8,128)(2,1)S(1)} async-done(((bf16[32,24,128]{2,1,0:T(8,128)(2,1)}), bf16[32,24,128]{2,1,0:T(8,128)(2,1)S(1)}, u32[]{:S(2)}, u32[]{:S(2)}) %all-to-all-start) | async-done | bytes 196640 | tf_op jit(solution)/shard_map/all_to_all | solution.py:490
  137.3 2.9 %final.1 = (bf16[8,256]{1,0:T(8,128)(2,1)}, f32[1,8]{1,0:T(1,128)}, f32[1,1]{1,0:T(1,128)}, bf16[1024,256]{1,0:T(8,128)(2,1)}) custom-call(s32[1]{0:T(128)S(6)} %copy.35.pointer, bf16[32,24,128]{2,1,0:T(8,128)(2,1)} %copy-done.3, bf16[64,256]{1,0:T(8,128)(2,1)S(1)} %get-tuple-element.96.query, s32[1,64]{1,0:T(1,128)} %bitcast.18, ...), custom_call_target="tpu_custom_call", output_to_operand_aliasing={{3}: (4, {})} | custom-call | tf_op jit(solution)/shard_map/final/pallas_call | solution.py:492
  (40 shorter events, 20.0 us)
Async XLA Ops:
  0.6 3.3 %collective-permute-start.2 = (bf16[8,256]{1,0:T(8,128)(2,1)}, bf16[8,256]{1,0:T(8,128)(2,1)S(1)}, u32[]{:S(2)}, u32[]{:S(2)}) collective-permute-start(bf16[8,256]{1,0:T(8,128)(2,1)} %left.1), channel_id=1, source_target_pairs={{0,4},{4,0},{8,12},{12,8},{16,20},{20,16},{24,28},{28,24},{1,5},{5... | collective-permute-start | bytes 12296 | tf_op jit(solution)/shard_map/ppermute | solution.py:438
  4.0 0.7 copy-start.1
  4.7 2.6 %collective-permute-start.3 = (bf16[16,256]{1,0:T(8,128)(2,1)S(1)}, bf16[16,256]{1,0:T(8,128)(2,1)S(1)}, u32[]{:S(2)}, u32[]{:S(2)}) collective-permute-start(bf16[16,256]{1,0:T(8,128)(2,1)S(1)} %merge.3.left), channel_id=1, source_target_pairs={{0,8},{4,12},{8,0},{12,4},{16,24},{20,28},{24,16},{28,20},{1,9},{5... | collective-permute-start | bytes 24584 | tf_op jit(solution)/shard_map/ppermute | solution.py:438
  7.2 10.1 %collective-permute-start.4 = (bf16[32,256]{1,0:T(8,128)(2,1)S(1)}, bf16[32,256]{1,0:T(8,128)(2,1)S(1)}, u32[]{:S(2)}, u32[]{:S(2)}) collective-permute-start(bf16[32,256]{1,0:T(8,128)(2,1)S(1)} %merge.4.left), channel_id=1, source_target_pairs={{0,16},{4,20},{8,24},{12,28},{16,0},{20,4},{24,8},{28,12},{1,17},{... | collective-permute-start | bytes 49160 | tf_op jit(solution)/shard_map/ppermute | solution.py:438
  9.7 9.5 %copy-start.4 = (f32[1,1024]{1,0:T(1,128)S(1)}, f32[1,1024]{1,0:T(1,128)}, u32[]{:S(2)}) copy-start(f32[1,1024]{1,0:T(1,128)} %g1.3) | copy-start | bytes 12292
  9.7 9.5 %copy-start.5 = (f32[1,1024]{1,0:T(1,128)S(1)}, f32[1,1024]{1,0:T(1,128)}, u32[]{:S(2)}) copy-start(f32[1,1024]{1,0:T(1,128)} %g2.3) | copy-start | bytes 12292
  19.2 102.2 %copy-start = (bf16[1024,256]{1,0:T(8,128)(2,1)S(1)}, bf16[1024,256]{1,0:T(8,128)(2,1)}, u32[]{:S(2)}) copy-start(bf16[1024,256]{1,0:T(8,128)(2,1)} %head.3) | copy-start | bytes 1572868
  19.2 102.2 %copy-start.2 = (f32[1024]{0:T(1024)S(1)}, f32[1024]{0:T(1024)}, u32[]{:S(2)}) copy-start(f32[1024]{0:T(1024)} %param.22) | copy-start | bytes 12292
  19.4 11.3 %collective-permute-start = (bf16[208,1024]{1,0:T(8,128)(2,1)S(1)}, bf16[208,1024]{1,0:T(8,128)(2,1)S(1)}, u32[]{:S(2)}, u32[]{:S(2)}) collective-permute-start(bf16[208,1024]{1,0:T(8,128)(2,1)S(1)} %get-tuple-element.148), channel_id=1, source_target_pairs={{0,1},{1,2},{2,3},{4,5},{5,6},{6,7},{8,9},{9,10},{10,11},{12,13},{... | collective-permute-start | bytes 1277960 | tf_op jit(solution)/shard_map/while/body/ppermute | solution.py:469
  25.7 10.9 %collective-permute-start.1 = (bf16[208,1024]{1,0:T(8,128)(2,1)S(1)}, bf16[208,1024]{1,0:T(8,128)(2,1)S(1)}, u32[]{:S(2)}, u32[]{:S(2)}) collective-permute-start(bf16[208,1024]{1,0:T(8,128)(2,1)S(1)} %get-tuple-element.58), channel_id=1, source_target_pairs={{0,1},{1,2},{2,3},{4,5},{5,6},{6,7},{8,9},{9,10},{10,11},{12,13},{... | collective-permute-start | bytes 1277960 | tf_op jit(solution)/shard_map/while/body/ppermute | solution.py:469
  36.6 10.9 %collective-permute-start = (bf16[208,1024]{1,0:T(8,128)(2,1)S(1)}, bf16[208,1024]{1,0:T(8,128)(2,1)S(1)}, u32[]{:S(2)}, u32[]{:S(2)}) collective-permute-start(bf16[208,1024]{1,0:T(8,128)(2,1)S(1)} %get-tuple-element.148), channel_id=1, source_target_pairs={{0,1},{1,2},{2,3},{4,5},{5,6},{6,7},{8,9},{9,10},{10,11},{12,13},{... | collective-permute-start | bytes 1277960 | tf_op jit(solution)/shard_map/while/body/ppermute | solution.py:469
  45.5 7.8 %collective-permute-start.1 = (bf16[208,1024]{1,0:T(8,128)(2,1)S(1)}, bf16[208,1024]{1,0:T(8,128)(2,1)S(1)}, u32[]{:S(2)}, u32[]{:S(2)}) collective-permute-start(bf16[208,1024]{1,0:T(8,128)(2,1)S(1)} %get-tuple-element.58), channel_id=1, source_target_pairs={{0,1},{1,2},{2,3},{4,5},{5,6},{6,7},{8,9},{9,10},{10,11},{12,13},{... | collective-permute-start | bytes 1277960 | tf_op jit(solution)/shard_map/while/body/ppermute | solution.py:469
  53.3 11.3 %collective-permute-start = (bf16[208,1024]{1,0:T(8,128)(2,1)S(1)}, bf16[208,1024]{1,0:T(8,128)(2,1)S(1)}, u32[]{:S(2)}, u32[]{:S(2)}) collective-permute-start(bf16[208,1024]{1,0:T(8,128)(2,1)S(1)} %get-tuple-element.148), channel_id=1, source_target_pairs={{0,1},{1,2},{2,3},{4,5},{5,6},{6,7},{8,9},{9,10},{10,11},{12,13},{... | collective-permute-start | bytes 1277960 | tf_op jit(solution)/shard_map/while/body/ppermute | solution.py:469
  62.7 7.8 %collective-permute-start.1 = (bf16[208,1024]{1,0:T(8,128)(2,1)S(1)}, bf16[208,1024]{1,0:T(8,128)(2,1)S(1)}, u32[]{:S(2)}, u32[]{:S(2)}) collective-permute-start(bf16[208,1024]{1,0:T(8,128)(2,1)S(1)} %get-tuple-element.58), channel_id=1, source_target_pairs={{0,1},{1,2},{2,3},{4,5},{5,6},{6,7},{8,9},{9,10},{10,11},{12,13},{... | collective-permute-start | bytes 1277960 | tf_op jit(solution)/shard_map/while/body/ppermute | solution.py:469
  70.5 11.3 %collective-permute-start = (bf16[208,1024]{1,0:T(8,128)(2,1)S(1)}, bf16[208,1024]{1,0:T(8,128)(2,1)S(1)}, u32[]{:S(2)}, u32[]{:S(2)}) collective-permute-start(bf16[208,1024]{1,0:T(8,128)(2,1)S(1)} %get-tuple-element.148), channel_id=1, source_target_pairs={{0,1},{1,2},{2,3},{4,5},{5,6},{6,7},{8,9},{9,10},{10,11},{12,13},{... | collective-permute-start | bytes 1277960 | tf_op jit(solution)/shard_map/while/body/ppermute | solution.py:469
  79.9 7.8 %collective-permute-start.1 = (bf16[208,1024]{1,0:T(8,128)(2,1)S(1)}, bf16[208,1024]{1,0:T(8,128)(2,1)S(1)}, u32[]{:S(2)}, u32[]{:S(2)}) collective-permute-start(bf16[208,1024]{1,0:T(8,128)(2,1)S(1)} %get-tuple-element.58), channel_id=1, source_target_pairs={{0,1},{1,2},{2,3},{4,5},{5,6},{6,7},{8,9},{9,10},{10,11},{12,13},{... | collective-permute-start | bytes 1277960 | tf_op jit(solution)/shard_map/while/body/ppermute | solution.py:469
  87.7 11.3 %collective-permute-start = (bf16[208,1024]{1,0:T(8,128)(2,1)S(1)}, bf16[208,1024]{1,0:T(8,128)(2,1)S(1)}, u32[]{:S(2)}, u32[]{:S(2)}) collective-permute-start(bf16[208,1024]{1,0:T(8,128)(2,1)S(1)} %get-tuple-element.148), channel_id=1, source_target_pairs={{0,1},{1,2},{2,3},{4,5},{5,6},{6,7},{8,9},{9,10},{10,11},{12,13},{... | collective-permute-start | bytes 1277960 | tf_op jit(solution)/shard_map/while/body/ppermute | solution.py:469
  97.2 7.0 %collective-permute-start.1 = (bf16[208,1024]{1,0:T(8,128)(2,1)S(1)}, bf16[208,1024]{1,0:T(8,128)(2,1)S(1)}, u32[]{:S(2)}, u32[]{:S(2)}) collective-permute-start(bf16[208,1024]{1,0:T(8,128)(2,1)S(1)} %get-tuple-element.58), channel_id=1, source_target_pairs={{0,1},{1,2},{2,3},{4,5},{5,6},{6,7},{8,9},{9,10},{10,11},{12,13},{... | collective-permute-start | bytes 1277960 | tf_op jit(solution)/shard_map/while/body/ppermute | solution.py:469
  104.1 12.2 %collective-permute-start = (bf16[208,1024]{1,0:T(8,128)(2,1)S(1)}, bf16[208,1024]{1,0:T(8,128)(2,1)S(1)}, u32[]{:S(2)}, u32[]{:S(2)}) collective-permute-start(bf16[208,1024]{1,0:T(8,128)(2,1)S(1)} %get-tuple-element.148), channel_id=1, source_target_pairs={{0,1},{1,2},{2,3},{4,5},{5,6},{6,7},{8,9},{9,10},{10,11},{12,13},{... | collective-permute-start | bytes 1277960 | tf_op jit(solution)/shard_map/while/body/ppermute | solution.py:469
  108.6 12.8 %collective-permute-start.1 = (bf16[208,1024]{1,0:T(8,128)(2,1)S(1)}, bf16[208,1024]{1,0:T(8,128)(2,1)S(1)}, u32[]{:S(2)}, u32[]{:S(2)}) collective-permute-start(bf16[208,1024]{1,0:T(8,128)(2,1)S(1)} %get-tuple-element.58), channel_id=1, source_target_pairs={{0,1},{1,2},{2,3},{4,5},{5,6},{6,7},{8,9},{9,10},{10,11},{12,13},{... | collective-permute-start | bytes 1277960 | tf_op jit(solution)/shard_map/while/body/ppermute | solution.py:469
  122.5 14.2 %all-to-all-start = ((bf16[32,24,128]{2,1,0:T(8,128)(2,1)}), bf16[32,24,128]{2,1,0:T(8,128)(2,1)S(1)}, u32[]{:S(2)}, u32[]{:S(2)}) async-start(bf16[32,24,128]{2,1,0:T(8,128)(2,1)} %head.2), calls=%async_computation | async-start | bytes 393216 | tf_op jit(solution)/shard_map/all_to_all | solution.py:490
  136.6 0.7 copy-start.3
where the time goes:
time: 141 us; the launch traced here: 140 us
  Pallas kernels  60.3 us (43%)
  starting transfers between devices  52.8 us (37%)
  waiting for transfers between devices  23.9 us (17%)
  between operations  1.54 us (1%)
    pallas_call x12, Pallas kernels, run_tick(): pl.pallas_call(functools.partial(tick_kernel, toks=toks), out_shape=(pltp...  46.8 us
    ppermute x12, starting transfers between devices, advance(): coming = lax.ppermute(sent, 'section', chain)  41.7 us
    ppermute x12, waiting for transfers between devices, advance(): coming = lax.ppermute(sent, 'section', chain)  13.1 us
    all_to_all x1, waiting for transfers between devices, on_device(): got = lax.all_to_all(message, ('dp', 'section'), 0, 0, tiled=True)  8.56 us
    pallas_call x1, Pallas kernels, first_tick(): pl.pallas_call(functools.partial(first_kernel, images=images, toks=toks),...  7.56 us
    ppermute x3, starting transfers between devices, on_device(): lax.ppermute(query, 'dp', [(k, k ^ hop) for k in range(groups)])  6.12 us
    all_to_all x1, starting transfers between devices, on_device(): got = lax.all_to_all(message, ('dp', 'section'), 0, 0, tiled=True)  4.95 us
    pallas_call x1, Pallas kernels, on_device(): pl.pallas_call(functools.partial(final_kernel, images=images, extra=extra...  2.91 us
  transfers between devices with their start and end apart: 16, of which 6 were waited for; matrix products, arithmetic and copies ran while one was open for 0% of the time, Pallas kernels for 39%

commit v1 on v0

--- a/solution.py
+++ b/solution.py
@@ -15,7 +15,6 @@
 WIDE = 256
 SHARPNESS = 0.2
 HOP = 2
-UNROLL = 2
 
 
 def layer_norm(values, gain):
@@ -84,18 +83,26 @@
             ctx[:, o : o + LANES] = got.astype(BF16)
 
     groups = width // WIDE
+    late = (groups - 1) * WIDE
     ready(0)
     project(0)
+    if groups > 1:
+        project(1)
     found = scores(0)
     for j in range(groups):
+        coming = None
         if j + 1 < groups:
-            project(j + 1)
+            coming = scores(j + 1)
+        if j + 2 < groups:
+            project(j + 2)
+        if j + 1 == groups:
+            ready(1)
+            for n in range(0, width, WIDE):
+                res[:, n : n + WIDE] += mm(ctx[:, 0:late], wout[0:late, n : n + WIDE])
         mix(j, soften(found))
-        if j + 1 < groups:
-            found = scores(j + 1)
-    ready(1)
+        found = coming
     for n in range(0, width, WIDE):
-        res[:, n : n + WIDE] += mm(ctx[...], wout[:, n : n + WIDE])
+        res[:, n : n + WIDE] += mm(ctx[:, late:width], wout[late:width, n : n + WIDE])
     norm[...] = layer_norm(res[...], g2[...]).astype(BF16)
     ready(2)
     for n in range(0, ff, WIDE):
@@ -107,30 +114,64 @@
         out_ref[:, n : n + WIDE] = (res[:, n : n + WIDE] + mm(act[...], wfc2[:, n : n + WIDE])).astype(BF16)
 
 
-def encode_class(x_ref, g1, wqkv, wout, g2, wfc1, wfc2, norm, qkv, toks):
+def by_columns(left, right, start, stop, store, compact):
+    size = 2 * WIDE if compact else WIDE
+
+    def part(o):
+        store(o - start, mm(left, right[:, pl.ds(o, size)]))
+
+    if compact:
+        lax.fori_loop(start // size, stop // size, lambda k, _: (part(pl.multiple_of(k * size, size)), 0)[1], 0)
+    else:
+        for o in range(start, stop, size):
+            part(o)
+
+
+def encode_class(x_ref, g1, wqkv, wout, g2, wfc1, wfc2, norm, qkv, row, toks, compact):
     rows, width = norm.shape
+    ff = wfc1.shape[1]
     heads = width // HEAD_DIM
     scale = 1.0 / math.sqrt(HEAD_DIM)
     norm[...] = layer_norm(x_ref[...].astype(F32), g1[...]).astype(BF16)
-    q = mm(norm[0:16, :], wqkv[:, 0:width])[0:1, :] * scale
+
+    def keep(o, y):
+        row[:, pl.ds(o, y.shape[1])] = y
+
+    by_columns(norm[0:8, :], wqkv, 0, width, keep, compact)
+    q = row[0:1, 0:width] * scale
     own = lax.broadcasted_iota(jnp.int32, (heads, width), 1) // HEAD_DIM
     own = own == lax.broadcasted_iota(jnp.int32, (heads, width), 0)
     q = jnp.where(own, jnp.broadcast_to(q, (heads, width)), 0.0).astype(BF16)
-    for o in range(width, 2 * width, WIDE):
-        qkv[:, o : o + WIDE] = mm(norm[...], wqkv[:, o : o + WIDE]).astype(BF16)
-    s = mm_t(q, qkv[:, width : 2 * width])
+
+    def keys(o, y):
+        qkv[:, pl.ds(o, y.shape[1])] = y.astype(BF16)
+
+    by_columns(norm[...], wqkv, width, 2 * width, keys, compact)
+    s = mm_t(q, qkv[:, 0:width])
     s = jnp.where(lax.broadcasted_iota(jnp.int32, s.shape, 1) < toks, s, -1e30)
     e = jnp.exp(s - jnp.max(s, axis=-1, keepdims=True))
     p = (e / jnp.sum(e, axis=-1, keepdims=True)).astype(BF16)
     mixed = mm(p, norm[...]).astype(BF16)
-    c = mm(mixed, wqkv[:, 2 * width : 3 * width])
-    c = jnp.sum(jnp.where(own, c, 0.0), axis=0, keepdims=True)
-    c = jnp.broadcast_to(c, (8, width)).astype(BF16)
-    r = x_ref[0:8, :].astype(F32)[0:1, :] + mm(c, wout[...])
+
+    def values(o, y):
+        lane = lax.broadcasted_iota(jnp.int32, y.shape, 1) + o
+        mine = lane // HEAD_DIM == lax.broadcasted_iota(jnp.int32, y.shape, 0)
+        y = jnp.sum(jnp.where(mine, y, 0.0), axis=0, keepdims=True)
+        row[:, pl.ds(o, y.shape[1])] = jnp.broadcast_to(y, (8, y.shape[1]))
+
+    by_columns(mixed, wqkv, 2 * width, 3 * width, values, compact)
+    c = row[:, 0:width].astype(BF16)
+    by_columns(c, wout, 0, width, keep, compact)
+    r = x_ref[0:8, :].astype(F32) + row[:, 0:width]
     n = layer_norm(r, g2[...]).astype(BF16)
-    t = mm(n, wfc1[...])
-    t = 0.5 * t * (1.0 + lax.erf(t * (1.0 / math.sqrt(2.0))))
-    return (r + mm(t.astype(BF16), wfc2[...]))[0:1, :].astype(BF16).astype(F32)
+
+    def active(o, t):
+        row[:, pl.ds(o, t.shape[1])] = 0.5 * t * (1.0 + lax.erf(t * (1.0 / math.sqrt(2.0))))
+
+    by_columns(n, wfc1, 0, ff, active, compact)
+    t = row[:, 0:ff].astype(BF16)
+    by_columns(t, wfc2, 0, width, keep, compact)
+    return (r + row[:, 0:width])[0:1, :].astype(BF16).astype(F32)
 
 
 def first_kernel(
@@ -144,10 +185,10 @@
     ]
     total = toks * images
     fetch = pltpu.make_async_copy(patch_hbm, flat.at[0:total, :], sems.at[4])
-    fetch.start()
+    section = lax.axis_index("section")
+    pl.when(section == 0)(fetch.start)
     for c in copies:
         c.start()
-    section = lax.axis_index("section")
     marks[...] = jnp.zeros_like(marks)
     blank[...] = jnp.zeros_like(blank)
     count[0] = 1
@@ -174,7 +215,6 @@
 
     @pl.when(section != 0)
     def _():
-        fetch.wait()
         for c in copies:
             c.wait()
 
@@ -216,7 +256,7 @@
 
 
 def tick_kernel(
-    tick, turned, came, marks_in, g1, wqkv, wout, g2, wfc1, wfc2, out_ref, marks, after, norm, qkv, ctx, res, act, *, toks
+    tick, turned, came, marks_in, g1, wqkv, wout, g2, wfc1, wfc2, out_ref, marks, after, norm, qkv, ctx, res, act, row, *, toks
 ):
     after[0] = tick[0] + 1
     section = lax.axis_index("section")
@@ -243,7 +283,7 @@
 
     @pl.when(jnp.logical_and(active, section == last))
     def _():
-        marks[pl.ds(step, 1), :] = encode_class(came, g1, wqkv, wout, g2, wfc1, wfc2, norm, qkv, toks)
+        marks[pl.ds(step, 1), :] = encode_class(came, g1, wqkv, wout, g2, wfc1, wfc2, norm, qkv, row, toks, True)
 
 
 def hold(x):
@@ -274,6 +314,7 @@
             pltpu.VMEM((rows, width), BF16),
             pltpu.VMEM((rows, width), F32),
             pltpu.VMEM((rows, ff), BF16),
+            pltpu.VMEM((8, max(ff, width)), F32),
         ],
         input_output_aliases={3: 1},
         compiler_params=pltpu.CompilerParams(vmem_limit_bytes=12 * 2**20),
@@ -299,20 +340,45 @@
     )(left, right)
 
 
-def lse_kernel(swapped, queue_hbm, out_ref, query_ref, copy_ref, ordered, queue, sems, *, images):
-    fetch = pltpu.make_async_copy(queue_hbm, queue, sems.at[0])
-    fetch.start()
+def class_kernel(came, marks_in, g1, wqkv, wout, g2, wfc1, wfc2, marks, norm, qkv, row, *, toks):
+    step = marks.shape[0] - 2
+
+    @pl.when(lax.axis_index("section") == lax.axis_size("section") - 1)
+    def _():
+        marks[step : step + 1, :] = encode_class(came, g1, wqkv, wout, g2, wfc1, wfc2, norm, qkv, row, toks, True)
+
+
+def run_class(came, marks, weights, toks):
+    rows, width = came.shape
+    whole = pl.BlockSpec(memory_space=pltpu.VMEM)
+    return pl.pallas_call(
+        functools.partial(class_kernel, toks=toks),
+        out_shape=pltpu.VMEM(marks.shape, F32),
+        in_specs=[whole] * 8,
+        out_specs=whole,
+        scratch_shapes=[
+            pltpu.VMEM((rows, width), BF16),
+            pltpu.VMEM((rows, width), BF16),
+            pltpu.VMEM((8, max(weights[4].shape[1], width)), F32),
+        ],
+        input_output_aliases={1: 0},
+        compiler_params=pltpu.CompilerParams(vmem_limit_bytes=12 * 2**20),
+        name="class",
+    )(hold(came), hold(marks), *held_weights(weights))
+
+
+def straighten(swapped, ordered, images):
     group = lax.axis_index("dp")
-    count = swapped.shape[0]
     ordered[...] = jnp.zeros_like(ordered)
-    for b in range(count // images):
+    for b in range(swapped.shape[0] // images):
         place = pl.multiple_of(jnp.bitwise_xor(group, b) * images, images)
         ordered[pl.ds(place, images), :] = swapped[b * images : (b + 1) * images, :].astype(F32)
-    query_ref[...] = ordered[0:count, :].astype(BF16)
+
+
+def score_shard(fetch, back, out_ref, ordered, queue):
+    lanes = out_ref.shape[1]
     fetch.wait()
-    back = pltpu.make_async_copy(queue, copy_ref, sems.at[1])
     back.start()
-    lanes = out_ref.shape[1]
     for k in range(out_ref.shape[0]):
         s = mm_t(queue[...], ordered[k * lanes : (k + 1) * lanes, :].astype(BF16)) * (1.0 / SHARPNESS)
         peak = jnp.max(s, axis=0, keepdims=True)
@@ -320,13 +386,40 @@
     back.wait()
 
 
-def head_kernel(came, marks, g1, wqkv, wout, g2, wfc1, wfc2, gain, head, lse, out_ref, found, norm, qkv, *, toks):
+def early_kernel(swapped, queue_hbm, out_ref, copy_ref, query_ref, ordered, queue, sems, *, images):
+    straighten(swapped, ordered, images)
+    query_ref[...] = ordered[0 : query_ref.shape[0], :].astype(BF16)
+
+    @pl.when(lax.axis_index("section") == lax.axis_size("section") - 1)
+    def _():
+        fetch = pltpu.make_async_copy(queue_hbm, queue, sems.at[0])
+        back = pltpu.make_async_copy(queue, copy_ref, sems.at[1])
+        fetch.start()
+        score_shard(fetch, back, out_ref, ordered, queue)
+
+
+def late_kernel(query, queue_hbm, lse_in, copy_in, out_ref, copy_ref, ordered, queue, sems):
+    @pl.when(lax.axis_index("section") != lax.axis_size("section") - 1)
+    def _():
+        fetch = pltpu.make_async_copy(queue_hbm, queue, sems.at[0])
+        back = pltpu.make_async_copy(queue, copy_ref, sems.at[1])
+        fetch.start()
+        ordered[...] = jnp.zeros_like(ordered)
+        ordered[0 : query.shape[0], :] = query[...].astype(F32)
+        score_shard(fetch, back, out_ref, ordered, queue)
+
+    @pl.when(lax.axis_index("section") == lax.axis_size("section") - 1)
+    def _():
+        out_ref[...] = lse_in[...]
+
+
+def head_kernel(came, marks, g1, wqkv, wout, g2, wfc1, wfc2, gain, head, lse, out_ref, found, norm, qkv, row, *, toks):
     images = found.shape[0]
 
     @pl.when(lax.axis_index("section") == lax.axis_size("section") - 1)
     def _():
         found[...] = marks[...]
-        found[images - 1 : images, :] = encode_class(came, g1, wqkv, wout, g2, wfc1, wfc2, norm, qkv, toks)
+        found[images - 1 : images, :] = encode_class(came, g1, wqkv, wout, g2, wfc1, wfc2, norm, qkv, row, toks, False)
 
     @pl.when(lax.axis_index("section") != lax.axis_size("section") - 1)
     def _():
@@ -374,6 +467,15 @@
         pieces.append(jnp.concatenate([one[h * images : (h + 1) * images] for h in range(halves)], axis=1))
     keys = jnp.concatenate(pieces, axis=0)
     keys16 = keys.astype(BF16)
+    row = lax.broadcasted_iota(jnp.int32, (span, count), 0) + (base - local)
+    slot = owner[...] - group * images
+    pick = jnp.logical_and(row == slot, jnp.logical_and(slot >= 0, slot < images))
+    fresh = mm(pick.astype(F32).astype(BF16), keys16)
+    hit = jnp.sum(pick.astype(F32), axis=1, keepdims=True) > 0.5
+    fetch.wait()
+    window[...] = jnp.where(hit, fresh, window[...].astype(F32)).astype(BF16)
+    back = pltpu.make_async_copy(window, queue_ref.at[pl.ds(base, span), :], sem)
+    back.start()
     msgs = got[...].astype(F32)
     off = halves * images
     lse = msgs[:, off : off + extra, :] + msgs[:, off + extra : off + 2 * extra, :] + msgs[:, off + 2 * extra : off + 3 * extra, :]
@@ -392,15 +494,6 @@
     loss_ref[...] = turned[0:1, 0:images]
     mine = got[group * n_sec + n_sec - 1].astype(F32)
     keys_ref[...] = jnp.concatenate([mine[h * images : (h + 1) * images] for h in range(halves)], axis=1).astype(BF16)
-    row = lax.broadcasted_iota(jnp.int32, (span, count), 0) + (base - local)
-    slot = owner[...] - group * images
-    pick = jnp.logical_and(row == slot, jnp.logical_and(slot >= 0, slot < images))
-    fresh = mm(pick.astype(F32).astype(BF16), keys16)
-    hit = jnp.sum(pick.astype(F32), axis=1, keepdims=True) > 0.5
-    fetch.wait()
-    window[...] = jnp.where(hit, fresh, window[...].astype(F32)).astype(BF16)
-    back = pltpu.make_async_copy(window, queue_ref.at[pl.ds(base, span), :], sem)
-    back.start()
     back.wait()
 
 
@@ -427,52 +520,83 @@
     kd = w_head.shape[1]
     peers = sections * groups
     count = groups * images
-    rows = -(-toks // 16) * 16
+    rows = -(-toks // 8) * 8
     whole = pl.BlockSpec(memory_space=pltpu.VMEM)
     smem = pl.BlockSpec(memory_space=pltpu.SMEM)
     hbm = pl.BlockSpec(memory_space=pl.ANY)
 
-    query = online_embeddings
-    hop = 1
-    while hop < groups:
-        query = merge(query, lax.ppermute(query, "dp", [(k, k ^ hop) for k in range(groups)]))
-        hop *= 2
     extra = -(-count // LANES)
-    lse, query, queue_copy = pl.pallas_call(
-        functools.partial(lse_kernel, images=images),
-        out_shape=(
-            pltpu.VMEM((extra, LANES), F32),
-            pltpu.VMEM((count, kd), BF16),
-            jax.ShapeDtypeStruct(queue.shape, BF16),
-        ),
-        in_specs=[whole, hbm],
-        out_specs=(whole, whole, hbm),
-        scratch_shapes=[
-            pltpu.VMEM((extra * LANES, kd), F32),
-            pltpu.VMEM(queue.shape, BF16),
-            pltpu.SemaphoreType.DMA((2,)),
-        ],
-        compiler_params=pltpu.CompilerParams(vmem_limit_bytes=4 * 2**20),
-        name="lse",
-    )(query, far(queue))
-
+    limit = pltpu.CompilerParams(vmem_limit_bytes=4 * 2**20)
+    shapes = (pltpu.VMEM((extra, LANES), F32), jax.ShapeDtypeStruct(queue.shape, BF16))
+    work = [
+        pltpu.VMEM((extra * LANES, kd), F32),
+        pltpu.VMEM(queue.shape, BF16),
+        pltpu.SemaphoreType.DMA((2,)),
+    ]
     chain = [(k, k + 1) for k in range(sections - 1)]
     ticks = images + HOP * (sections - 1)
+    hops = [1 << k for k in range(max(groups - 1, 1).bit_length()) if 1 << k < groups]
+
+    def exchange(rows, hop):
+        pairs = [(k * sections + j, (k ^ hop) * sections + j) for k in range(groups) for j in range(sections)]
+        return lax.ppermute(rows, ("dp", "section"), pairs)
+
+    swapped = online_embeddings
+    other = exchange(swapped, hops[0])
     sent, turned, *held, marks, blank, tick = first_tick(
         patches, (ln1_gain, w_qkv[0], w_out[0], ln2_gain, w_fc1[0], w_fc2[0]), rows
     )
     weights = (ln1_gain, held[0], held[1], ln2_gain, held[2], held[3])
+    loops = ticks - 4
+    unroll = next(k for k in (2, 1) if loops % k == 0)
+
+    def one(tick, came, sent, marks):
+        coming = lax.ppermute(sent, "section", chain)
+        sent, marks, tick = run_tick(tick, turned, came, marks, weights, toks)
+        return tick, coming, sent, marks
 
     def advance(carry):
-        tick, came, sent, marks = carry
-        for _ in range(UNROLL):
-            coming = lax.ppermute(sent, "section", chain)
-            sent, marks, tick = run_tick(tick, turned, came, marks, weights, toks)
-            came = coming
-        return tick, came, sent, marks
-
-    _, came, sent, marks = lax.while_loop(lambda carry: carry[0][0] < ticks - 1, advance, (tick, blank, sent, marks))
-
+        for _ in range(unroll):
+            carry = one(*carry)
+        return carry
+
+    other, sent = lax.optimization_barrier((other, sent))
+    swapped = merge(swapped, other)
+    if len(hops) > 1:
+        other = exchange(swapped, hops[1])
+    tick, came, sent, marks = one(tick, blank, sent, marks)
+    for hop in hops[1:]:
+        if hop != hops[1]:
+            other = exchange(swapped, hop)
+        other, sent = lax.optimization_barrier((other, sent))
+        swapped = merge(swapped, other)
+    lse, queue_copy, query = pl.pallas_call(
+        functools.partial(early_kernel, images=images),
+        out_shape=shapes + (pltpu.VMEM((count, kd), BF16),),
+        in_specs=[whole, hbm],
+        out_specs=(whole, hbm, whole),
+        scratch_shapes=work,
+        compiler_params=limit,
+        name="early",
+    )(hold(swapped), far(queue))
+    lse, sent = lax.optimization_barrier((lse, sent))
+    carry = lax.while_loop(lambda carry: carry[0][0] <= loops + 1, advance, (tick, came, sent, marks))
+    _, came, sent, marks = carry
+    coming = lax.ppermute(sent, "section", chain[-1:])
+    marks = run_class(came, marks, weights, toks)
+    came = coming
+
+    lse, marks = lax.optimization_barrier((lse, marks))
+    lse, queue_copy = pl.pallas_call(
+        late_kernel,
+        out_shape=shapes,
+        in_specs=[whole, hbm, whole, hbm],
+        out_specs=(whole, hbm),
+        scratch_shapes=work,
+        input_output_aliases={3: 1},
+        compiler_params=limit,
+        name="late",
+    )(hold(query), far(queue), hold(lse), far(queue_copy))
     height = -(-(kd // LANES * images + 3 * extra) // 8) * 8
     message = pl.pallas_call(
         functools.partial(head_kernel, toks=toks),
@@ -483,6 +607,7 @@
             pltpu.VMEM((images, width), F32),
             pltpu.VMEM((rows, width), BF16),
             pltpu.VMEM((rows, 3 * width), BF16),
+            pltpu.VMEM((8, max(w_fc1.shape[2], width)), F32),
         ],
         compiler_params=pltpu.CompilerParams(vmem_limit_bytes=12 * 2**20),
         name="head",
@@ -502,7 +627,7 @@
         scratch_shapes=[pltpu.VMEM((32, kd), BF16), pltpu.SemaphoreType.DMA],
         input_output_aliases={4: 3},
         name="final",
-    )(pointer, got, hold(query), owner.reshape(1, count), far(queue_copy))
+    )(pointer, hold(got), hold(query), owner.reshape(1, count), far(queue_copy))
     return keys, loss.reshape(images), total.reshape(()), new_queue
 
 

time: 141 us -> 130 us (0.922)
  waiting for transfers between devices: 23.9 us -> 15.8 us
  Pallas kernels: 60.3 us -> 57.5 us
    ppermute x15, waiting for transfers between devices: 15.4 us -> 7.24 us  [the longest x11 4.86 us: one(): coming = lax.ppermute(sent, 'section', chain)]
    all_to_all x1, starting transfers between devices: 4.95 us -> 9.56 us  [on_device(): got = lax.all_to_all(message, ('dp', 'section'), 0, 0, tiled=True)]
    ppermute x15, starting transfers between devices: 47.8 us -> 44.2 us  [the longest x11 37.8 us: one(): coming = lax.ppermute(sent, 'section', chain)]
    pallas_call x12 -> x11, Pallas kernels: 46.8 us -> 45 us  [run_tick(): pl.pallas_call(functools.partial(tick_kernel, toks=toks), out_shape=(pltp...]
  transfers between devices with their start and end apart: 16 -> 16, of which waited for: 6 -> 4; matrix products, arithmetic and copies ran while one was open for 0% -> 0% of each run, Pallas kernels for 39% -> 42%
where the time goes in v1:
time: 130 us; the launch traced here: 129 us
  Pallas kernels  57.5 us (44%)
  starting transfers between devices  53.8 us (41%)
  waiting for transfers between devices  15.8 us (12%)
  between operations  1.6 us (1%)
    pallas_call x11, Pallas kernels, run_tick(): pl.pallas_call(functools.partial(tick_kernel, toks=toks), out_shape=(pltp...  45 us
    ppermute x11, starting transfers between devices, one(): coming = lax.ppermute(sent, 'section', chain)  37.8 us
    all_to_all x1, starting transfers between devices, on_device(): got = lax.all_to_all(message, ('dp', 'section'), 0, 0, tiled=True)  9.56 us
    all_to_all x1, waiting for transfers between devices, on_device(): got = lax.all_to_all(message, ('dp', 'section'), 0, 0, tiled=True)  8.56 us
    pallas_call x1, Pallas kernels, first_tick(): pl.pallas_call(functools.partial(first_kernel, images=images, toks=toks),...  6.61 us
    ppermute x3, starting transfers between devices, exchange(): return lax.ppermute(rows, ('dp', 'section'), pairs)  5.79 us
    ppermute x11, waiting for transfers between devices, one(): coming = lax.ppermute(sent, 'section', chain)  4.86 us
    pallas_call x1, Pallas kernels, on_device(): pl.pallas_call(functools.partial(final_kernel, images=images, extra=extra...  2.74 us
  transfers between devices with their start and end apart: 16, of which 4 were waited for; matrix products, arithmetic and copies ran while one was open for 0% of the time, Pallas kernels for 42%

profile of v1, /device:TPU:1, one launch (start us, length us, event | category | flops | bytes accessed | tf_op | source)
XLA Modules:
  0.0 129.1 jit_solution(3666188646132190183)
XLA Ops:
  0.6 2.1 %collective-permute-start.2 = (bf16[8,256]{1,0:T(8,128)(2,1)}, bf16[8,256]{1,0:T(8,128)(2,1)S(1)}, u32[]{:S(2)}, u32[]{:S(2)}) collective-permute-start(bf16[8,256]{1,0:T(8,128)(2,1)} %left.1), channel_id=1, source_target_pairs={{0,4},{1,5},{2,6},{3,7},{4,0},{5,1},{6,2},{7,3},{8,12},{9,13},{10,... | collective-permute-start | bytes 12296 | tf_op jit(solution)/shard_map/ppermute | solution.py:542
  2.8 6.6 %first.1 = (bf16[200,1024]{1,0:T(8,128)(2,1)S(1)}, bf16[8,200,1024]{2,1,0:T(8,128)(2,1)S(1)}, bf16[1024,3072]{1,0:T(8,128)(2,1)S(1)}, bf16[1024,1024]{1,0:T(8,12...) custom-call(bf16[1576,1024]{1,0:T(8,128)(2,1)} %bitcast.16, ...), custom_call_target="tpu_custom_call" | custom-call | tf_op jit(solution)/shard_map/first/pallas_call | solution.py:229
  9.4 4.0 %collective-permute-start.3 = (bf16[200,1024]{1,0:T(8,128)(2,1)S(1)}, bf16[200,1024]{1,0:T(8,128)(2,1)S(1)}, u32[]{:S(2)}, u32[]{:S(2)}) collective-permute-start(bf16[200,1024]{1,0:T(8,128)(2,1)S(1)} %get-tuple-element.110), channel_id=1, source_target_pairs={{0,1},{1,2},{2,3},{4,5},{5,6},{6,7},{8,9},{9,10},{10,11},{12,13},{... | collective-permute-start | bytes 1228808 | tf_op jit(solution)/shard_map/ppermute | solution.py:554
  15.9 2.3 %collective-permute-start.5 = (bf16[32,256]{1,0:T(8,128)(2,1)S(1)}, bf16[32,256]{1,0:T(8,128)(2,1)S(1)}, u32[]{:S(2)}, u32[]{:S(2)}) collective-permute-start(bf16[32,256]{1,0:T(8,128)(2,1)S(1)} %merge.4.left), channel_id=1, source_target_pairs={{0,16},{1,17},{2,18},{3,19},{4,20},{5,21},{6,22},{7,23},{8,24},{9,... | collective-permute-start | bytes 49160 | tf_op jit(solution)/shard_map/ppermute | solution.py:542
  19.5 84.2 %while.13 = (s32[1]{0:T(128)S(4)}, bf16[200,1024]{1,0:T(8,128)(2,1)S(1)}, bf16[200,1024]{1,0:T(8,128)(2,1)S(1)}, f32[8,1024]{1,0:T(8,128)S(1)}, bf16[8,200,1024]...) while((s32[1]{0:T(128)S(4)}, ...), condition=%region_1.0_spmd, body=%region_0.0_spmd | while | flops 1 | bytes 3276977 | solution.py:583
  19.7 4.2 %collective-permute-start = (bf16[200,1024]{1,0:T(8,128)(2,1)S(1)}, bf16[200,1024]{1,0:T(8,128)(2,1)S(1)}, u32[]{:S(2)}, u32[]{:S(2)}) collective-permute-start(bf16[200,1024]{1,0:T(8,128)(2,1)S(1)} %get-tuple-element.180), channel_id=1, source_target_pairs={{0,1},{1,2},{2,3},{4,5},{5,6},{6,7},{8,9},{9,10},{10,11},{12,13},{... | collective-permute-start | bytes 1228808 | tf_op jit(solution)/shard_map/while/body/ppermute | solution.py:554
  23.9 5.6 %block.3 = (bf16[200,1024]{1,0:T(8,128)(2,1)S(1)}, f32[8,1024]{1,0:T(8,128)S(1)}, s32[1]{0:T(128)S(4)}) custom-call(s32[1]{0:T(128)S(4)} %get-tuple-element.178.tick, bf16[8,200,1024]{2,1,0:T(8,128)(2,1)S(1)} %get-tuple-element.193.turned, bf16[200,1024]{1,0:T(8,128)(2,1)S(1)} %get-tuple-element.179.came, ...), custom_call_target="tpu_custom_call", output_to_operand_aliasing={{1}: (3, {})} | custom-call | tf_op jit(solution)/shard_map/while/body/block/pallas_call | solution.py:306
  31.5 5.6 %block.4 = (bf16[200,1024]{1,0:T(8,128)(2,1)S(1)}, f32[8,1024]{1,0:T(8,128)S(1)}, s32[1]{0:T(128)S(4)}) custom-call(s32[1]{0:T(128)S(4)} %get-tuple-element.54.tick, bf16[8,200,1024]{2,1,0:T(8,128)(2,1)S(1)} %get-tuple-element.193.turned, bf16[200,1024]{1,0:T(8,128)(2,1)S(1)} %collective-permute-done.came, ...), custom_call_target="tpu_custom_call", output_to_operand_aliasing={{1}: (3, {})} | custom-call | tf_op jit(solution)/shard_map/while/body/block/pallas_call | solution.py:306
  37.1 3.6 %collective-permute-start = (bf16[200,1024]{1,0:T(8,128)(2,1)S(1)}, bf16[200,1024]{1,0:T(8,128)(2,1)S(1)}, u32[]{:S(2)}, u32[]{:S(2)}) collective-permute-start(bf16[200,1024]{1,0:T(8,128)(2,1)S(1)} %get-tuple-element.180), channel_id=1, source_target_pairs={{0,1},{1,2},{2,3},{4,5},{5,6},{6,7},{8,9},{9,10},{10,11},{12,13},{... | collective-permute-start | bytes 1228808 | tf_op jit(solution)/shard_map/while/body/ppermute | solution.py:554
  40.7 5.6 %block.3 = (bf16[200,1024]{1,0:T(8,128)(2,1)S(1)}, f32[8,1024]{1,0:T(8,128)S(1)}, s32[1]{0:T(128)S(4)}) custom-call(s32[1]{0:T(128)S(4)} %get-tuple-element.178.tick, bf16[8,200,1024]{2,1,0:T(8,128)(2,1)S(1)} %get-tuple-element.193.turned, bf16[200,1024]{1,0:T(8,128)(2,1)S(1)} %get-tuple-element.179.came, ...), custom_call_target="tpu_custom_call", output_to_operand_aliasing={{1}: (3, {})} | custom-call | tf_op jit(solution)/shard_map/while/body/block/pallas_call | solution.py:306
  46.4 1.9 %collective-permute-start.1 = (bf16[200,1024]{1,0:T(8,128)(2,1)S(1)}, bf16[200,1024]{1,0:T(8,128)(2,1)S(1)}, u32[]{:S(2)}, u32[]{:S(2)}) collective-permute-start(bf16[200,1024]{1,0:T(8,128)(2,1)S(1)} %get-tuple-element.58), channel_id=1, source_target_pairs={{0,1},{1,2},{2,3},{4,5},{5,6},{6,7},{8,9},{9,10},{10,11},{12,13},{... | collective-permute-start | bytes 1228808 | tf_op jit(solution)/shard_map/while/body/ppermute | solution.py:554
  48.3 5.6 %block.4 = (bf16[200,1024]{1,0:T(8,128)(2,1)S(1)}, f32[8,1024]{1,0:T(8,128)S(1)}, s32[1]{0:T(128)S(4)}) custom-call(s32[1]{0:T(128)S(4)} %get-tuple-element.54.tick, bf16[8,200,1024]{2,1,0:T(8,128)(2,1)S(1)} %get-tuple-element.193.turned, bf16[200,1024]{1,0:T(8,128)(2,1)S(1)} %collective-permute-done.came, ...), custom_call_target="tpu_custom_call", output_to_operand_aliasing={{1}: (3, {})} | custom-call | tf_op jit(solution)/shard_map/while/body/block/pallas_call | solution.py:306
  54.0 3.6 %collective-permute-start = (bf16[200,1024]{1,0:T(8,128)(2,1)S(1)}, bf16[200,1024]{1,0:T(8,128)(2,1)S(1)}, u32[]{:S(2)}, u32[]{:S(2)}) collective-permute-start(bf16[200,1024]{1,0:T(8,128)(2,1)S(1)} %get-tuple-element.180), channel_id=1, source_target_pairs={{0,1},{1,2},{2,3},{4,5},{5,6},{6,7},{8,9},{9,10},{10,11},{12,13},{... | collective-permute-start | bytes 1228808 | tf_op jit(solution)/shard_map/while/body/ppermute | solution.py:554
  57.6 5.6 %block.3 = (bf16[200,1024]{1,0:T(8,128)(2,1)S(1)}, f32[8,1024]{1,0:T(8,128)S(1)}, s32[1]{0:T(128)S(4)}) custom-call(s32[1]{0:T(128)S(4)} %get-tuple-element.178.tick, bf16[8,200,1024]{2,1,0:T(8,128)(2,1)S(1)} %get-tuple-element.193.turned, bf16[200,1024]{1,0:T(8,128)(2,1)S(1)} %get-tuple-element.179.came, ...), custom_call_target="tpu_custom_call", output_to_operand_aliasing={{1}: (3, {})} | custom-call | tf_op jit(solution)/shard_map/while/body/block/pallas_call | solution.py:306
  65.1 5.6 %block.4 = (bf16[200,1024]{1,0:T(8,128)(2,1)S(1)}, f32[8,1024]{1,0:T(8,128)S(1)}, s32[1]{0:T(128)S(4)}) custom-call(s32[1]{0:T(128)S(4)} %get-tuple-element.54.tick, bf16[8,200,1024]{2,1,0:T(8,128)(2,1)S(1)} %get-tuple-element.193.turned, bf16[200,1024]{1,0:T(8,128)(2,1)S(1)} %collective-permute-done.came, ...), custom_call_target="tpu_custom_call", output_to_operand_aliasing={{1}: (3, {})} | custom-call | tf_op jit(solution)/shard_map/while/body/block/pallas_call | solution.py:306
  70.8 3.6 %collective-permute-start = (bf16[200,1024]{1,0:T(8,128)(2,1)S(1)}, bf16[200,1024]{1,0:T(8,128)(2,1)S(1)}, u32[]{:S(2)}, u32[]{:S(2)}) collective-permute-start(bf16[200,1024]{1,0:T(8,128)(2,1)S(1)} %get-tuple-element.180), channel_id=1, source_target_pairs={{0,1},{1,2},{2,3},{4,5},{5,6},{6,7},{8,9},{9,10},{10,11},{12,13},{... | collective-permute-start | bytes 1228808 | tf_op jit(solution)/shard_map/while/body/ppermute | solution.py:554
  74.4 5.6 %block.3 = (bf16[200,1024]{1,0:T(8,128)(2,1)S(1)}, f32[8,1024]{1,0:T(8,128)S(1)}, s32[1]{0:T(128)S(4)}) custom-call(s32[1]{0:T(128)S(4)} %get-tuple-element.178.tick, bf16[8,200,1024]{2,1,0:T(8,128)(2,1)S(1)} %get-tuple-element.193.turned, bf16[200,1024]{1,0:T(8,128)(2,1)S(1)} %get-tuple-element.179.came, ...), custom_call_target="tpu_custom_call", output_to_operand_aliasing={{1}: (3, {})} | custom-call | tf_op jit(solution)/shard_map/while/body/block/pallas_call | solution.py:306
  82.0 5.6 %block.4 = (bf16[200,1024]{1,0:T(8,128)(2,1)S(1)}, f32[8,1024]{1,0:T(8,128)S(1)}, s32[1]{0:T(128)S(4)}) custom-call(s32[1]{0:T(128)S(4)} %get-tuple-element.54.tick, bf16[8,200,1024]{2,1,0:T(8,128)(2,1)S(1)} %get-tuple-element.193.turned, bf16[200,1024]{1,0:T(8,128)(2,1)S(1)} %collective-permute-done.came, ...), custom_call_target="tpu_custom_call", output_to_operand_aliasing={{1}: (3, {})} | custom-call | tf_op jit(solution)/shard_map/while/body/block/pallas_call | solution.py:306
  87.6 3.6 %collective-permute-start = (bf16[200,1024]{1,0:T(8,128)(2,1)S(1)}, bf16[200,1024]{1,0:T(8,128)(2,1)S(1)}, u32[]{:S(2)}, u32[]{:S(2)}) collective-permute-start(bf16[200,1024]{1,0:T(8,128)(2,1)S(1)} %get-tuple-element.180), channel_id=1, source_target_pairs={{0,1},{1,2},{2,3},{4,5},{5,6},{6,7},{8,9},{9,10},{10,11},{12,13},{... | collective-permute-start | bytes 1228808 | tf_op jit(solution)/shard_map/while/body/ppermute | solution.py:554
  91.2 7.5 %collective-permute-start.1 = (bf16[200,1024]{1,0:T(8,128)(2,1)S(1)}, bf16[200,1024]{1,0:T(8,128)(2,1)S(1)}, u32[]{:S(2)}, u32[]{:S(2)}) collective-permute-start(bf16[200,1024]{1,0:T(8,128)(2,1)S(1)} %get-tuple-element.58), channel_id=1, source_target_pairs={{0,1},{1,2},{2,3},{4,5},{5,6},{6,7},{8,9},{9,10},{10,11},{12,13},{... | collective-permute-start | bytes 1228808 | tf_op jit(solution)/shard_map/while/body/ppermute | solution.py:554
  98.8 4.8 %collective-permute-done.1 = bf16[200,1024]{1,0:T(8,128)(2,1)S(1)} collective-permute-done((bf16[200,1024]{1,0:T(8,128)(2,1)S(1)}, bf16[200,1024]{1,0:T(8,128)(2,1)S(1)}, u32[]{:S(2)}, u32[]{:S(2)}) %collective-permute-start.1) | collective-permute-done | bytes 409632 | tf_op jit(solution)/shard_map/while/body/ppermute | solution.py:554
  107.5 9.6 %all-to-all-start = ((bf16[32,24,128]{2,1,0:T(8,128)(2,1)}), bf16[32,24,128]{2,1,0:T(8,128)(2,1)S(1)}, u32[]{:S(2)}, u32[]{:S(2)}) async-start(bf16[32,24,128]{2,1,0:T(8,128)(2,1)} %head.2), calls=%async_computation | async-start | bytes 393216 | tf_op jit(solution)/shard_map/all_to_all | solution.py:615
  117.7 8.6 %all-to-all-done.got = bf16[32,24,128]{2,1,0:T(8,128)(2,1)S(1)} async-done(((bf16[32,24,128]{2,1,0:T(8,128)(2,1)}), bf16[32,24,128]{2,1,0:T(8,128)(2,1)S(1)}, u32[]{:S(2)}, u32[]{:S(2)}) %all-to-all-start) | async-done | bytes 196640 | tf_op jit(solution)/shard_map/all_to_all | solution.py:615
  126.2 2.7 %final.1 = (bf16[8,256]{1,0:T(8,128)(2,1)}, f32[1,8]{1,0:T(1,128)}, f32[1,1]{1,0:T(1,128)}, bf16[1024,256]{1,0:T(8,128)(2,1)}) custom-call(s32[1]{0:T(128)S(6)} %copy.41.pointer, bf16[32,24,128]{2,1,0:T(8,128)(2,1)S(1)} %all-to-all-done.got, bf16[64,256]{1,0:T(8,128)(2,1)S(1)} %get-tuple-element.125.query, ...), custom_call_target="tpu_custom_call", output_to_operand_aliasing={{3}: (4, {})} | custom-call | tf_op jit(solution)/shard_map/final/pallas_call | solution.py:617
  (39 shorter events, 13.4 us)
Async XLA Ops:
  0.6 8.7 %collective-permute-start.2 = (bf16[8,256]{1,0:T(8,128)(2,1)}, bf16[8,256]{1,0:T(8,128)(2,1)S(1)}, u32[]{:S(2)}, u32[]{:S(2)}) collective-permute-start(bf16[8,256]{1,0:T(8,128)(2,1)} %left.1), channel_id=1, source_target_pairs={{0,4},{1,5},{2,6},{3,7},{4,0},{5,1},{6,2},{7,3},{8,12},{9,13},{10,... | collective-permute-start | bytes 12296 | tf_op jit(solution)/shard_map/ppermute | solution.py:542
  2.8 10.6 %copy-start.2 = (bf16[8,256]{1,0:T(8,128)(2,1)S(1)}, bf16[8,256]{1,0:T(8,128)(2,1)}, u32[]{:S(2)}) copy-start(bf16[8,256]{1,0:T(8,128)(2,1)} %left.1) | copy-start | bytes 12292
  2.8 12.0 %copy-start.3 = (f32[1,1024]{1,0:T(1,128)S(1)}, f32[1,1024]{1,0:T(1,128)}, u32[]{:S(2)}) copy-start(f32[1,1024]{1,0:T(1,128)} %g1.7) | copy-start | bytes 12292
  2.8 12.0 %copy-start.4 = (f32[1,1024]{1,0:T(1,128)S(1)}, f32[1,1024]{1,0:T(1,128)}, u32[]{:S(2)}) copy-start(f32[1,1024]{1,0:T(1,128)} %g2.7) | copy-start | bytes 12292
  9.4 10.1 %collective-permute-start.3 = (bf16[200,1024]{1,0:T(8,128)(2,1)S(1)}, bf16[200,1024]{1,0:T(8,128)(2,1)S(1)}, u32[]{:S(2)}, u32[]{:S(2)}) collective-permute-start(bf16[200,1024]{1,0:T(8,128)(2,1)S(1)} %get-tuple-element.110), channel_id=1, source_target_pairs={{0,1},{1,2},{2,3},{4,5},{5,6},{6,7},{8,9},{9,10},{10,11},{12,13},{... | collective-permute-start | bytes 1228808 | tf_op jit(solution)/shard_map/ppermute | solution.py:554
  13.4 2.6 %collective-permute-start.4 = (bf16[16,256]{1,0:T(8,128)(2,1)S(1)}, bf16[16,256]{1,0:T(8,128)(2,1)S(1)}, u32[]{:S(2)}, u32[]{:S(2)}) collective-permute-start(bf16[16,256]{1,0:T(8,128)(2,1)S(1)} %merge.3.left), channel_id=1, source_target_pairs={{0,8},{1,9},{2,10},{3,11},{4,12},{5,13},{6,14},{7,15},{8,0},{9,1},... | collective-permute-start | bytes 24584 | tf_op jit(solution)/shard_map/ppermute | solution.py:542
  15.9 3.5 %collective-permute-start.5 = (bf16[32,256]{1,0:T(8,128)(2,1)S(1)}, bf16[32,256]{1,0:T(8,128)(2,1)S(1)}, u32[]{:S(2)}, u32[]{:S(2)}) collective-permute-start(bf16[32,256]{1,0:T(8,128)(2,1)S(1)} %merge.4.left), channel_id=1, source_target_pairs={{0,16},{1,17},{2,18},{3,19},{4,20},{5,21},{6,22},{7,23},{8,24},{9,... | collective-permute-start | bytes 49160 | tf_op jit(solution)/shard_map/ppermute | solution.py:542
  19.7 11.8 %collective-permute-start = (bf16[200,1024]{1,0:T(8,128)(2,1)S(1)}, bf16[200,1024]{1,0:T(8,128)(2,1)S(1)}, u32[]{:S(2)}, u32[]{:S(2)}) collective-permute-start(bf16[200,1024]{1,0:T(8,128)(2,1)S(1)} %get-tuple-element.180), channel_id=1, source_target_pairs={{0,1},{1,2},{2,3},{4,5},{5,6},{6,7},{8,9},{9,10},{10,11},{12,13},{... | collective-permute-start | bytes 1228808 | tf_op jit(solution)/shard_map/while/body/ppermute | solution.py:554
  29.6 7.6 %collective-permute-start.1 = (bf16[200,1024]{1,0:T(8,128)(2,1)S(1)}, bf16[200,1024]{1,0:T(8,128)(2,1)S(1)}, u32[]{:S(2)}, u32[]{:S(2)}) collective-permute-start(bf16[200,1024]{1,0:T(8,128)(2,1)S(1)} %get-tuple-element.58), channel_id=1, source_target_pairs={{0,1},{1,2},{2,3},{4,5},{5,6},{6,7},{8,9},{9,10},{10,11},{12,13},{... | collective-permute-start | bytes 1228808 | tf_op jit(solution)/shard_map/while/body/ppermute | solution.py:554
  37.1 11.2 %collective-permute-start = (bf16[200,1024]{1,0:T(8,128)(2,1)S(1)}, bf16[200,1024]{1,0:T(8,128)(2,1)S(1)}, u32[]{:S(2)}, u32[]{:S(2)}) collective-permute-start(bf16[200,1024]{1,0:T(8,128)(2,1)S(1)} %get-tuple-element.180), channel_id=1, source_target_pairs={{0,1},{1,2},{2,3},{4,5},{5,6},{6,7},{8,9},{9,10},{10,11},{12,13},{... | collective-permute-start | bytes 1228808 | tf_op jit(solution)/shard_map/while/body/ppermute | solution.py:554
  46.4 7.6 %collective-permute-start.1 = (bf16[200,1024]{1,0:T(8,128)(2,1)S(1)}, bf16[200,1024]{1,0:T(8,128)(2,1)S(1)}, u32[]{:S(2)}, u32[]{:S(2)}) collective-permute-start(bf16[200,1024]{1,0:T(8,128)(2,1)S(1)} %get-tuple-element.58), channel_id=1, source_target_pairs={{0,1},{1,2},{2,3},{4,5},{5,6},{6,7},{8,9},{9,10},{10,11},{12,13},{... | collective-permute-start | bytes 1228808 | tf_op jit(solution)/shard_map/while/body/ppermute | solution.py:554
  54.0 11.1 %collective-permute-start = (bf16[200,1024]{1,0:T(8,128)(2,1)S(1)}, bf16[200,1024]{1,0:T(8,128)(2,1)S(1)}, u32[]{:S(2)}, u32[]{:S(2)}) collective-permute-start(bf16[200,1024]{1,0:T(8,128)(2,1)S(1)} %get-tuple-element.180), channel_id=1, source_target_pairs={{0,1},{1,2},{2,3},{4,5},{5,6},{6,7},{8,9},{9,10},{10,11},{12,13},{... | collective-permute-start | bytes 1228808 | tf_op jit(solution)/shard_map/while/body/ppermute | solution.py:554
  63.2 7.6 %collective-permute-start.1 = (bf16[200,1024]{1,0:T(8,128)(2,1)S(1)}, bf16[200,1024]{1,0:T(8,128)(2,1)S(1)}, u32[]{:S(2)}, u32[]{:S(2)}) collective-permute-start(bf16[200,1024]{1,0:T(8,128)(2,1)S(1)} %get-tuple-element.58), channel_id=1, source_target_pairs={{0,1},{1,2},{2,3},{4,5},{5,6},{6,7},{8,9},{9,10},{10,11},{12,13},{... | collective-permute-start | bytes 1228808 | tf_op jit(solution)/shard_map/while/body/ppermute | solution.py:554
  70.8 11.2 %collective-permute-start = (bf16[200,1024]{1,0:T(8,128)(2,1)S(1)}, bf16[200,1024]{1,0:T(8,128)(2,1)S(1)}, u32[]{:S(2)}, u32[]{:S(2)}) collective-permute-start(bf16[200,1024]{1,0:T(8,128)(2,1)S(1)} %get-tuple-element.180), channel_id=1, source_target_pairs={{0,1},{1,2},{2,3},{4,5},{5,6},{6,7},{8,9},{9,10},{10,11},{12,13},{... | collective-permute-start | bytes 1228808 | tf_op jit(solution)/shard_map/while/body/ppermute | solution.py:554
  80.0 7.6 %collective-permute-start.1 = (bf16[200,1024]{1,0:T(8,128)(2,1)S(1)}, bf16[200,1024]{1,0:T(8,128)(2,1)S(1)}, u32[]{:S(2)}, u32[]{:S(2)}) collective-permute-start(bf16[200,1024]{1,0:T(8,128)(2,1)S(1)} %get-tuple-element.58), channel_id=1, source_target_pairs={{0,1},{1,2},{2,3},{4,5},{5,6},{6,7},{8,9},{9,10},{10,11},{12,13},{... | collective-permute-start | bytes 1228808 | tf_op jit(solution)/shard_map/while/body/ppermute | solution.py:554
  87.6 11.2 %collective-permute-start = (bf16[200,1024]{1,0:T(8,128)(2,1)S(1)}, bf16[200,1024]{1,0:T(8,128)(2,1)S(1)}, u32[]{:S(2)}, u32[]{:S(2)}) collective-permute-start(bf16[200,1024]{1,0:T(8,128)(2,1)S(1)} %get-tuple-element.180), channel_id=1, source_target_pairs={{0,1},{1,2},{2,3},{4,5},{5,6},{6,7},{8,9},{9,10},{10,11},{12,13},{... | collective-permute-start | bytes 1228808 | tf_op jit(solution)/shard_map/while/body/ppermute | solution.py:554
  91.2 12.4 %collective-permute-start.1 = (bf16[200,1024]{1,0:T(8,128)(2,1)S(1)}, bf16[200,1024]{1,0:T(8,128)(2,1)S(1)}, u32[]{:S(2)}, u32[]{:S(2)}) collective-permute-start(bf16[200,1024]{1,0:T(8,128)(2,1)S(1)} %get-tuple-element.58), channel_id=1, source_target_pairs={{0,1},{1,2},{2,3},{4,5},{5,6},{6,7},{8,9},{9,10},{10,11},{12,13},{... | collective-permute-start | bytes 1228808 | tf_op jit(solution)/shard_map/while/body/ppermute | solution.py:554
  103.7 2.7 %collective-permute-start.6 = (bf16[200,1024]{1,0:T(8,128)(2,1)S(1)}, bf16[200,1024]{1,0:T(8,128)(2,1)S(1)}, u32[]{:S(2)}, u32[]{:S(2)}) collective-permute-start(bf16[200,1024]{1,0:T(8,128)(2,1)S(1)} %get-tuple-element.120), channel_id=1, source_target_pairs={{2,3},{6,7},{10,11},{14,15},{18,19},{22,23},{26,27},{30,31}} | collective-permute-start | bytes 1228808 | tf_op jit(solution)/shard_map/ppermute | solution.py:585
  104.3 2.0 %copy-start = (bf16[1024,256]{1,0:T(8,128)(2,1)S(1)}, bf16[1024,256]{1,0:T(8,128)(2,1)}, u32[]{:S(2)}) copy-start(bf16[1024,256]{1,0:T(8,128)(2,1)} %head.3) | copy-start | bytes 1572868
  104.4 2.0 %copy-start.1 = (f32[1024]{0:T(1024)S(1)}, f32[1024]{0:T(1024)}, u32[]{:S(2)}) copy-start(f32[1024]{0:T(1024)} %param.22) | copy-start | bytes 12292
  107.5 18.8 %all-to-all-start = ((bf16[32,24,128]{2,1,0:T(8,128)(2,1)}), bf16[32,24,128]{2,1,0:T(8,128)(2,1)S(1)}, u32[]{:S(2)}, u32[]{:S(2)}) async-start(bf16[32,24,128]{2,1,0:T(8,128)(2,1)} %head.2), calls=%async_computation | async-start | bytes 393216 | tf_op jit(solution)/shard_map/all_to_all | solution.py:615

commit v2 on v1

--- a/solution.py
+++ b/solution.py
@@ -398,7 +398,22 @@
         score_shard(fetch, back, out_ref, ordered, queue)
 
 
-def late_kernel(query, queue_hbm, lse_in, copy_in, out_ref, copy_ref, ordered, queue, sems):
+def window_base(pointer, share, span):
+    local = pointer[0] - lax.axis_index("section") * share
+    return local, pl.multiple_of(jnp.clip((local // 16) * 16, 0, share - span), 16)
+
+
+def late_kernel(
+    query, queue_hbm, pointer, owner, lse_in, copy_in,
+    out_ref, copy_ref, window, owner_ref, pointer_ref, ordered, queue, sems,
+):
+    share, span = queue_hbm.shape[0], window.shape[0]
+    pointer_ref[0] = pointer[0]
+    owner_ref[...] = owner[...]
+    _, base = window_base(pointer, share, span)
+    bring = pltpu.make_async_copy(queue_hbm.at[pl.ds(base, span), :], window, sems.at[2])
+    bring.start()
+
     @pl.when(lax.axis_index("section") != lax.axis_size("section") - 1)
     def _():
         fetch = pltpu.make_async_copy(queue_hbm, queue, sems.at[0])
@@ -411,6 +426,8 @@
     @pl.when(lax.axis_index("section") == lax.axis_size("section") - 1)
     def _():
         out_ref[...] = lse_in[...]
+
+    bring.wait()
 
 
 def head_kernel(came, marks, g1, wqkv, wout, g2, wfc1, wfc2, gain, head, lse, out_ref, found, norm, qkv, row, *, toks):
@@ -443,21 +460,15 @@
 
 
 def final_kernel(
-    pointer, got, query, owner, queue_in, keys_ref, loss_ref, total_ref, queue_ref, window, sem, *, images, extra, kd
+    pointer, got, query, owner, window, queue_in, keys_ref, loss_ref, total_ref, queue_ref, merged, sem, *, images, kd
 ):
     section = lax.axis_index("section")
     group = lax.axis_index("dp")
-    start = pointer[0]
-    share = queue_ref.shape[0]
-    local = start - section * share
     span = window.shape[0]
-    base = jnp.clip((local // 16) * 16, 0, share - span)
-    base = pl.multiple_of(base, 16)
-    fetch = pltpu.make_async_copy(queue_ref.at[pl.ds(base, span), :], window, sem)
-    fetch.start()
+    local, base = window_base(pointer, queue_ref.shape[0], span)
+    extra = -(-query.shape[0] // got.shape[2])
     peers, rows, lanes = got.shape
     halves = kd // lanes
-    last = peers // query.shape[0] * images
     count = query.shape[0]
     n_sec = peers * images // count
     pieces = []
@@ -472,9 +483,8 @@
     pick = jnp.logical_and(row == slot, jnp.logical_and(slot >= 0, slot < images))
     fresh = mm(pick.astype(F32).astype(BF16), keys16)
     hit = jnp.sum(pick.astype(F32), axis=1, keepdims=True) > 0.5
-    fetch.wait()
-    window[...] = jnp.where(hit, fresh, window[...].astype(F32)).astype(BF16)
-    back = pltpu.make_async_copy(window, queue_ref.at[pl.ds(base, span), :], sem)
+    merged[...] = jnp.where(hit, fresh, window[...].astype(F32)).astype(BF16)
+    back = pltpu.make_async_copy(merged, queue_ref.at[pl.ds(base, span), :], sem)
     back.start()
     msgs = got[...].astype(F32)
     off = halves * images
@@ -531,7 +541,7 @@
     work = [
         pltpu.VMEM((extra * LANES, kd), F32),
         pltpu.VMEM(queue.shape, BF16),
-        pltpu.SemaphoreType.DMA((2,)),
+        pltpu.SemaphoreType.DMA((3,)),
     ]
     chain = [(k, k + 1) for k in range(sections - 1)]
     ticks = images + HOP * (sections - 1)
@@ -587,16 +597,21 @@
     came = coming
 
     lse, marks = lax.optimization_barrier((lse, marks))
-    lse, queue_copy = pl.pallas_call(
+    lse, queue_copy, window, owner_row, start = pl.pallas_call(
         late_kernel,
-        out_shape=shapes,
-        in_specs=[whole, hbm, whole, hbm],
-        out_specs=(whole, hbm),
+        out_shape=shapes
+        + (
+            pltpu.VMEM((32, kd), BF16),
+            pltpu.VMEM((1, count), jnp.int32),
+            pltpu.SMEM((1,), jnp.int32),
+        ),
+        in_specs=[whole, hbm, smem, whole, whole, hbm],
+        out_specs=(whole, hbm, whole, whole, smem),
         scratch_shapes=work,
-        input_output_aliases={3: 1},
+        input_output_aliases={5: 1},
         compiler_params=limit,
         name="late",
-    )(hold(query), far(queue), hold(lse), far(queue_copy))
+    )(hold(query), far(queue), pointer, owner.reshape(1, count), hold(lse), far(queue_copy))
     height = -(-(kd // LANES * images + 3 * extra) // 8) * 8
     message = pl.pallas_call(
         functools.partial(head_kernel, toks=toks),
@@ -615,19 +630,19 @@
     got = lax.all_to_all(message, ("dp", "section"), 0, 0, tiled=True)
 
     keys, loss, total, new_queue = pl.pallas_call(
-        functools.partial(final_kernel, images=images, extra=extra, kd=kd),
+        functools.partial(final_kernel, images=images, kd=kd),
         out_shape=(
             jax.ShapeDtypeStruct((images, kd), BF16),
             jax.ShapeDtypeStruct((1, images), F32),
             jax.ShapeDtypeStruct((1, 1), F32),
             jax.ShapeDtypeStruct(queue.shape, BF16),
         ),
-        in_specs=[smem, whole, whole, whole, hbm],
+        in_specs=[smem, whole, whole, whole, whole, hbm],
         out_specs=(whole, whole, whole, hbm),
         scratch_shapes=[pltpu.VMEM((32, kd), BF16), pltpu.SemaphoreType.DMA],
-        input_output_aliases={4: 3},
+        input_output_aliases={5: 3},
         name="final",
-    )(pointer, hold(got), hold(query), owner.reshape(1, count), far(queue_copy))
+    )(start, hold(got), hold(query), hold(owner_row), hold(window), far(queue_copy))
     return keys, loss.reshape(images), total.reshape(()), new_queue
 
 

time: 130 us -> 127 us (0.977)
  blocking collectives: 0 us -> 17.3 us
  starting transfers between devices: 53.8 us -> 44.2 us
  waiting for transfers between devices: 15.8 us -> 7.24 us
  Pallas kernels: 57.5 us -> 55.5 us
    all_to_all x0 -> x1, blocking collectives: none -> 17.3 us  [on_device(): got = lax.all_to_all(message, ('dp', 'section'), 0, 0, tiled=True)]
    all_to_all x1 -> x0, starting transfers between devices: 9.56 us -> none  [on_device(): got = lax.all_to_all(message, ('dp', 'section'), 0, 0, tiled=True)]
    all_to_all x1 -> x0, waiting for transfers between devices: 8.56 us -> none  [on_device(): got = lax.all_to_all(message, ('dp', 'section'), 0, 0, tiled=True)]
    pallas_call x2, Pallas kernels: 4.65 us -> 3.29 us  [the longest x1 1.94 us: on_device(): pl.pallas_call(late_kernel, out_shape=shapes + (pltpu.VMEM((32, kd), BF16...]
  transfers between devices with their start and end apart: 16 -> 15, of which waited for: 4 -> 3; matrix products, arithmetic and copies ran while one was open for 0% -> 0% of each run, Pallas kernels for 42% -> 42%
where the time goes in v2:
time: 127 us
  Pallas kernels  55.5 us (44%)
  starting transfers between devices  44.2 us (35%)
  blocking collectives  17.3 us (14%)
  waiting for transfers between devices  7.24 us (6%)
  between operations  1.6 us (1%)
    pallas_call x11, Pallas kernels, run_tick(): pl.pallas_call(functools.partial(tick_kernel, toks=toks), out_shape=(pltp...  45 us
    ppermute x11, starting transfers between devices, one(): coming = lax.ppermute(sent, 'section', chain)  37.7 us
    all_to_all x1, blocking collectives, on_device(): got = lax.all_to_all(message, ('dp', 'section'), 0, 0, tiled=True)  17.3 us
    pallas_call x1, Pallas kernels, first_tick(): pl.pallas_call(functools.partial(first_kernel, images=images, toks=toks),...  6.61 us
    ppermute x3, starting transfers between devices, exchange(): return lax.ppermute(rows, ('dp', 'section'), pairs)  5.79 us
    ppermute x11, waiting for transfers between devices, one(): coming = lax.ppermute(sent, 'section', chain)  4.86 us
  transfers between devices with their start and end apart: 15, of which 3 were waited for; matrix products, arithmetic and copies ran while one was open for 0% of the time, Pallas kernels for 42%

profile of v2, /device:TPU:1, one launch (start us, length us, event | category | flops | bytes accessed | tf_op | source)
XLA Modules:
  0.0 126.9 jit_solution(11094199038792637879)
XLA Ops:
  0.6 2.1 %collective-permute-start.2 = (bf16[8,256]{1,0:T(8,128)(2,1)}, bf16[8,256]{1,0:T(8,128)(2,1)S(1)}, u32[]{:S(2)}, u32[]{:S(2)}) collective-permute-start(bf16[8,256]{1,0:T(8,128)(2,1)} %left.1), channel_id=1, source_target_pairs={{0,4},{1,5},{2,6},{3,7},{4,0},{5,1},{6,2},{7,3},{8,12},{9,13},{10,... | collective-permute-start | bytes 12296 | tf_op jit(solution)/shard_map/ppermute | solution.py:552
  2.8 6.6 %first.1 = (bf16[200,1024]{1,0:T(8,128)(2,1)S(1)}, bf16[8,200,1024]{2,1,0:T(8,128)(2,1)S(1)}, bf16[1024,3072]{1,0:T(8,128)(2,1)S(1)}, bf16[1024,1024]{1,0:T(8,12...) custom-call(bf16[1576,1024]{1,0:T(8,128)(2,1)} %bitcast.17, ...), custom_call_target="tpu_custom_call" | custom-call | tf_op jit(solution)/shard_map/first/pallas_call | solution.py:229
  9.4 4.0 %collective-permute-start.5 = (bf16[200,1024]{1,0:T(8,128)(2,1)S(1)}, bf16[200,1024]{1,0:T(8,128)(2,1)S(1)}, u32[]{:S(2)}, u32[]{:S(2)}) collective-permute-start(bf16[200,1024]{1,0:T(8,128)(2,1)S(1)} %get-tuple-element.122), channel_id=1, source_target_pairs={{0,1},{1,2},{2,3},{4,5},{5,6},{6,7},{8,9},{9,10},{10,11},{12,13},{... | collective-permute-start | bytes 1228808 | tf_op jit(solution)/shard_map/ppermute | solution.py:564
  15.9 2.3 %collective-permute-start.4 = (bf16[32,256]{1,0:T(8,128)(2,1)S(1)}, bf16[32,256]{1,0:T(8,128)(2,1)S(1)}, u32[]{:S(2)}, u32[]{:S(2)}) collective-permute-start(bf16[32,256]{1,0:T(8,128)(2,1)S(1)} %merge.4.left), channel_id=1, source_target_pairs={{0,16},{1,17},{2,18},{3,19},{4,20},{5,21},{6,22},{7,23},{8,24},{9,... | collective-permute-start | bytes 49160 | tf_op jit(solution)/shard_map/ppermute | solution.py:552
  19.5 84.1 %while.13 = (s32[1]{0:T(128)S(4)}, bf16[200,1024]{1,0:T(8,128)(2,1)S(1)}, bf16[200,1024]{1,0:T(8,128)(2,1)S(1)}, f32[8,1024]{1,0:T(8,128)S(1)}, bf16[8,200,1024]...) while((s32[1]{0:T(128)S(4)}, ...), condition=%region_1.0_spmd, body=%region_0.0_spmd | while | flops 1 | bytes 3276977 | solution.py:593
  19.7 4.2 %collective-permute-start = (bf16[200,1024]{1,0:T(8,128)(2,1)S(1)}, bf16[200,1024]{1,0:T(8,128)(2,1)S(1)}, u32[]{:S(2)}, u32[]{:S(2)}) collective-permute-start(bf16[200,1024]{1,0:T(8,128)(2,1)S(1)} %get-tuple-element.186), channel_id=1, source_target_pairs={{0,1},{1,2},{2,3},{4,5},{5,6},{6,7},{8,9},{9,10},{10,11},{12,13},{... | collective-permute-start | bytes 1228808 | tf_op jit(solution)/shard_map/while/body/ppermute | solution.py:564
  23.9 5.6 %block.3 = (bf16[200,1024]{1,0:T(8,128)(2,1)S(1)}, f32[8,1024]{1,0:T(8,128)S(1)}, s32[1]{0:T(128)S(4)}) custom-call(s32[1]{0:T(128)S(4)} %get-tuple-element.184.tick, bf16[8,200,1024]{2,1,0:T(8,128)(2,1)S(1)} %get-tuple-element.199.turned, bf16[200,1024]{1,0:T(8,128)(2,1)S(1)} %get-tuple-element.185.came, ...), custom_call_target="tpu_custom_call", output_to_operand_aliasing={{1}: (3, {})} | custom-call | tf_op jit(solution)/shard_map/while/body/block/pallas_call | solution.py:306
  29.6 1.9 %collective-permute-start.1 = (bf16[200,1024]{1,0:T(8,128)(2,1)S(1)}, bf16[200,1024]{1,0:T(8,128)(2,1)S(1)}, u32[]{:S(2)}, u32[]{:S(2)}) collective-permute-start(bf16[200,1024]{1,0:T(8,128)(2,1)S(1)} %get-tuple-element.58), channel_id=1, source_target_pairs={{0,1},{1,2},{2,3},{4,5},{5,6},{6,7},{8,9},{9,10},{10,11},{12,13},{... | collective-permute-start | bytes 1228808 | tf_op jit(solution)/shard_map/while/body/ppermute | solution.py:564
  31.5 5.6 %block.4 = (bf16[200,1024]{1,0:T(8,128)(2,1)S(1)}, f32[8,1024]{1,0:T(8,128)S(1)}, s32[1]{0:T(128)S(4)}) custom-call(s32[1]{0:T(128)S(4)} %get-tuple-element.54.tick, bf16[8,200,1024]{2,1,0:T(8,128)(2,1)S(1)} %get-tuple-element.199.turned, bf16[200,1024]{1,0:T(8,128)(2,1)S(1)} %collective-permute-done.came, ...), custom_call_target="tpu_custom_call", output_to_operand_aliasing={{1}: (3, {})} | custom-call | tf_op jit(solution)/shard_map/while/body/block/pallas_call | solution.py:306
  37.1 3.6 %collective-permute-start = (bf16[200,1024]{1,0:T(8,128)(2,1)S(1)}, bf16[200,1024]{1,0:T(8,128)(2,1)S(1)}, u32[]{:S(2)}, u32[]{:S(2)}) collective-permute-start(bf16[200,1024]{1,0:T(8,128)(2,1)S(1)} %get-tuple-element.186), channel_id=1, source_target_pairs={{0,1},{1,2},{2,3},{4,5},{5,6},{6,7},{8,9},{9,10},{10,11},{12,13},{... | collective-permute-start | bytes 1228808 | tf_op jit(solution)/shard_map/while/body/ppermute | solution.py:564
  40.7 5.6 %block.3 = (bf16[200,1024]{1,0:T(8,128)(2,1)S(1)}, f32[8,1024]{1,0:T(8,128)S(1)}, s32[1]{0:T(128)S(4)}) custom-call(s32[1]{0:T(128)S(4)} %get-tuple-element.184.tick, bf16[8,200,1024]{2,1,0:T(8,128)(2,1)S(1)} %get-tuple-element.199.turned, bf16[200,1024]{1,0:T(8,128)(2,1)S(1)} %get-tuple-element.185.came, ...), custom_call_target="tpu_custom_call", output_to_operand_aliasing={{1}: (3, {})} | custom-call | tf_op jit(solution)/shard_map/while/body/block/pallas_call | solution.py:306
  48.3 5.6 %block.4 = (bf16[200,1024]{1,0:T(8,128)(2,1)S(1)}, f32[8,1024]{1,0:T(8,128)S(1)}, s32[1]{0:T(128)S(4)}) custom-call(s32[1]{0:T(128)S(4)} %get-tuple-element.54.tick, bf16[8,200,1024]{2,1,0:T(8,128)(2,1)S(1)} %get-tuple-element.199.turned, bf16[200,1024]{1,0:T(8,128)(2,1)S(1)} %collective-permute-done.came, ...), custom_call_target="tpu_custom_call", output_to_operand_aliasing={{1}: (3, {})} | custom-call | tf_op jit(solution)/shard_map/while/body/block/pallas_call | solution.py:306
  54.0 3.6 %collective-permute-start = (bf16[200,1024]{1,0:T(8,128)(2,1)S(1)}, bf16[200,1024]{1,0:T(8,128)(2,1)S(1)}, u32[]{:S(2)}, u32[]{:S(2)}) collective-permute-start(bf16[200,1024]{1,0:T(8,128)(2,1)S(1)} %get-tuple-element.186), channel_id=1, source_target_pairs={{0,1},{1,2},{2,3},{4,5},{5,6},{6,7},{8,9},{9,10},{10,11},{12,13},{... | collective-permute-start | bytes 1228808 | tf_op jit(solution)/shard_map/while/body/ppermute | solution.py:564
  57.6 5.6 %block.3 = (bf16[200,1024]{1,0:T(8,128)(2,1)S(1)}, f32[8,1024]{1,0:T(8,128)S(1)}, s32[1]{0:T(128)S(4)}) custom-call(s32[1]{0:T(128)S(4)} %get-tuple-element.184.tick, bf16[8,200,1024]{2,1,0:T(8,128)(2,1)S(1)} %get-tuple-element.199.turned, bf16[200,1024]{1,0:T(8,128)(2,1)S(1)} %get-tuple-element.185.came, ...), custom_call_target="tpu_custom_call", output_to_operand_aliasing={{1}: (3, {})} | custom-call | tf_op jit(solution)/shard_map/while/body/block/pallas_call | solution.py:306
  65.1 5.6 %block.4 = (bf16[200,1024]{1,0:T(8,128)(2,1)S(1)}, f32[8,1024]{1,0:T(8,128)S(1)}, s32[1]{0:T(128)S(4)}) custom-call(s32[1]{0:T(128)S(4)} %get-tuple-element.54.tick, bf16[8,200,1024]{2,1,0:T(8,128)(2,1)S(1)} %get-tuple-element.199.turned, bf16[200,1024]{1,0:T(8,128)(2,1)S(1)} %collective-permute-done.came, ...), custom_call_target="tpu_custom_call", output_to_operand_aliasing={{1}: (3, {})} | custom-call | tf_op jit(solution)/shard_map/while/body/block/pallas_call | solution.py:306
  70.8 3.6 %collective-permute-start = (bf16[200,1024]{1,0:T(8,128)(2,1)S(1)}, bf16[200,1024]{1,0:T(8,128)(2,1)S(1)}, u32[]{:S(2)}, u32[]{:S(2)}) collective-permute-start(bf16[200,1024]{1,0:T(8,128)(2,1)S(1)} %get-tuple-element.186), channel_id=1, source_target_pairs={{0,1},{1,2},{2,3},{4,5},{5,6},{6,7},{8,9},{9,10},{10,11},{12,13},{... | collective-permute-start | bytes 1228808 | tf_op jit(solution)/shard_map/while/body/ppermute | solution.py:564
  74.4 5.6 %block.3 = (bf16[200,1024]{1,0:T(8,128)(2,1)S(1)}, f32[8,1024]{1,0:T(8,128)S(1)}, s32[1]{0:T(128)S(4)}) custom-call(s32[1]{0:T(128)S(4)} %get-tuple-element.184.tick, bf16[8,200,1024]{2,1,0:T(8,128)(2,1)S(1)} %get-tuple-element.199.turned, bf16[200,1024]{1,0:T(8,128)(2,1)S(1)} %get-tuple-element.185.came, ...), custom_call_target="tpu_custom_call", output_to_operand_aliasing={{1}: (3, {})} | custom-call | tf_op jit(solution)/shard_map/while/body/block/pallas_call | solution.py:306
  80.0 1.9 %collective-permute-start.1 = (bf16[200,1024]{1,0:T(8,128)(2,1)S(1)}, bf16[200,1024]{1,0:T(8,128)(2,1)S(1)}, u32[]{:S(2)}, u32[]{:S(2)}) collective-permute-start(bf16[200,1024]{1,0:T(8,128)(2,1)S(1)} %get-tuple-element.58), channel_id=1, source_target_pairs={{0,1},{1,2},{2,3},{4,5},{5,6},{6,7},{8,9},{9,10},{10,11},{12,13},{... | collective-permute-start | bytes 1228808 | tf_op jit(solution)/shard_map/while/body/ppermute | solution.py:564
  82.0 5.6 %block.4 = (bf16[200,1024]{1,0:T(8,128)(2,1)S(1)}, f32[8,1024]{1,0:T(8,128)S(1)}, s32[1]{0:T(128)S(4)}) custom-call(s32[1]{0:T(128)S(4)} %get-tuple-element.54.tick, bf16[8,200,1024]{2,1,0:T(8,128)(2,1)S(1)} %get-tuple-element.199.turned, bf16[200,1024]{1,0:T(8,128)(2,1)S(1)} %collective-permute-done.came, ...), custom_call_target="tpu_custom_call", output_to_operand_aliasing={{1}: (3, {})} | custom-call | tf_op jit(solution)/shard_map/while/body/block/pallas_call | solution.py:306
  87.6 3.6 %collective-permute-start = (bf16[200,1024]{1,0:T(8,128)(2,1)S(1)}, bf16[200,1024]{1,0:T(8,128)(2,1)S(1)}, u32[]{:S(2)}, u32[]{:S(2)}) collective-permute-start(bf16[200,1024]{1,0:T(8,128)(2,1)S(1)} %get-tuple-element.186), channel_id=1, source_target_pairs={{0,1},{1,2},{2,3},{4,5},{5,6},{6,7},{8,9},{9,10},{10,11},{12,13},{... | collective-permute-start | bytes 1228808 | tf_op jit(solution)/shard_map/while/body/ppermute | solution.py:564
  91.2 7.5 %collective-permute-start.1 = (bf16[200,1024]{1,0:T(8,128)(2,1)S(1)}, bf16[200,1024]{1,0:T(8,128)(2,1)S(1)}, u32[]{:S(2)}, u32[]{:S(2)}) collective-permute-start(bf16[200,1024]{1,0:T(8,128)(2,1)S(1)} %get-tuple-element.58), channel_id=1, source_target_pairs={{0,1},{1,2},{2,3},{4,5},{5,6},{6,7},{8,9},{9,10},{10,11},{12,13},{... | collective-permute-start | bytes 1228808 | tf_op jit(solution)/shard_map/while/body/ppermute | solution.py:564
  98.8 4.8 %collective-permute-done.1 = bf16[200,1024]{1,0:T(8,128)(2,1)S(1)} collective-permute-done((bf16[200,1024]{1,0:T(8,128)(2,1)S(1)}, bf16[200,1024]{1,0:T(8,128)(2,1)S(1)}, u32[]{:S(2)}, u32[]{:S(2)}) %collective-permute-start.1) | collective-permute-done | bytes 409632 | tf_op jit(solution)/shard_map/while/body/ppermute | solution.py:564
  105.6 1.9 %late.1 = (f32[1,128]{1,0:T(1,128)S(1)}, bf16[1024,256]{1,0:T(8,128)(2,1)}, bf16[32,256]{1,0:T(8,128)(2,1)S(1)}, s32[1,64]{1,0:T(1,128)S(1)}, s32[1]{0:T(128)S(4)}) custom-call(bf16[64,256]{1,0:T(8,128)(2,1)S(1)} %get-tuple-element.117.query, bf16[1024,256]{1,0:T(8,128)(2,1)} %queue_hbm.3, s32[1]{0:T(128)S(6)} %copy.41.pointer, ...), custom_call_target="tpu_custom_call", output_to_operand_aliasing={{1}: (5, {})} | custom-call | tf_op jit(solution)/shard_map/late/pallas_call | solution.py:600
  108.1 17.3 %all_to_all.5.got = bf16[32,24,128]{2,1,0:T(8,128)(2,1)S(1)} all-to-all(bf16[32,24,128]{2,1,0:T(8,128)(2,1)S(1)} %head.2), channel_id=1, replica_groups=mesh['dp'=8,'section'=4] {'dp','section'}, dimensions={0} | all-to-all | bytes 393216 | tf_op jit(solution)/shard_map/all_to_all | solution.py:630
  (40 shorter events, 10.8 us)
Async XLA Ops:
  0.6 8.7 %collective-permute-start.2 = (bf16[8,256]{1,0:T(8,128)(2,1)}, bf16[8,256]{1,0:T(8,128)(2,1)S(1)}, u32[]{:S(2)}, u32[]{:S(2)}) collective-permute-start(bf16[8,256]{1,0:T(8,128)(2,1)} %left.1), channel_id=1, source_target_pairs={{0,4},{1,5},{2,6},{3,7},{4,0},{5,1},{6,2},{7,3},{8,12},{9,13},{10,... | collective-permute-start | bytes 12296 | tf_op jit(solution)/shard_map/ppermute | solution.py:552
  2.8 10.6 %copy-start.2 = (bf16[8,256]{1,0:T(8,128)(2,1)S(1)}, bf16[8,256]{1,0:T(8,128)(2,1)}, u32[]{:S(2)}) copy-start(bf16[8,256]{1,0:T(8,128)(2,1)} %left.1) | copy-start | bytes 12292
  2.8 12.0 %copy-start.4 = (f32[1,1024]{1,0:T(1,128)S(1)}, f32[1,1024]{1,0:T(1,128)}, u32[]{:S(2)}) copy-start(f32[1,1024]{1,0:T(1,128)} %g1.7) | copy-start | bytes 12292
  2.8 12.0 %copy-start.5 = (f32[1,1024]{1,0:T(1,128)S(1)}, f32[1,1024]{1,0:T(1,128)}, u32[]{:S(2)}) copy-start(f32[1,1024]{1,0:T(1,128)} %g2.7) | copy-start | bytes 12292
  9.4 10.1 %collective-permute-start.5 = (bf16[200,1024]{1,0:T(8,128)(2,1)S(1)}, bf16[200,1024]{1,0:T(8,128)(2,1)S(1)}, u32[]{:S(2)}, u32[]{:S(2)}) collective-permute-start(bf16[200,1024]{1,0:T(8,128)(2,1)S(1)} %get-tuple-element.122), channel_id=1, source_target_pairs={{0,1},{1,2},{2,3},{4,5},{5,6},{6,7},{8,9},{9,10},{10,11},{12,13},{... | collective-permute-start | bytes 1228808 | tf_op jit(solution)/shard_map/ppermute | solution.py:564
  13.4 2.6 %collective-permute-start.3 = (bf16[16,256]{1,0:T(8,128)(2,1)S(1)}, bf16[16,256]{1,0:T(8,128)(2,1)S(1)}, u32[]{:S(2)}, u32[]{:S(2)}) collective-permute-start(bf16[16,256]{1,0:T(8,128)(2,1)S(1)} %merge.3.left), channel_id=1, source_target_pairs={{0,8},{1,9},{2,10},{3,11},{4,12},{5,13},{6,14},{7,15},{8,0},{9,1},... | collective-permute-start | bytes 24584 | tf_op jit(solution)/shard_map/ppermute | solution.py:552
  15.9 3.5 %collective-permute-start.4 = (bf16[32,256]{1,0:T(8,128)(2,1)S(1)}, bf16[32,256]{1,0:T(8,128)(2,1)S(1)}, u32[]{:S(2)}, u32[]{:S(2)}) collective-permute-start(bf16[32,256]{1,0:T(8,128)(2,1)S(1)} %merge.4.left), channel_id=1, source_target_pairs={{0,16},{1,17},{2,18},{3,19},{4,20},{5,21},{6,22},{7,23},{8,24},{9,... | collective-permute-start | bytes 49160 | tf_op jit(solution)/shard_map/ppermute | solution.py:552
  19.7 11.8 %collective-permute-start = (bf16[200,1024]{1,0:T(8,128)(2,1)S(1)}, bf16[200,1024]{1,0:T(8,128)(2,1)S(1)}, u32[]{:S(2)}, u32[]{:S(2)}) collective-permute-start(bf16[200,1024]{1,0:T(8,128)(2,1)S(1)} %get-tuple-element.186), channel_id=1, source_target_pairs={{0,1},{1,2},{2,3},{4,5},{5,6},{6,7},{8,9},{9,10},{10,11},{12,13},{... | collective-permute-start | bytes 1228808 | tf_op jit(solution)/shard_map/while/body/ppermute | solution.py:564
  29.6 7.6 %collective-permute-start.1 = (bf16[200,1024]{1,0:T(8,128)(2,1)S(1)}, bf16[200,1024]{1,0:T(8,128)(2,1)S(1)}, u32[]{:S(2)}, u32[]{:S(2)}) collective-permute-start(bf16[200,1024]{1,0:T(8,128)(2,1)S(1)} %get-tuple-element.58), channel_id=1, source_target_pairs={{0,1},{1,2},{2,3},{4,5},{5,6},{6,7},{8,9},{9,10},{10,11},{12,13},{... | collective-permute-start | bytes 1228808 | tf_op jit(solution)/shard_map/while/body/ppermute | solution.py:564
  37.1 11.2 %collective-permute-start = (bf16[200,1024]{1,0:T(8,128)(2,1)S(1)}, bf16[200,1024]{1,0:T(8,128)(2,1)S(1)}, u32[]{:S(2)}, u32[]{:S(2)}) collective-permute-start(bf16[200,1024]{1,0:T(8,128)(2,1)S(1)} %get-tuple-element.186), channel_id=1, source_target_pairs={{0,1},{1,2},{2,3},{4,5},{5,6},{6,7},{8,9},{9,10},{10,11},{12,13},{... | collective-permute-start | bytes 1228808 | tf_op jit(solution)/shard_map/while/body/ppermute | solution.py:564
  46.4 7.6 %collective-permute-start.1 = (bf16[200,1024]{1,0:T(8,128)(2,1)S(1)}, bf16[200,1024]{1,0:T(8,128)(2,1)S(1)}, u32[]{:S(2)}, u32[]{:S(2)}) collective-permute-start(bf16[200,1024]{1,0:T(8,128)(2,1)S(1)} %get-tuple-element.58), channel_id=1, source_target_pairs={{0,1},{1,2},{2,3},{4,5},{5,6},{6,7},{8,9},{9,10},{10,11},{12,13},{... | collective-permute-start | bytes 1228808 | tf_op jit(solution)/shard_map/while/body/ppermute | solution.py:564
  54.0 11.2 %collective-permute-start = (bf16[200,1024]{1,0:T(8,128)(2,1)S(1)}, bf16[200,1024]{1,0:T(8,128)(2,1)S(1)}, u32[]{:S(2)}, u32[]{:S(2)}) collective-permute-start(bf16[200,1024]{1,0:T(8,128)(2,1)S(1)} %get-tuple-element.186), channel_id=1, source_target_pairs={{0,1},{1,2},{2,3},{4,5},{5,6},{6,7},{8,9},{9,10},{10,11},{12,13},{... | collective-permute-start | bytes 1228808 | tf_op jit(solution)/shard_map/while/body/ppermute | solution.py:564
  63.2 7.6 %collective-permute-start.1 = (bf16[200,1024]{1,0:T(8,128)(2,1)S(1)}, bf16[200,1024]{1,0:T(8,128)(2,1)S(1)}, u32[]{:S(2)}, u32[]{:S(2)}) collective-permute-start(bf16[200,1024]{1,0:T(8,128)(2,1)S(1)} %get-tuple-element.58), channel_id=1, source_target_pairs={{0,1},{1,2},{2,3},{4,5},{5,6},{6,7},{8,9},{9,10},{10,11},{12,13},{... | collective-permute-start | bytes 1228808 | tf_op jit(solution)/shard_map/while/body/ppermute | solution.py:564
  70.8 11.2 %collective-permute-start = (bf16[200,1024]{1,0:T(8,128)(2,1)S(1)}, bf16[200,1024]{1,0:T(8,128)(2,1)S(1)}, u32[]{:S(2)}, u32[]{:S(2)}) collective-permute-start(bf16[200,1024]{1,0:T(8,128)(2,1)S(1)} %get-tuple-element.186), channel_id=1, source_target_pairs={{0,1},{1,2},{2,3},{4,5},{5,6},{6,7},{8,9},{9,10},{10,11},{12,13},{... | collective-permute-start | bytes 1228808 | tf_op jit(solution)/shard_map/while/body/ppermute | solution.py:564
  80.0 7.6 %collective-permute-start.1 = (bf16[200,1024]{1,0:T(8,128)(2,1)S(1)}, bf16[200,1024]{1,0:T(8,128)(2,1)S(1)}, u32[]{:S(2)}, u32[]{:S(2)}) collective-permute-start(bf16[200,1024]{1,0:T(8,128)(2,1)S(1)} %get-tuple-element.58), channel_id=1, source_target_pairs={{0,1},{1,2},{2,3},{4,5},{5,6},{6,7},{8,9},{9,10},{10,11},{12,13},{... | collective-permute-start | bytes 1228808 | tf_op jit(solution)/shard_map/while/body/ppermute | solution.py:564
  87.6 11.1 %collective-permute-start = (bf16[200,1024]{1,0:T(8,128)(2,1)S(1)}, bf16[200,1024]{1,0:T(8,128)(2,1)S(1)}, u32[]{:S(2)}, u32[]{:S(2)}) collective-permute-start(bf16[200,1024]{1,0:T(8,128)(2,1)S(1)} %get-tuple-element.186), channel_id=1, source_target_pairs={{0,1},{1,2},{2,3},{4,5},{5,6},{6,7},{8,9},{9,10},{10,11},{12,13},{... | collective-permute-start | bytes 1228808 | tf_op jit(solution)/shard_map/while/body/ppermute | solution.py:564
  91.2 12.4 %collective-permute-start.1 = (bf16[200,1024]{1,0:T(8,128)(2,1)S(1)}, bf16[200,1024]{1,0:T(8,128)(2,1)S(1)}, u32[]{:S(2)}, u32[]{:S(2)}) collective-permute-start(bf16[200,1024]{1,0:T(8,128)(2,1)S(1)} %get-tuple-element.58), channel_id=1, source_target_pairs={{0,1},{1,2},{2,3},{4,5},{5,6},{6,7},{8,9},{9,10},{10,11},{12,13},{... | collective-permute-start | bytes 1228808 | tf_op jit(solution)/shard_map/while/body/ppermute | solution.py:564
  103.6 3.9 %collective-permute-start.6 = (bf16[200,1024]{1,0:T(8,128)(2,1)S(1)}, bf16[200,1024]{1,0:T(8,128)(2,1)S(1)}, u32[]{:S(2)}, u32[]{:S(2)}) collective-permute-start(bf16[200,1024]{1,0:T(8,128)(2,1)S(1)} %get-tuple-element.130), channel_id=1, source_target_pairs={{2,3},{6,7},{10,11},{14,15},{18,19},{22,23},{26,27},{30,31}} | collective-permute-start | bytes 1228808 | tf_op jit(solution)/shard_map/ppermute | solution.py:595
  105.0 0.7 copy-start.3
  105.0 2.6 %copy-start = (bf16[1024,256]{1,0:T(8,128)(2,1)S(1)}, bf16[1024,256]{1,0:T(8,128)(2,1)}, u32[]{:S(2)}) copy-start(bf16[1024,256]{1,0:T(8,128)(2,1)} %head.3) | copy-start | bytes 1572868
  105.0 2.6 %copy-start.1 = (f32[1024]{0:T(1024)S(1)}, f32[1024]{0:T(1024)}, u32[]{:S(2)}) copy-start(f32[1024]{0:T(1024)} %param.22) | copy-start | bytes 12292

commit v3 on v2

--- a/solution.py
+++ b/solution.py
@@ -322,22 +322,24 @@
     )(tick, hold(turned), hold(came), hold(marks), *held_weights(weights))
 
 
-def merge_kernel(left, right, out_ref):
-    half = left.shape[0]
-    out_ref[0:half, :] = left[...]
-    out_ref[half : 2 * half, :] = right[...]
-
-
-def merge(left, right):
+def merge_kernel(*refs):
+    out_ref = refs[-1]
+    size = refs[0].shape[0]
+    for k, piece in enumerate(refs[:-1]):
+        out_ref[k * size : (k + 1) * size, :] = piece[...]
+
+
+def merge(*pieces):
+    size, width = pieces[0].shape
     whole = pl.BlockSpec(memory_space=pltpu.VMEM)
     return pl.pallas_call(
         merge_kernel,
-        out_shape=pltpu.VMEM((2 * left.shape[0], left.shape[1]), left.dtype),
-        in_specs=[whole, whole],
+        out_shape=pltpu.VMEM((len(pieces) * size, width), pieces[0].dtype),
+        in_specs=[whole] * len(pieces),
         out_specs=whole,
         compiler_params=pltpu.CompilerParams(vmem_limit_bytes=2**20),
         name="merge",
-    )(left, right)
+    )(*pieces)
 
 
 def class_kernel(came, marks_in, g1, wqkv, wout, g2, wfc1, wfc2, marks, norm, qkv, row, *, toks):
@@ -545,14 +547,12 @@
     ]
     chain = [(k, k + 1) for k in range(sections - 1)]
     ticks = images + HOP * (sections - 1)
-    hops = [1 << k for k in range(max(groups - 1, 1).bit_length()) if 1 << k < groups]
-
     def exchange(rows, hop):
         pairs = [(k * sections + j, (k ^ hop) * sections + j) for k in range(groups) for j in range(sections)]
         return lax.ppermute(rows, ("dp", "section"), pairs)
 
     swapped = online_embeddings
-    other = exchange(swapped, hops[0])
+    other = exchange(swapped, 1)
     sent, turned, *held, marks, blank, tick = first_tick(
         patches, (ln1_gain, w_qkv[0], w_out[0], ln2_gain, w_fc1[0], w_fc2[0]), rows
     )
@@ -572,14 +572,15 @@
 
     other, sent = lax.optimization_barrier((other, sent))
     swapped = merge(swapped, other)
-    if len(hops) > 1:
-        other = exchange(swapped, hops[1])
+    near = [hop for hop in (2, 4, 6) if hop < groups]
+    others = [exchange(swapped, hop) for hop in near]
     tick, came, sent, marks = one(tick, blank, sent, marks)
-    for hop in hops[1:]:
-        if hop != hops[1]:
-            other = exchange(swapped, hop)
-        other, sent = lax.optimization_barrier((other, sent))
-        swapped = merge(swapped, other)
+    *others, sent = lax.optimization_barrier((*others, sent))
+    swapped = merge(swapped, *others)
+    hop = 8
+    while hop < groups:
+        swapped = merge(swapped, exchange(swapped, hop))
+        hop *= 2
     lse, queue_copy, query = pl.pallas_call(
         functools.partial(early_kernel, images=images),
         out_shape=shapes + (pltpu.VMEM((count, kd), BF16),),

time: 127 us -> 126 us (level)
  blocking collectives: 17.3 us -> 14.6 us
  waiting for transfers between devices: 7.24 us -> 9.11 us
    all_to_all x1, blocking collectives: 17.3 us -> 14.6 us  [on_device(): got = lax.all_to_all(message, ('dp', 'section'), 0, 0, tiled=True)]
    ppermute x3 -> x4, waiting for transfers between devices: 2.38 us -> 4.25 us  [exchange(): return lax.ppermute(rows, ('dp', 'section'), pairs)]
    ppermute x3 -> x4, starting transfers between devices: 5.79 us -> 5.8 us  [exchange(): return lax.ppermute(rows, ('dp', 'section'), pairs)]
  transfers between devices with their start and end apart: 15 -> 16, of which waited for: 3 -> 3; matrix products, arithmetic and copies ran while one was open for 0% -> 0% of each run, Pallas kernels for 42% -> 43%
where the time goes in v3:
time: 126 us
  Pallas kernels  55.5 us (44%)
  starting transfers between devices  43.6 us (35%)
  blocking collectives  14.6 us (12%)
  waiting for transfers between devices  9.11 us (7%)
  between operations  1.62 us (1%)
    pallas_call x11, Pallas kernels, run_tick(): pl.pallas_call(functools.partial(tick_kernel, toks=toks), out_shape=(pltp...  45.1 us
    ppermute x11, starting transfers between devices, one(): coming = lax.ppermute(sent, 'section', chain)  37.2 us
    all_to_all x1, blocking collectives, on_device(): got = lax.all_to_all(message, ('dp', 'section'), 0, 0, tiled=True)  14.6 us
    pallas_call x1, Pallas kernels, first_tick(): pl.pallas_call(functools.partial(first_kernel, images=images, toks=toks),...  6.61 us
    ppermute x4, starting transfers between devices, exchange(): return lax.ppermute(rows, ('dp', 'section'), pairs)  5.8 us
    ppermute x11, waiting for transfers between devices, one(): coming = lax.ppermute(sent, 'section', chain)  4.86 us
    ppermute x4, waiting for transfers between devices, exchange(): return lax.ppermute(rows, ('dp', 'section'), pairs)  4.25 us
  transfers between devices with their start and end apart: 16, of which 3 were waited for; matrix products, arithmetic and copies ran while one was open for 0% of the time, Pallas kernels for 43%

profile of v3, /device:TPU:1, one launch (start us, length us, event | category | flops | bytes accessed | tf_op | source)
XLA Modules:
  0.0 125.5 jit_solution(3302225130493192544)
XLA Ops:
  0.6 2.1 %collective-permute-start.2 = (bf16[8,256]{1,0:T(8,128)(2,1)}, bf16[8,256]{1,0:T(8,128)(2,1)S(1)}, u32[]{:S(2)}, u32[]{:S(2)}) collective-permute-start(bf16[8,256]{1,0:T(8,128)(2,1)} %refs_0_.1), channel_id=1, source_target_pairs={{0,4},{1,5},{2,6},{3,7},{4,0},{5,1},{6,2},{7,3},{8,12},{9,13},{10,... | collective-permute-start | bytes 12296 | tf_op jit(solution)/shard_map/ppermute | solution.py:552
  2.8 6.6 %first.1 = (bf16[200,1024]{1,0:T(8,128)(2,1)S(1)}, bf16[8,200,1024]{2,1,0:T(8,128)(2,1)S(1)}, bf16[1024,3072]{1,0:T(8,128)(2,1)S(1)}, bf16[1024,1024]{1,0:T(8,12...) custom-call(bf16[1576,1024]{1,0:T(8,128)(2,1)} %bitcast.17, ...), custom_call_target="tpu_custom_call" | custom-call | tf_op jit(solution)/shard_map/first/pallas_call | solution.py:229
  9.4 4.0 %collective-permute-start.6 = (bf16[200,1024]{1,0:T(8,128)(2,1)S(1)}, bf16[200,1024]{1,0:T(8,128)(2,1)S(1)}, u32[]{:S(2)}, u32[]{:S(2)}) collective-permute-start(bf16[200,1024]{1,0:T(8,128)(2,1)S(1)} %get-tuple-element.122), channel_id=1, source_target_pairs={{0,1},{1,2},{2,3},{4,5},{5,6},{6,7},{8,9},{9,10},{10,11},{12,13},{... | collective-permute-start | bytes 1228808 | tf_op jit(solution)/shard_map/ppermute | solution.py:564
  14.7 2.3 %collective-permute-start.4 = (bf16[16,256]{1,0:T(8,128)(2,1)S(1)}, bf16[16,256]{1,0:T(8,128)(2,1)S(1)}, u32[]{:S(2)}, u32[]{:S(2)}) collective-permute-start(bf16[16,256]{1,0:T(8,128)(2,1)S(1)} %merge.2.refs_0_), channel_id=1, source_target_pairs={{0,16},{1,17},{2,18},{3,19},{4,20},{5,21},{6,22},{7,23},{8,24},{9,... | collective-permute-start | bytes 24584 | tf_op jit(solution)/shard_map/ppermute | solution.py:552
  18.1 3.2 %collective-permute-done.5.refs_3_ = bf16[16,256]{1,0:T(8,128)(2,1)S(1)} collective-permute-done((bf16[16,256]{1,0:T(8,128)(2,1)S(1)}, bf16[16,256]{1,0:T(8,128)(2,1)S(1)}, u32[]{:S(2)}, u32[]{:S(2)}) %collective-permute-start.5) | collective-permute-done | bytes 8224 | tf_op jit(solution)/shard_map/ppermute | solution.py:552
  21.4 83.6 %while.13 = (s32[1]{0:T(128)S(4)}, bf16[200,1024]{1,0:T(8,128)(2,1)S(1)}, bf16[200,1024]{1,0:T(8,128)(2,1)S(1)}, f32[8,1024]{1,0:T(8,128)S(1)}, bf16[8,200,1024]...) while((s32[1]{0:T(128)S(4)}, ...), condition=%region_1.0_spmd, body=%region_0.0_spmd | while | flops 1 | bytes 3276977 | solution.py:594
  21.6 3.6 %collective-permute-start = (bf16[200,1024]{1,0:T(8,128)(2,1)S(1)}, bf16[200,1024]{1,0:T(8,128)(2,1)S(1)}, u32[]{:S(2)}, u32[]{:S(2)}) collective-permute-start(bf16[200,1024]{1,0:T(8,128)(2,1)S(1)} %get-tuple-element.186), channel_id=1, source_target_pairs={{0,1},{1,2},{2,3},{4,5},{5,6},{6,7},{8,9},{9,10},{10,11},{12,13},{... | collective-permute-start | bytes 1228808 | tf_op jit(solution)/shard_map/while/body/ppermute | solution.py:564
  25.3 5.6 %block.3 = (bf16[200,1024]{1,0:T(8,128)(2,1)S(1)}, f32[8,1024]{1,0:T(8,128)S(1)}, s32[1]{0:T(128)S(4)}) custom-call(s32[1]{0:T(128)S(4)} %get-tuple-element.184.tick, bf16[8,200,1024]{2,1,0:T(8,128)(2,1)S(1)} %get-tuple-element.199.turned, bf16[200,1024]{1,0:T(8,128)(2,1)S(1)} %get-tuple-element.185.came, ...), custom_call_target="tpu_custom_call", output_to_operand_aliasing={{1}: (3, {})} | custom-call | tf_op jit(solution)/shard_map/while/body/block/pallas_call | solution.py:306
  32.8 5.6 %block.4 = (bf16[200,1024]{1,0:T(8,128)(2,1)S(1)}, f32[8,1024]{1,0:T(8,128)S(1)}, s32[1]{0:T(128)S(4)}) custom-call(s32[1]{0:T(128)S(4)} %get-tuple-element.54.tick, bf16[8,200,1024]{2,1,0:T(8,128)(2,1)S(1)} %get-tuple-element.199.turned, bf16[200,1024]{1,0:T(8,128)(2,1)S(1)} %collective-permute-done.came, ...), custom_call_target="tpu_custom_call", output_to_operand_aliasing={{1}: (3, {})} | custom-call | tf_op jit(solution)/shard_map/while/body/block/pallas_call | solution.py:306
  38.5 3.6 %collective-permute-start = (bf16[200,1024]{1,0:T(8,128)(2,1)S(1)}, bf16[200,1024]{1,0:T(8,128)(2,1)S(1)}, u32[]{:S(2)}, u32[]{:S(2)}) collective-permute-start(bf16[200,1024]{1,0:T(8,128)(2,1)S(1)} %get-tuple-element.186), channel_id=1, source_target_pairs={{0,1},{1,2},{2,3},{4,5},{5,6},{6,7},{8,9},{9,10},{10,11},{12,13},{... | collective-permute-start | bytes 1228808 | tf_op jit(solution)/shard_map/while/body/ppermute | solution.py:564
  42.1 5.6 %block.3 = (bf16[200,1024]{1,0:T(8,128)(2,1)S(1)}, f32[8,1024]{1,0:T(8,128)S(1)}, s32[1]{0:T(128)S(4)}) custom-call(s32[1]{0:T(128)S(4)} %get-tuple-element.184.tick, bf16[8,200,1024]{2,1,0:T(8,128)(2,1)S(1)} %get-tuple-element.199.turned, bf16[200,1024]{1,0:T(8,128)(2,1)S(1)} %get-tuple-element.185.came, ...), custom_call_target="tpu_custom_call", output_to_operand_aliasing={{1}: (3, {})} | custom-call | tf_op jit(solution)/shard_map/while/body/block/pallas_call | solution.py:306
  49.7 5.6 %block.4 = (bf16[200,1024]{1,0:T(8,128)(2,1)S(1)}, f32[8,1024]{1,0:T(8,128)S(1)}, s32[1]{0:T(128)S(4)}) custom-call(s32[1]{0:T(128)S(4)} %get-tuple-element.54.tick, bf16[8,200,1024]{2,1,0:T(8,128)(2,1)S(1)} %get-tuple-element.199.turned, bf16[200,1024]{1,0:T(8,128)(2,1)S(1)} %collective-permute-done.came, ...), custom_call_target="tpu_custom_call", output_to_operand_aliasing={{1}: (3, {})} | custom-call | tf_op jit(solution)/shard_map/while/body/block/pallas_call | solution.py:306
  55.3 3.6 %collective-permute-start = (bf16[200,1024]{1,0:T(8,128)(2,1)S(1)}, bf16[200,1024]{1,0:T(8,128)(2,1)S(1)}, u32[]{:S(2)}, u32[]{:S(2)}) collective-permute-start(bf16[200,1024]{1,0:T(8,128)(2,1)S(1)} %get-tuple-element.186), channel_id=1, source_target_pairs={{0,1},{1,2},{2,3},{4,5},{5,6},{6,7},{8,9},{9,10},{10,11},{12,13},{... | collective-permute-start | bytes 1228808 | tf_op jit(solution)/shard_map/while/body/ppermute | solution.py:564
  58.9 5.6 %block.3 = (bf16[200,1024]{1,0:T(8,128)(2,1)S(1)}, f32[8,1024]{1,0:T(8,128)S(1)}, s32[1]{0:T(128)S(4)}) custom-call(s32[1]{0:T(128)S(4)} %get-tuple-element.184.tick, bf16[8,200,1024]{2,1,0:T(8,128)(2,1)S(1)} %get-tuple-element.199.turned, bf16[200,1024]{1,0:T(8,128)(2,1)S(1)} %get-tuple-element.185.came, ...), custom_call_target="tpu_custom_call", output_to_operand_aliasing={{1}: (3, {})} | custom-call | tf_op jit(solution)/shard_map/while/body/block/pallas_call | solution.py:306
  64.5 1.9 %collective-permute-start.1 = (bf16[200,1024]{1,0:T(8,128)(2,1)S(1)}, bf16[200,1024]{1,0:T(8,128)(2,1)S(1)}, u32[]{:S(2)}, u32[]{:S(2)}) collective-permute-start(bf16[200,1024]{1,0:T(8,128)(2,1)S(1)} %get-tuple-element.58), channel_id=1, source_target_pairs={{0,1},{1,2},{2,3},{4,5},{5,6},{6,7},{8,9},{9,10},{10,11},{12,13},{... | collective-permute-start | bytes 1228808 | tf_op jit(solution)/shard_map/while/body/ppermute | solution.py:564
  66.5 5.6 %block.4 = (bf16[200,1024]{1,0:T(8,128)(2,1)S(1)}, f32[8,1024]{1,0:T(8,128)S(1)}, s32[1]{0:T(128)S(4)}) custom-call(s32[1]{0:T(128)S(4)} %get-tuple-element.54.tick, bf16[8,200,1024]{2,1,0:T(8,128)(2,1)S(1)} %get-tuple-element.199.turned, bf16[200,1024]{1,0:T(8,128)(2,1)S(1)} %collective-permute-done.came, ...), custom_call_target="tpu_custom_call", output_to_operand_aliasing={{1}: (3, {})} | custom-call | tf_op jit(solution)/shard_map/while/body/block/pallas_call | solution.py:306
  72.1 3.6 %collective-permute-start = (bf16[200,1024]{1,0:T(8,128)(2,1)S(1)}, bf16[200,1024]{1,0:T(8,128)(2,1)S(1)}, u32[]{:S(2)}, u32[]{:S(2)}) collective-permute-start(bf16[200,1024]{1,0:T(8,128)(2,1)S(1)} %get-tuple-element.186), channel_id=1, source_target_pairs={{0,1},{1,2},{2,3},{4,5},{5,6},{6,7},{8,9},{9,10},{10,11},{12,13},{... | collective-permute-start | bytes 1228808 | tf_op jit(solution)/shard_map/while/body/ppermute | solution.py:564
  75.7 5.6 %block.3 = (bf16[200,1024]{1,0:T(8,128)(2,1)S(1)}, f32[8,1024]{1,0:T(8,128)S(1)}, s32[1]{0:T(128)S(4)}) custom-call(s32[1]{0:T(128)S(4)} %get-tuple-element.184.tick, bf16[8,200,1024]{2,1,0:T(8,128)(2,1)S(1)} %get-tuple-element.199.turned, bf16[200,1024]{1,0:T(8,128)(2,1)S(1)} %get-tuple-element.185.came, ...), custom_call_target="tpu_custom_call", output_to_operand_aliasing={{1}: (3, {})} | custom-call | tf_op jit(solution)/shard_map/while/body/block/pallas_call | solution.py:306
  83.3 5.6 %block.4 = (bf16[200,1024]{1,0:T(8,128)(2,1)S(1)}, f32[8,1024]{1,0:T(8,128)S(1)}, s32[1]{0:T(128)S(4)}) custom-call(s32[1]{0:T(128)S(4)} %get-tuple-element.54.tick, bf16[8,200,1024]{2,1,0:T(8,128)(2,1)S(1)} %get-tuple-element.199.turned, bf16[200,1024]{1,0:T(8,128)(2,1)S(1)} %collective-permute-done.came, ...), custom_call_target="tpu_custom_call", output_to_operand_aliasing={{1}: (3, {})} | custom-call | tf_op jit(solution)/shard_map/while/body/block/pallas_call | solution.py:306
  89.0 3.6 %collective-permute-start = (bf16[200,1024]{1,0:T(8,128)(2,1)S(1)}, bf16[200,1024]{1,0:T(8,128)(2,1)S(1)}, u32[]{:S(2)}, u32[]{:S(2)}) collective-permute-start(bf16[200,1024]{1,0:T(8,128)(2,1)S(1)} %get-tuple-element.186), channel_id=1, source_target_pairs={{0,1},{1,2},{2,3},{4,5},{5,6},{6,7},{8,9},{9,10},{10,11},{12,13},{... | collective-permute-start | bytes 1228808 | tf_op jit(solution)/shard_map/while/body/ppermute | solution.py:564
  92.6 7.5 %collective-permute-start.1 = (bf16[200,1024]{1,0:T(8,128)(2,1)S(1)}, bf16[200,1024]{1,0:T(8,128)(2,1)S(1)}, u32[]{:S(2)}, u32[]{:S(2)}) collective-permute-start(bf16[200,1024]{1,0:T(8,128)(2,1)S(1)} %get-tuple-element.58), channel_id=1, source_target_pairs={{0,1},{1,2},{2,3},{4,5},{5,6},{6,7},{8,9},{9,10},{10,11},{12,13},{... | collective-permute-start | bytes 1228808 | tf_op jit(solution)/shard_map/while/body/ppermute | solution.py:564
  100.1 4.8 %collective-permute-done.1 = bf16[200,1024]{1,0:T(8,128)(2,1)S(1)} collective-permute-done((bf16[200,1024]{1,0:T(8,128)(2,1)S(1)}, bf16[200,1024]{1,0:T(8,128)(2,1)S(1)}, u32[]{:S(2)}, u32[]{:S(2)}) %collective-permute-start.1) | collective-permute-done | bytes 409632 | tf_op jit(solution)/shard_map/while/body/ppermute | solution.py:564
  107.0 1.9 %late.1 = (f32[1,128]{1,0:T(1,128)S(1)}, bf16[1024,256]{1,0:T(8,128)(2,1)}, bf16[32,256]{1,0:T(8,128)(2,1)S(1)}, s32[1,64]{1,0:T(1,128)S(1)}, s32[1]{0:T(128)S(4)}) custom-call(bf16[64,256]{1,0:T(8,128)(2,1)S(1)} %get-tuple-element.117.query, bf16[1024,256]{1,0:T(8,128)(2,1)} %queue_hbm.3, s32[1]{0:T(128)S(6)} %copy.41.pointer, ...), custom_call_target="tpu_custom_call", output_to_operand_aliasing={{1}: (5, {})} | custom-call | tf_op jit(solution)/shard_map/late/pallas_call | solution.py:601
  109.4 14.6 %all_to_all.5.got = bf16[32,24,128]{2,1,0:T(8,128)(2,1)S(1)} all-to-all(bf16[32,24,128]{2,1,0:T(8,128)(2,1)S(1)} %head.2), channel_id=1, replica_groups=mesh['dp'=8,'section'=4] {'dp','section'}, dimensions={0} | all-to-all | bytes 393216 | tf_op jit(solution)/shard_map/all_to_all | solution.py:631
  (41 shorter events, 11.5 us)
Async XLA Ops:
  0.6 8.7 %collective-permute-start.2 = (bf16[8,256]{1,0:T(8,128)(2,1)}, bf16[8,256]{1,0:T(8,128)(2,1)S(1)}, u32[]{:S(2)}, u32[]{:S(2)}) collective-permute-start(bf16[8,256]{1,0:T(8,128)(2,1)} %refs_0_.1), channel_id=1, source_target_pairs={{0,4},{1,5},{2,6},{3,7},{4,0},{5,1},{6,2},{7,3},{8,12},{9,13},{10,... | collective-permute-start | bytes 12296 | tf_op jit(solution)/shard_map/ppermute | solution.py:552
  2.8 10.6 %copy-start.2 = (bf16[8,256]{1,0:T(8,128)(2,1)S(1)}, bf16[8,256]{1,0:T(8,128)(2,1)}, u32[]{:S(2)}) copy-start(bf16[8,256]{1,0:T(8,128)(2,1)} %refs_0_.1) | copy-start | bytes 12292
  2.8 14.3 %copy-start.4 = (f32[1,1024]{1,0:T(1,128)S(1)}, f32[1,1024]{1,0:T(1,128)}, u32[]{:S(2)}) copy-start(f32[1,1024]{1,0:T(1,128)} %g1.7) | copy-start | bytes 12292
  2.8 14.3 %copy-start.5 = (f32[1,1024]{1,0:T(1,128)S(1)}, f32[1,1024]{1,0:T(1,128)}, u32[]{:S(2)}) copy-start(f32[1,1024]{1,0:T(1,128)} %g2.7) | copy-start | bytes 12292
  9.4 12.0 %collective-permute-start.6 = (bf16[200,1024]{1,0:T(8,128)(2,1)S(1)}, bf16[200,1024]{1,0:T(8,128)(2,1)S(1)}, u32[]{:S(2)}, u32[]{:S(2)}) collective-permute-start(bf16[200,1024]{1,0:T(8,128)(2,1)S(1)} %get-tuple-element.122), channel_id=1, source_target_pairs={{0,1},{1,2},{2,3},{4,5},{5,6},{6,7},{8,9},{9,10},{10,11},{12,13},{... | collective-permute-start | bytes 1228808 | tf_op jit(solution)/shard_map/ppermute | solution.py:564
  13.4 3.7 %collective-permute-start.3 = (bf16[16,256]{1,0:T(8,128)(2,1)S(1)}, bf16[16,256]{1,0:T(8,128)(2,1)S(1)}, u32[]{:S(2)}, u32[]{:S(2)}) collective-permute-start(bf16[16,256]{1,0:T(8,128)(2,1)S(1)} %merge.2.refs_0_), channel_id=1, source_target_pairs={{0,8},{1,9},{2,10},{3,11},{4,12},{5,13},{6,14},{7,15},{8,0},{9,1},... | collective-permute-start | bytes 24584 | tf_op jit(solution)/shard_map/ppermute | solution.py:552
  14.7 3.4 %collective-permute-start.4 = (bf16[16,256]{1,0:T(8,128)(2,1)S(1)}, bf16[16,256]{1,0:T(8,128)(2,1)S(1)}, u32[]{:S(2)}, u32[]{:S(2)}) collective-permute-start(bf16[16,256]{1,0:T(8,128)(2,1)S(1)} %merge.2.refs_0_), channel_id=1, source_target_pairs={{0,16},{1,17},{2,18},{3,19},{4,20},{5,21},{6,22},{7,23},{8,24},{9,... | collective-permute-start | bytes 24584 | tf_op jit(solution)/shard_map/ppermute | solution.py:552
  17.1 4.3 %collective-permute-start.5 = (bf16[16,256]{1,0:T(8,128)(2,1)S(1)}, bf16[16,256]{1,0:T(8,128)(2,1)S(1)}, u32[]{:S(2)}, u32[]{:S(2)}) collective-permute-start(bf16[16,256]{1,0:T(8,128)(2,1)S(1)} %merge.2.refs_0_), channel_id=1, source_target_pairs={{0,24},{1,25},{2,26},{3,27},{4,28},{5,29},{6,30},{7,31},{8,16},{9,... | collective-permute-start | bytes 24584 | tf_op jit(solution)/shard_map/ppermute | solution.py:552
  21.6 11.2 %collective-permute-start = (bf16[200,1024]{1,0:T(8,128)(2,1)S(1)}, bf16[200,1024]{1,0:T(8,128)(2,1)S(1)}, u32[]{:S(2)}, u32[]{:S(2)}) collective-permute-start(bf16[200,1024]{1,0:T(8,128)(2,1)S(1)} %get-tuple-element.186), channel_id=1, source_target_pairs={{0,1},{1,2},{2,3},{4,5},{5,6},{6,7},{8,9},{9,10},{10,11},{12,13},{... | collective-permute-start | bytes 1228808 | tf_op jit(solution)/shard_map/while/body/ppermute | solution.py:564
  30.9 7.6 %collective-permute-start.1 = (bf16[200,1024]{1,0:T(8,128)(2,1)S(1)}, bf16[200,1024]{1,0:T(8,128)(2,1)S(1)}, u32[]{:S(2)}, u32[]{:S(2)}) collective-permute-start(bf16[200,1024]{1,0:T(8,128)(2,1)S(1)} %get-tuple-element.58), channel_id=1, source_target_pairs={{0,1},{1,2},{2,3},{4,5},{5,6},{6,7},{8,9},{9,10},{10,11},{12,13},{... | collective-permute-start | bytes 1228808 | tf_op jit(solution)/shard_map/while/body/ppermute | solution.py:564
  38.5 11.2 %collective-permute-start = (bf16[200,1024]{1,0:T(8,128)(2,1)S(1)}, bf16[200,1024]{1,0:T(8,128)(2,1)S(1)}, u32[]{:S(2)}, u32[]{:S(2)}) collective-permute-start(bf16[200,1024]{1,0:T(8,128)(2,1)S(1)} %get-tuple-element.186), channel_id=1, source_target_pairs={{0,1},{1,2},{2,3},{4,5},{5,6},{6,7},{8,9},{9,10},{10,11},{12,13},{... | collective-permute-start | bytes 1228808 | tf_op jit(solution)/shard_map/while/body/ppermute | solution.py:564
  47.7 7.6 %collective-permute-start.1 = (bf16[200,1024]{1,0:T(8,128)(2,1)S(1)}, bf16[200,1024]{1,0:T(8,128)(2,1)S(1)}, u32[]{:S(2)}, u32[]{:S(2)}) collective-permute-start(bf16[200,1024]{1,0:T(8,128)(2,1)S(1)} %get-tuple-element.58), channel_id=1, source_target_pairs={{0,1},{1,2},{2,3},{4,5},{5,6},{6,7},{8,9},{9,10},{10,11},{12,13},{... | collective-permute-start | bytes 1228808 | tf_op jit(solution)/shard_map/while/body/ppermute | solution.py:564
  55.3 11.2 %collective-permute-start = (bf16[200,1024]{1,0:T(8,128)(2,1)S(1)}, bf16[200,1024]{1,0:T(8,128)(2,1)S(1)}, u32[]{:S(2)}, u32[]{:S(2)}) collective-permute-start(bf16[200,1024]{1,0:T(8,128)(2,1)S(1)} %get-tuple-element.186), channel_id=1, source_target_pairs={{0,1},{1,2},{2,3},{4,5},{5,6},{6,7},{8,9},{9,10},{10,11},{12,13},{... | collective-permute-start | bytes 1228808 | tf_op jit(solution)/shard_map/while/body/ppermute | solution.py:564
  64.5 7.6 %collective-permute-start.1 = (bf16[200,1024]{1,0:T(8,128)(2,1)S(1)}, bf16[200,1024]{1,0:T(8,128)(2,1)S(1)}, u32[]{:S(2)}, u32[]{:S(2)}) collective-permute-start(bf16[200,1024]{1,0:T(8,128)(2,1)S(1)} %get-tuple-element.58), channel_id=1, source_target_pairs={{0,1},{1,2},{2,3},{4,5},{5,6},{6,7},{8,9},{9,10},{10,11},{12,13},{... | collective-permute-start | bytes 1228808 | tf_op jit(solution)/shard_map/while/body/ppermute | solution.py:564
  72.1 11.1 %collective-permute-start = (bf16[200,1024]{1,0:T(8,128)(2,1)S(1)}, bf16[200,1024]{1,0:T(8,128)(2,1)S(1)}, u32[]{:S(2)}, u32[]{:S(2)}) collective-permute-start(bf16[200,1024]{1,0:T(8,128)(2,1)S(1)} %get-tuple-element.186), channel_id=1, source_target_pairs={{0,1},{1,2},{2,3},{4,5},{5,6},{6,7},{8,9},{9,10},{10,11},{12,13},{... | collective-permute-start | bytes 1228808 | tf_op jit(solution)/shard_map/while/body/ppermute | solution.py:564
  81.4 7.6 %collective-permute-start.1 = (bf16[200,1024]{1,0:T(8,128)(2,1)S(1)}, bf16[200,1024]{1,0:T(8,128)(2,1)S(1)}, u32[]{:S(2)}, u32[]{:S(2)}) collective-permute-start(bf16[200,1024]{1,0:T(8,128)(2,1)S(1)} %get-tuple-element.58), channel_id=1, source_target_pairs={{0,1},{1,2},{2,3},{4,5},{5,6},{6,7},{8,9},{9,10},{10,11},{12,13},{... | collective-permute-start | bytes 1228808 | tf_op jit(solution)/shard_map/while/body/ppermute | solution.py:564
  89.0 11.2 %collective-permute-start = (bf16[200,1024]{1,0:T(8,128)(2,1)S(1)}, bf16[200,1024]{1,0:T(8,128)(2,1)S(1)}, u32[]{:S(2)}, u32[]{:S(2)}) collective-permute-start(bf16[200,1024]{1,0:T(8,128)(2,1)S(1)} %get-tuple-element.186), channel_id=1, source_target_pairs={{0,1},{1,2},{2,3},{4,5},{5,6},{6,7},{8,9},{9,10},{10,11},{12,13},{... | collective-permute-start | bytes 1228808 | tf_op jit(solution)/shard_map/while/body/ppermute | solution.py:564
  92.6 12.4 %collective-permute-start.1 = (bf16[200,1024]{1,0:T(8,128)(2,1)S(1)}, bf16[200,1024]{1,0:T(8,128)(2,1)S(1)}, u32[]{:S(2)}, u32[]{:S(2)}) collective-permute-start(bf16[200,1024]{1,0:T(8,128)(2,1)S(1)} %get-tuple-element.58), channel_id=1, source_target_pairs={{0,1},{1,2},{2,3},{4,5},{5,6},{6,7},{8,9},{9,10},{10,11},{12,13},{... | collective-permute-start | bytes 1228808 | tf_op jit(solution)/shard_map/while/body/ppermute | solution.py:564
  105.0 3.9 %collective-permute-start.7 = (bf16[200,1024]{1,0:T(8,128)(2,1)S(1)}, bf16[200,1024]{1,0:T(8,128)(2,1)S(1)}, u32[]{:S(2)}, u32[]{:S(2)}) collective-permute-start(bf16[200,1024]{1,0:T(8,128)(2,1)S(1)} %get-tuple-element.130), channel_id=1, source_target_pairs={{2,3},{6,7},{10,11},{14,15},{18,19},{22,23},{26,27},{30,31}} | collective-permute-start | bytes 1228808 | tf_op jit(solution)/shard_map/ppermute | solution.py:596
  106.3 0.7 copy-start.3
  106.3 2.6 %copy-start = (bf16[1024,256]{1,0:T(8,128)(2,1)S(1)}, bf16[1024,256]{1,0:T(8,128)(2,1)}, u32[]{:S(2)}) copy-start(bf16[1024,256]{1,0:T(8,128)(2,1)} %head.3) | copy-start | bytes 1572868
  106.3 2.6 %copy-start.1 = (f32[1024]{0:T(1024)S(1)}, f32[1024]{0:T(1024)}, u32[]{:S(2)}) copy-start(f32[1024]{0:T(1024)} %param.22) | copy-start | bytes 12292

commit v4 on v3

--- a/solution.py
+++ b/solution.py
@@ -347,7 +347,7 @@
 
     @pl.when(lax.axis_index("section") == lax.axis_size("section") - 1)
     def _():
-        marks[step : step + 1, :] = encode_class(came, g1, wqkv, wout, g2, wfc1, wfc2, norm, qkv, row, toks, True)
+        marks[step : step + 1, :] = encode_class(came, g1, wqkv, wout, g2, wfc1, wfc2, norm, qkv, row, toks, False)
 
 
 def run_class(came, marks, weights, toks):

time: 126 us -> 126 us (level)
  no operation moved by 1% of the time
where the time goes in v4:
time: 126 us
  Pallas kernels  55.5 us (44%)
  starting transfers between devices  43.6 us (35%)
  blocking collectives  14.6 us (12%)
  waiting for transfers between devices  9.11 us (7%)
  between operations  1.62 us (1%)
    pallas_call x11, Pallas kernels, run_tick(): pl.pallas_call(functools.partial(tick_kernel, toks=toks), out_shape=(pltp...  45.1 us
    ppermute x11, starting transfers between devices, one(): coming = lax.ppermute(sent, 'section', chain)  37.2 us
    all_to_all x1, blocking collectives, on_device(): got = lax.all_to_all(message, ('dp', 'section'), 0, 0, tiled=True)  14.6 us
    pallas_call x1, Pallas kernels, first_tick(): pl.pallas_call(functools.partial(first_kernel, images=images, toks=toks),...  6.61 us
    ppermute x4, starting transfers between devices, exchange(): return lax.ppermute(rows, ('dp', 'section'), pairs)  5.8 us
    ppermute x11, waiting for transfers between devices, one(): coming = lax.ppermute(sent, 'section', chain)  4.86 us
    ppermute x4, waiting for transfers between devices, exchange(): return lax.ppermute(rows, ('dp', 'section'), pairs)  4.25 us
  transfers between devices with their start and end apart: 16, of which 3 were waited for; matrix products, arithmetic and copies ran while one was open for 0% of the time, Pallas kernels for 43%

profile of v4, /device:TPU:1, one launch (start us, length us, event | category | flops | bytes accessed | tf_op | source)
XLA Modules:
  0.0 125.5 jit_solution(11183667607013205987)
XLA Ops:
  0.6 2.1 %collective-permute-start.2 = (bf16[8,256]{1,0:T(8,128)(2,1)}, bf16[8,256]{1,0:T(8,128)(2,1)S(1)}, u32[]{:S(2)}, u32[]{:S(2)}) collective-permute-start(bf16[8,256]{1,0:T(8,128)(2,1)} %refs_0_.1), channel_id=1, source_target_pairs={{0,4},{1,5},{2,6},{3,7},{4,0},{5,1},{6,2},{7,3},{8,12},{9,13},{10,... | collective-permute-start | bytes 12296 | tf_op jit(solution)/shard_map/ppermute | solution.py:552
  2.8 6.6 %first.1 = (bf16[200,1024]{1,0:T(8,128)(2,1)S(1)}, bf16[8,200,1024]{2,1,0:T(8,128)(2,1)S(1)}, bf16[1024,3072]{1,0:T(8,128)(2,1)S(1)}, bf16[1024,1024]{1,0:T(8,12...) custom-call(bf16[1576,1024]{1,0:T(8,128)(2,1)} %bitcast.17, ...), custom_call_target="tpu_custom_call" | custom-call | tf_op jit(solution)/shard_map/first/pallas_call | solution.py:229
  9.4 4.0 %collective-permute-start.6 = (bf16[200,1024]{1,0:T(8,128)(2,1)S(1)}, bf16[200,1024]{1,0:T(8,128)(2,1)S(1)}, u32[]{:S(2)}, u32[]{:S(2)}) collective-permute-start(bf16[200,1024]{1,0:T(8,128)(2,1)S(1)} %get-tuple-element.122), channel_id=1, source_target_pairs={{0,1},{1,2},{2,3},{4,5},{5,6},{6,7},{8,9},{9,10},{10,11},{12,13},{... | collective-permute-start | bytes 1228808 | tf_op jit(solution)/shard_map/ppermute | solution.py:564
  14.7 2.3 %collective-permute-start.4 = (bf16[16,256]{1,0:T(8,128)(2,1)S(1)}, bf16[16,256]{1,0:T(8,128)(2,1)S(1)}, u32[]{:S(2)}, u32[]{:S(2)}) collective-permute-start(bf16[16,256]{1,0:T(8,128)(2,1)S(1)} %merge.2.refs_0_), channel_id=1, source_target_pairs={{0,16},{1,17},{2,18},{3,19},{4,20},{5,21},{6,22},{7,23},{8,24},{9,... | collective-permute-start | bytes 24584 | tf_op jit(solution)/shard_map/ppermute | solution.py:552
  18.1 3.2 %collective-permute-done.5.refs_3_ = bf16[16,256]{1,0:T(8,128)(2,1)S(1)} collective-permute-done((bf16[16,256]{1,0:T(8,128)(2,1)S(1)}, bf16[16,256]{1,0:T(8,128)(2,1)S(1)}, u32[]{:S(2)}, u32[]{:S(2)}) %collective-permute-start.5) | collective-permute-done | bytes 8224 | tf_op jit(solution)/shard_map/ppermute | solution.py:552
  21.4 83.6 %while.13 = (s32[1]{0:T(128)S(4)}, bf16[200,1024]{1,0:T(8,128)(2,1)S(1)}, bf16[200,1024]{1,0:T(8,128)(2,1)S(1)}, f32[8,1024]{1,0:T(8,128)S(1)}, bf16[8,200,1024]...) while((s32[1]{0:T(128)S(4)}, ...), condition=%region_1.0_spmd, body=%region_0.0_spmd | while | flops 1 | bytes 3276977 | solution.py:594
  21.6 3.6 %collective-permute-start = (bf16[200,1024]{1,0:T(8,128)(2,1)S(1)}, bf16[200,1024]{1,0:T(8,128)(2,1)S(1)}, u32[]{:S(2)}, u32[]{:S(2)}) collective-permute-start(bf16[200,1024]{1,0:T(8,128)(2,1)S(1)} %get-tuple-element.186), channel_id=1, source_target_pairs={{0,1},{1,2},{2,3},{4,5},{5,6},{6,7},{8,9},{9,10},{10,11},{12,13},{... | collective-permute-start | bytes 1228808 | tf_op jit(solution)/shard_map/while/body/ppermute | solution.py:564
  25.3 5.6 %block.3 = (bf16[200,1024]{1,0:T(8,128)(2,1)S(1)}, f32[8,1024]{1,0:T(8,128)S(1)}, s32[1]{0:T(128)S(4)}) custom-call(s32[1]{0:T(128)S(4)} %get-tuple-element.184.tick, bf16[8,200,1024]{2,1,0:T(8,128)(2,1)S(1)} %get-tuple-element.199.turned, bf16[200,1024]{1,0:T(8,128)(2,1)S(1)} %get-tuple-element.185.came, ...), custom_call_target="tpu_custom_call", output_to_operand_aliasing={{1}: (3, {})} | custom-call | tf_op jit(solution)/shard_map/while/body/block/pallas_call | solution.py:306
  32.8 5.6 %block.4 = (bf16[200,1024]{1,0:T(8,128)(2,1)S(1)}, f32[8,1024]{1,0:T(8,128)S(1)}, s32[1]{0:T(128)S(4)}) custom-call(s32[1]{0:T(128)S(4)} %get-tuple-element.54.tick, bf16[8,200,1024]{2,1,0:T(8,128)(2,1)S(1)} %get-tuple-element.199.turned, bf16[200,1024]{1,0:T(8,128)(2,1)S(1)} %collective-permute-done.came, ...), custom_call_target="tpu_custom_call", output_to_operand_aliasing={{1}: (3, {})} | custom-call | tf_op jit(solution)/shard_map/while/body/block/pallas_call | solution.py:306
  38.5 3.6 %collective-permute-start = (bf16[200,1024]{1,0:T(8,128)(2,1)S(1)}, bf16[200,1024]{1,0:T(8,128)(2,1)S(1)}, u32[]{:S(2)}, u32[]{:S(2)}) collective-permute-start(bf16[200,1024]{1,0:T(8,128)(2,1)S(1)} %get-tuple-element.186), channel_id=1, source_target_pairs={{0,1},{1,2},{2,3},{4,5},{5,6},{6,7},{8,9},{9,10},{10,11},{12,13},{... | collective-permute-start | bytes 1228808 | tf_op jit(solution)/shard_map/while/body/ppermute | solution.py:564
  42.1 5.6 %block.3 = (bf16[200,1024]{1,0:T(8,128)(2,1)S(1)}, f32[8,1024]{1,0:T(8,128)S(1)}, s32[1]{0:T(128)S(4)}) custom-call(s32[1]{0:T(128)S(4)} %get-tuple-element.184.tick, bf16[8,200,1024]{2,1,0:T(8,128)(2,1)S(1)} %get-tuple-element.199.turned, bf16[200,1024]{1,0:T(8,128)(2,1)S(1)} %get-tuple-element.185.came, ...), custom_call_target="tpu_custom_call", output_to_operand_aliasing={{1}: (3, {})} | custom-call | tf_op jit(solution)/shard_map/while/body/block/pallas_call | solution.py:306
  49.7 5.6 %block.4 = (bf16[200,1024]{1,0:T(8,128)(2,1)S(1)}, f32[8,1024]{1,0:T(8,128)S(1)}, s32[1]{0:T(128)S(4)}) custom-call(s32[1]{0:T(128)S(4)} %get-tuple-element.54.tick, bf16[8,200,1024]{2,1,0:T(8,128)(2,1)S(1)} %get-tuple-element.199.turned, bf16[200,1024]{1,0:T(8,128)(2,1)S(1)} %collective-permute-done.came, ...), custom_call_target="tpu_custom_call", output_to_operand_aliasing={{1}: (3, {})} | custom-call | tf_op jit(solution)/shard_map/while/body/block/pallas_call | solution.py:306
  55.3 3.6 %collective-permute-start = (bf16[200,1024]{1,0:T(8,128)(2,1)S(1)}, bf16[200,1024]{1,0:T(8,128)(2,1)S(1)}, u32[]{:S(2)}, u32[]{:S(2)}) collective-permute-start(bf16[200,1024]{1,0:T(8,128)(2,1)S(1)} %get-tuple-element.186), channel_id=1, source_target_pairs={{0,1},{1,2},{2,3},{4,5},{5,6},{6,7},{8,9},{9,10},{10,11},{12,13},{... | collective-permute-start | bytes 1228808 | tf_op jit(solution)/shard_map/while/body/ppermute | solution.py:564
  58.9 5.6 %block.3 = (bf16[200,1024]{1,0:T(8,128)(2,1)S(1)}, f32[8,1024]{1,0:T(8,128)S(1)}, s32[1]{0:T(128)S(4)}) custom-call(s32[1]{0:T(128)S(4)} %get-tuple-element.184.tick, bf16[8,200,1024]{2,1,0:T(8,128)(2,1)S(1)} %get-tuple-element.199.turned, bf16[200,1024]{1,0:T(8,128)(2,1)S(1)} %get-tuple-element.185.came, ...), custom_call_target="tpu_custom_call", output_to_operand_aliasing={{1}: (3, {})} | custom-call | tf_op jit(solution)/shard_map/while/body/block/pallas_call | solution.py:306
  64.5 1.9 %collective-permute-start.1 = (bf16[200,1024]{1,0:T(8,128)(2,1)S(1)}, bf16[200,1024]{1,0:T(8,128)(2,1)S(1)}, u32[]{:S(2)}, u32[]{:S(2)}) collective-permute-start(bf16[200,1024]{1,0:T(8,128)(2,1)S(1)} %get-tuple-element.58), channel_id=1, source_target_pairs={{0,1},{1,2},{2,3},{4,5},{5,6},{6,7},{8,9},{9,10},{10,11},{12,13},{... | collective-permute-start | bytes 1228808 | tf_op jit(solution)/shard_map/while/body/ppermute | solution.py:564
  66.5 5.6 %block.4 = (bf16[200,1024]{1,0:T(8,128)(2,1)S(1)}, f32[8,1024]{1,0:T(8,128)S(1)}, s32[1]{0:T(128)S(4)}) custom-call(s32[1]{0:T(128)S(4)} %get-tuple-element.54.tick, bf16[8,200,1024]{2,1,0:T(8,128)(2,1)S(1)} %get-tuple-element.199.turned, bf16[200,1024]{1,0:T(8,128)(2,1)S(1)} %collective-permute-done.came, ...), custom_call_target="tpu_custom_call", output_to_operand_aliasing={{1}: (3, {})} | custom-call | tf_op jit(solution)/shard_map/while/body/block/pallas_call | solution.py:306
  72.1 3.6 %collective-permute-start = (bf16[200,1024]{1,0:T(8,128)(2,1)S(1)}, bf16[200,1024]{1,0:T(8,128)(2,1)S(1)}, u32[]{:S(2)}, u32[]{:S(2)}) collective-permute-start(bf16[200,1024]{1,0:T(8,128)(2,1)S(1)} %get-tuple-element.186), channel_id=1, source_target_pairs={{0,1},{1,2},{2,3},{4,5},{5,6},{6,7},{8,9},{9,10},{10,11},{12,13},{... | collective-permute-start | bytes 1228808 | tf_op jit(solution)/shard_map/while/body/ppermute | solution.py:564
  75.7 5.6 %block.3 = (bf16[200,1024]{1,0:T(8,128)(2,1)S(1)}, f32[8,1024]{1,0:T(8,128)S(1)}, s32[1]{0:T(128)S(4)}) custom-call(s32[1]{0:T(128)S(4)} %get-tuple-element.184.tick, bf16[8,200,1024]{2,1,0:T(8,128)(2,1)S(1)} %get-tuple-element.199.turned, bf16[200,1024]{1,0:T(8,128)(2,1)S(1)} %get-tuple-element.185.came, ...), custom_call_target="tpu_custom_call", output_to_operand_aliasing={{1}: (3, {})} | custom-call | tf_op jit(solution)/shard_map/while/body/block/pallas_call | solution.py:306
  83.3 5.6 %block.4 = (bf16[200,1024]{1,0:T(8,128)(2,1)S(1)}, f32[8,1024]{1,0:T(8,128)S(1)}, s32[1]{0:T(128)S(4)}) custom-call(s32[1]{0:T(128)S(4)} %get-tuple-element.54.tick, bf16[8,200,1024]{2,1,0:T(8,128)(2,1)S(1)} %get-tuple-element.199.turned, bf16[200,1024]{1,0:T(8,128)(2,1)S(1)} %collective-permute-done.came, ...), custom_call_target="tpu_custom_call", output_to_operand_aliasing={{1}: (3, {})} | custom-call | tf_op jit(solution)/shard_map/while/body/block/pallas_call | solution.py:306
  89.0 3.6 %collective-permute-start = (bf16[200,1024]{1,0:T(8,128)(2,1)S(1)}, bf16[200,1024]{1,0:T(8,128)(2,1)S(1)}, u32[]{:S(2)}, u32[]{:S(2)}) collective-permute-start(bf16[200,1024]{1,0:T(8,128)(2,1)S(1)} %get-tuple-element.186), channel_id=1, source_target_pairs={{0,1},{1,2},{2,3},{4,5},{5,6},{6,7},{8,9},{9,10},{10,11},{12,13},{... | collective-permute-start | bytes 1228808 | tf_op jit(solution)/shard_map/while/body/ppermute | solution.py:564
  92.6 7.5 %collective-permute-start.1 = (bf16[200,1024]{1,0:T(8,128)(2,1)S(1)}, bf16[200,1024]{1,0:T(8,128)(2,1)S(1)}, u32[]{:S(2)}, u32[]{:S(2)}) collective-permute-start(bf16[200,1024]{1,0:T(8,128)(2,1)S(1)} %get-tuple-element.58), channel_id=1, source_target_pairs={{0,1},{1,2},{2,3},{4,5},{5,6},{6,7},{8,9},{9,10},{10,11},{12,13},{... | collective-permute-start | bytes 1228808 | tf_op jit(solution)/shard_map/while/body/ppermute | solution.py:564
  100.1 4.8 %collective-permute-done.1 = bf16[200,1024]{1,0:T(8,128)(2,1)S(1)} collective-permute-done((bf16[200,1024]{1,0:T(8,128)(2,1)S(1)}, bf16[200,1024]{1,0:T(8,128)(2,1)S(1)}, u32[]{:S(2)}, u32[]{:S(2)}) %collective-permute-start.1) | collective-permute-done | bytes 409632 | tf_op jit(solution)/shard_map/while/body/ppermute | solution.py:564
  107.0 1.9 %late.1 = (f32[1,128]{1,0:T(1,128)S(1)}, bf16[1024,256]{1,0:T(8,128)(2,1)}, bf16[32,256]{1,0:T(8,128)(2,1)S(1)}, s32[1,64]{1,0:T(1,128)S(1)}, s32[1]{0:T(128)S(4)}) custom-call(bf16[64,256]{1,0:T(8,128)(2,1)S(1)} %get-tuple-element.117.query, bf16[1024,256]{1,0:T(8,128)(2,1)} %queue_hbm.3, s32[1]{0:T(128)S(6)} %copy.41.pointer, ...), custom_call_target="tpu_custom_call", output_to_operand_aliasing={{1}: (5, {})} | custom-call | tf_op jit(solution)/shard_map/late/pallas_call | solution.py:601
  109.4 14.6 %all_to_all.5.got = bf16[32,24,128]{2,1,0:T(8,128)(2,1)S(1)} all-to-all(bf16[32,24,128]{2,1,0:T(8,128)(2,1)S(1)} %head.2), channel_id=1, replica_groups=mesh['dp'=8,'section'=4] {'dp','section'}, dimensions={0} | all-to-all | bytes 393216 | tf_op jit(solution)/shard_map/all_to_all | solution.py:631
  (41 shorter events, 11.5 us)
Async XLA Ops:
  0.6 8.7 %collective-permute-start.2 = (bf16[8,256]{1,0:T(8,128)(2,1)}, bf16[8,256]{1,0:T(8,128)(2,1)S(1)}, u32[]{:S(2)}, u32[]{:S(2)}) collective-permute-start(bf16[8,256]{1,0:T(8,128)(2,1)} %refs_0_.1), channel_id=1, source_target_pairs={{0,4},{1,5},{2,6},{3,7},{4,0},{5,1},{6,2},{7,3},{8,12},{9,13},{10,... | collective-permute-start | bytes 12296 | tf_op jit(solution)/shard_map/ppermute | solution.py:552
  2.8 10.6 %copy-start.2 = (bf16[8,256]{1,0:T(8,128)(2,1)S(1)}, bf16[8,256]{1,0:T(8,128)(2,1)}, u32[]{:S(2)}) copy-start(bf16[8,256]{1,0:T(8,128)(2,1)} %refs_0_.1) | copy-start | bytes 12292
  2.8 14.3 %copy-start.4 = (f32[1,1024]{1,0:T(1,128)S(1)}, f32[1,1024]{1,0:T(1,128)}, u32[]{:S(2)}) copy-start(f32[1,1024]{1,0:T(1,128)} %g1.7) | copy-start | bytes 12292
  2.8 14.3 %copy-start.5 = (f32[1,1024]{1,0:T(1,128)S(1)}, f32[1,1024]{1,0:T(1,128)}, u32[]{:S(2)}) copy-start(f32[1,1024]{1,0:T(1,128)} %g2.7) | copy-start | bytes 12292
  9.4 12.0 %collective-permute-start.6 = (bf16[200,1024]{1,0:T(8,128)(2,1)S(1)}, bf16[200,1024]{1,0:T(8,128)(2,1)S(1)}, u32[]{:S(2)}, u32[]{:S(2)}) collective-permute-start(bf16[200,1024]{1,0:T(8,128)(2,1)S(1)} %get-tuple-element.122), channel_id=1, source_target_pairs={{0,1},{1,2},{2,3},{4,5},{5,6},{6,7},{8,9},{9,10},{10,11},{12,13},{... | collective-permute-start | bytes 1228808 | tf_op jit(solution)/shard_map/ppermute | solution.py:564
  13.4 3.7 %collective-permute-start.3 = (bf16[16,256]{1,0:T(8,128)(2,1)S(1)}, bf16[16,256]{1,0:T(8,128)(2,1)S(1)}, u32[]{:S(2)}, u32[]{:S(2)}) collective-permute-start(bf16[16,256]{1,0:T(8,128)(2,1)S(1)} %merge.2.refs_0_), channel_id=1, source_target_pairs={{0,8},{1,9},{2,10},{3,11},{4,12},{5,13},{6,14},{7,15},{8,0},{9,1},... | collective-permute-start | bytes 24584 | tf_op jit(solution)/shard_map/ppermute | solution.py:552
  14.7 3.4 %collective-permute-start.4 = (bf16[16,256]{1,0:T(8,128)(2,1)S(1)}, bf16[16,256]{1,0:T(8,128)(2,1)S(1)}, u32[]{:S(2)}, u32[]{:S(2)}) collective-permute-start(bf16[16,256]{1,0:T(8,128)(2,1)S(1)} %merge.2.refs_0_), channel_id=1, source_target_pairs={{0,16},{1,17},{2,18},{3,19},{4,20},{5,21},{6,22},{7,23},{8,24},{9,... | collective-permute-start | bytes 24584 | tf_op jit(solution)/shard_map/ppermute | solution.py:552
  17.1 4.3 %collective-permute-start.5 = (bf16[16,256]{1,0:T(8,128)(2,1)S(1)}, bf16[16,256]{1,0:T(8,128)(2,1)S(1)}, u32[]{:S(2)}, u32[]{:S(2)}) collective-permute-start(bf16[16,256]{1,0:T(8,128)(2,1)S(1)} %merge.2.refs_0_), channel_id=1, source_target_pairs={{0,24},{1,25},{2,26},{3,27},{4,28},{5,29},{6,30},{7,31},{8,16},{9,... | collective-permute-start | bytes 24584 | tf_op jit(solution)/shard_map/ppermute | solution.py:552
  21.6 11.2 %collective-permute-start = (bf16[200,1024]{1,0:T(8,128)(2,1)S(1)}, bf16[200,1024]{1,0:T(8,128)(2,1)S(1)}, u32[]{:S(2)}, u32[]{:S(2)}) collective-permute-start(bf16[200,1024]{1,0:T(8,128)(2,1)S(1)} %get-tuple-element.186), channel_id=1, source_target_pairs={{0,1},{1,2},{2,3},{4,5},{5,6},{6,7},{8,9},{9,10},{10,11},{12,13},{... | collective-permute-start | bytes 1228808 | tf_op jit(solution)/shard_map/while/body/ppermute | solution.py:564
  30.9 7.6 %collective-permute-start.1 = (bf16[200,1024]{1,0:T(8,128)(2,1)S(1)}, bf16[200,1024]{1,0:T(8,128)(2,1)S(1)}, u32[]{:S(2)}, u32[]{:S(2)}) collective-permute-start(bf16[200,1024]{1,0:T(8,128)(2,1)S(1)} %get-tuple-element.58), channel_id=1, source_target_pairs={{0,1},{1,2},{2,3},{4,5},{5,6},{6,7},{8,9},{9,10},{10,11},{12,13},{... | collective-permute-start | bytes 1228808 | tf_op jit(solution)/shard_map/while/body/ppermute | solution.py:564
  38.5 11.2 %collective-permute-start = (bf16[200,1024]{1,0:T(8,128)(2,1)S(1)}, bf16[200,1024]{1,0:T(8,128)(2,1)S(1)}, u32[]{:S(2)}, u32[]{:S(2)}) collective-permute-start(bf16[200,1024]{1,0:T(8,128)(2,1)S(1)} %get-tuple-element.186), channel_id=1, source_target_pairs={{0,1},{1,2},{2,3},{4,5},{5,6},{6,7},{8,9},{9,10},{10,11},{12,13},{... | collective-permute-start | bytes 1228808 | tf_op jit(solution)/shard_map/while/body/ppermute | solution.py:564
  47.7 7.6 %collective-permute-start.1 = (bf16[200,1024]{1,0:T(8,128)(2,1)S(1)}, bf16[200,1024]{1,0:T(8,128)(2,1)S(1)}, u32[]{:S(2)}, u32[]{:S(2)}) collective-permute-start(bf16[200,1024]{1,0:T(8,128)(2,1)S(1)} %get-tuple-element.58), channel_id=1, source_target_pairs={{0,1},{1,2},{2,3},{4,5},{5,6},{6,7},{8,9},{9,10},{10,11},{12,13},{... | collective-permute-start | bytes 1228808 | tf_op jit(solution)/shard_map/while/body/ppermute | solution.py:564
  55.3 11.2 %collective-permute-start = (bf16[200,1024]{1,0:T(8,128)(2,1)S(1)}, bf16[200,1024]{1,0:T(8,128)(2,1)S(1)}, u32[]{:S(2)}, u32[]{:S(2)}) collective-permute-start(bf16[200,1024]{1,0:T(8,128)(2,1)S(1)} %get-tuple-element.186), channel_id=1, source_target_pairs={{0,1},{1,2},{2,3},{4,5},{5,6},{6,7},{8,9},{9,10},{10,11},{12,13},{... | collective-permute-start | bytes 1228808 | tf_op jit(solution)/shard_map/while/body/ppermute | solution.py:564
  64.5 7.6 %collective-permute-start.1 = (bf16[200,1024]{1,0:T(8,128)(2,1)S(1)}, bf16[200,1024]{1,0:T(8,128)(2,1)S(1)}, u32[]{:S(2)}, u32[]{:S(2)}) collective-permute-start(bf16[200,1024]{1,0:T(8,128)(2,1)S(1)} %get-tuple-element.58), channel_id=1, source_target_pairs={{0,1},{1,2},{2,3},{4,5},{5,6},{6,7},{8,9},{9,10},{10,11},{12,13},{... | collective-permute-start | bytes 1228808 | tf_op jit(solution)/shard_map/while/body/ppermute | solution.py:564
  72.1 11.1 %collective-permute-start = (bf16[200,1024]{1,0:T(8,128)(2,1)S(1)}, bf16[200,1024]{1,0:T(8,128)(2,1)S(1)}, u32[]{:S(2)}, u32[]{:S(2)}) collective-permute-start(bf16[200,1024]{1,0:T(8,128)(2,1)S(1)} %get-tuple-element.186), channel_id=1, source_target_pairs={{0,1},{1,2},{2,3},{4,5},{5,6},{6,7},{8,9},{9,10},{10,11},{12,13},{... | collective-permute-start | bytes 1228808 | tf_op jit(solution)/shard_map/while/body/ppermute | solution.py:564
  81.4 7.6 %collective-permute-start.1 = (bf16[200,1024]{1,0:T(8,128)(2,1)S(1)}, bf16[200,1024]{1,0:T(8,128)(2,1)S(1)}, u32[]{:S(2)}, u32[]{:S(2)}) collective-permute-start(bf16[200,1024]{1,0:T(8,128)(2,1)S(1)} %get-tuple-element.58), channel_id=1, source_target_pairs={{0,1},{1,2},{2,3},{4,5},{5,6},{6,7},{8,9},{9,10},{10,11},{12,13},{... | collective-permute-start | bytes 1228808 | tf_op jit(solution)/shard_map/while/body/ppermute | solution.py:564
  89.0 11.2 %collective-permute-start = (bf16[200,1024]{1,0:T(8,128)(2,1)S(1)}, bf16[200,1024]{1,0:T(8,128)(2,1)S(1)}, u32[]{:S(2)}, u32[]{:S(2)}) collective-permute-start(bf16[200,1024]{1,0:T(8,128)(2,1)S(1)} %get-tuple-element.186), channel_id=1, source_target_pairs={{0,1},{1,2},{2,3},{4,5},{5,6},{6,7},{8,9},{9,10},{10,11},{12,13},{... | collective-permute-start | bytes 1228808 | tf_op jit(solution)/shard_map/while/body/ppermute | solution.py:564
  92.6 12.4 %collective-permute-start.1 = (bf16[200,1024]{1,0:T(8,128)(2,1)S(1)}, bf16[200,1024]{1,0:T(8,128)(2,1)S(1)}, u32[]{:S(2)}, u32[]{:S(2)}) collective-permute-start(bf16[200,1024]{1,0:T(8,128)(2,1)S(1)} %get-tuple-element.58), channel_id=1, source_target_pairs={{0,1},{1,2},{2,3},{4,5},{5,6},{6,7},{8,9},{9,10},{10,11},{12,13},{... | collective-permute-start | bytes 1228808 | tf_op jit(solution)/shard_map/while/body/ppermute | solution.py:564
  105.0 3.9 %collective-permute-start.7 = (bf16[200,1024]{1,0:T(8,128)(2,1)S(1)}, bf16[200,1024]{1,0:T(8,128)(2,1)S(1)}, u32[]{:S(2)}, u32[]{:S(2)}) collective-permute-start(bf16[200,1024]{1,0:T(8,128)(2,1)S(1)} %get-tuple-element.130), channel_id=1, source_target_pairs={{2,3},{6,7},{10,11},{14,15},{18,19},{22,23},{26,27},{30,31}} | collective-permute-start | bytes 1228808 | tf_op jit(solution)/shard_map/ppermute | solution.py:596
  106.3 0.7 copy-start.3
  106.3 2.6 %copy-start = (bf16[1024,256]{1,0:T(8,128)(2,1)S(1)}, bf16[1024,256]{1,0:T(8,128)(2,1)}, u32[]{:S(2)}) copy-start(bf16[1024,256]{1,0:T(8,128)(2,1)} %head.3) | copy-start | bytes 1572868
  106.3 2.6 %copy-start.1 = (f32[1024]{0:T(1024)S(1)}, f32[1024]{0:T(1024)}, u32[]{:S(2)}) copy-start(f32[1024]{0:T(1024)} %param.22) | copy-start | bytes 12292
